TPU v7x, 32 devices: a whole 2x2x4 slice. The times are simulated.
32 devices in a mesh: dp: 4 (over y, x), expert: 8 (over z, core).
Axes of the slice: x: 2, y: 2, z: 4, core: 2. Of those that a mesh axis runs over, the one named last changes fastest.
Arguments:
- residual_in: bfloat16 [4096, 2048], P(('dp', 'expert')), may hold values from -6 to 6
- queries: bfloat16 [4096, 2048], P(('dp', 'expert')), may hold values from -6 to 6
- keys_in: bfloat16 [4096, 2048], P(('dp', 'expert')), may hold values from -6 to 6
- values_in: bfloat16 [4096, 2048], P(('dp', 'expert')), may hold values from -6 to 6
- out_gate: bfloat16 [4096, 2048], P(('dp', 'expert')), may hold values from -6 to 6
- log_decay: float32 [16, 4096], P(None, ('dp', 'expert')), may hold values from -0.7 to 0
- beta_rate: float32 [16, 4096], P(None, ('dp', 'expert')), may hold values from 0.05 to 0.95
- head_gain: float32 [128], replicated, may hold values from 0.1 to 1.9
- moe_gain: float32 [2048], replicated, may hold values from 0.1 to 1.9
- state_cache: float32 [32, 2, 16, 128, 128], P(('dp', 'expert')), may hold values from -1.8 to 1.8
- hit_holder: int32 [32], P(('dp', 'expert')), may hold values from 0 to 3
- hit_slot: int32 [32], P(('dp', 'expert')), may hold values from 0 to 1
- expert_ids: int32 [4096, 10], P(('dp', 'expert')), may hold values from 0 to 31, all different within a row; in each aligned block of 128 rows (0 to 127, 128 to 255, ...) at most 56 rows name the same one
- gate_weight: float32 [4096, 10], P(('dp', 'expert')), may hold values from 0.03 to 0.3
- w_gate: bfloat16 [32, 2048, 512], P('expert'), may hold values from -0.125 to 0.125
- w_up: bfloat16 [32, 2048, 512], P('expert'), may hold values from -0.125 to 0.125
- w_down: bfloat16 [32, 512, 2048], P('expert'), may hold values from -0.25 to 0.25
Outputs:
- mixer_out: bfloat16 [4096, 2048], P(('dp', 'expert'))
- expert_out: bfloat16 [4096, 2048], P(('dp', 'expert'))
- next_state: float32 [32, 16, 128, 128], P(('dp', 'expert'))
Inputs may be any that keep to these rules, and one draw needn't show every extreme that they name: `expert_ids`: within the 128 rows of one device no expert is named by more than 56 of them, and the 10 numbers of a row differ.
All inputs are finite; a program needn't handle non-finite values.
Results may differ from a plain program's by a relative error of at most 0.014.
Values may be sent and summed in bfloat16 or wider, within the bound.
No kernel may reach another device: no remote copies, remote signals or barrier semaphores. Data moves between devices by JAX's collectives and lax.ppermute only.
A program may use at most 128 MiB of HBM per device.

v0:
```python
import jax
import jax.numpy as jnp
from jax import lax
from jax.sharding import PartitionSpec as P

MOST = 56


TOP_PRECISION = lax.Precision.HIGHEST


def unit_rows(block):
    block = block.astype(jnp.float32)
    return block / jnp.sqrt(jnp.sum(block * block, axis=-1, keepdims=True) + 1e-06)


def local(
    residual_in,
    queries,
    keys_in,
    values_in,
    out_gate,
    log_decay,
    beta_rate,
    head_gain,
    moe_gain,
    state_cache,
    hit_holder,
    hit_slot,
    expert_ids,
    gate_weight,
    w_gate,
    w_up,
    w_down,
):
    tok_rows = queries.shape[0]
    head_count = log_decay.shape[0]
    own_holder = hit_holder[0]
    own_slot = hit_slot[0]
    empty_state = jnp.zeros(state_cache.shape[2:], jnp.float32)
    piece = lax.all_gather(state_cache.astype(jnp.bfloat16), "dp", axis=0, tiled=True).astype(
        jnp.float32
    )
    owner = jnp.arange(piece.shape[0], dtype=jnp.int32)
    match = (owner == own_holder)[:, None] & (
        jnp.arange(piece.shape[1], dtype=jnp.int32) == own_slot
    )[None, :]
    initial_state = empty_state + jnp.sum(
        jnp.where(match[:, :, None, None, None], piece, 0.0), axis=(0, 1)
    )
    query_normalized = unit_rows(queries.reshape(tok_rows, head_count, -1)).transpose(1, 0, 2)
    key_normalized = unit_rows(keys_in.reshape(tok_rows, head_count, -1)).transpose(1, 0, 2)
    v_rows = values_in.reshape(tok_rows, head_count, -1).astype(jnp.float32).transpose(1, 0, 2)
    log_total = jnp.cumsum(log_decay, axis=1)
    row_after = jnp.arange(tok_rows)[:, None]
    row_before = jnp.arange(tok_rows)[None, :]
    strict = row_after > row_before
    inclusive = row_after >= row_before
    log_gap = log_total[:, :, None] - log_total[:, None, :]
    strict_ratio = jnp.where(strict, jnp.exp(jnp.where(strict, log_gap, 0.0)), 0.0)
    incl_ratio = jnp.where(inclusive, jnp.exp(jnp.where(inclusive, log_gap, 0.0)), 0.0)
    key_key = jnp.einsum("htk,hjk->htj", key_normalized, key_normalized, precision=TOP_PRECISION)
    strict_mix = beta_rate[:, :, None] * strict_ratio * key_key
    inverse = jnp.eye(tok_rows, dtype=jnp.float32)[None] - strict_mix
    powered = strict_mix
    reach = 2
    while reach < tok_rows:
        powered = jnp.einsum("hij,hjk->hik", powered, powered, precision=TOP_PRECISION)
        inverse = inverse + jnp.einsum("hij,hjk->hik", inverse, powered, precision=TOP_PRECISION)
        reach = reach * 2
    growth = jnp.exp(log_total)
    update_baseline = jnp.einsum(
        "htj,hjv->htv", inverse, beta_rate[:, :, None] * v_rows, precision=TOP_PRECISION
    )
    write_baseline = jnp.einsum(
        "htj,hjk->htk",
        inverse,
        (beta_rate * growth)[:, :, None] * key_normalized,
        precision=TOP_PRECISION,
    )
    mixing = incl_ratio * jnp.einsum(
        "htk,hjk->htj", query_normalized, key_normalized, precision=TOP_PRECISION
    )
    corrections = update_baseline - jnp.einsum(
        "rsa,rax->rsx", write_baseline, initial_state, precision=TOP_PRECISION
    )
    outputs = growth[:, :, None] * jnp.einsum(
        "rsa,rax->rsx", query_normalized, initial_state, precision=TOP_PRECISION
    )
    outputs = outputs + jnp.einsum("htj,hjv->htv", mixing, corrections, precision=TOP_PRECISION)
    trailing_decay = jnp.exp(log_total[:, -1:] - log_total)
    next_state = growth[:, -1][:, None, None] * initial_state + jnp.einsum(
        "jwn,jwc->jnc",
        key_normalized * trailing_decay[:, :, None],
        corrections,
        precision=TOP_PRECISION,
    )
    o_rows = outputs.transpose(1, 0, 2)
    scaled = (
        o_rows / jnp.sqrt(jnp.mean(o_rows * o_rows, axis=-1, keepdims=True) + 1e-06) * head_gain
    )
    gated = scaled * jax.nn.silu(out_gate.reshape(tok_rows, head_count, -1).astype(jnp.float32))
    mixer_out = (residual_in.astype(jnp.float32) + gated.reshape(tok_rows, -1)).astype(jnp.bfloat16)
    mixer_f = mixer_out.astype(jnp.float32)
    moe_in = (
        mixer_f / jnp.sqrt(jnp.mean(mixer_f * mixer_f, axis=-1, keepdims=True) + 1e-06) * moe_gain
    ).astype(jnp.bfloat16)
    group = lax.axis_size("expert")
    local_experts = w_gate.shape[0]
    experts_all = group * local_experts
    top = expert_ids.shape[1]
    flat_ids = expert_ids.reshape(-1)
    onehot = (flat_ids[:, None] == jnp.arange(experts_all, dtype=jnp.int32)[None, :]).astype(
        jnp.int32
    )
    slot_rank = jnp.sum(jnp.cumsum(onehot, axis=0) * onehot, axis=1) - 1
    slot_index = flat_ids * MOST + slot_rank
    source_row = jnp.arange(flat_ids.shape[0], dtype=jnp.int32) // top
    slot_token = jnp.full((experts_all * MOST,), tok_rows, jnp.int32).at[slot_index].set(source_row)
    padded = jnp.concatenate([moe_in, jnp.zeros((1, moe_in.shape[1]), jnp.bfloat16)], axis=0)
    outgoing = padded[slot_token].reshape(group, local_experts, MOST, -1)
    arrived = lax.all_to_all(outgoing, "expert", split_axis=0, concat_axis=0, tiled=True)
    gate_part = jnp.einsum("aemd,edf->aemf", arrived, w_gate, preferred_element_type=jnp.float32)
    up_part = jnp.einsum("aemd,edf->aemf", arrived, w_up, preferred_element_type=jnp.float32)
    hidden_rows = (jax.nn.silu(gate_part) * up_part).astype(jnp.bfloat16)
    rows_out = jnp.einsum(
        "aemf,efd->aemd", hidden_rows, w_down, preferred_element_type=jnp.float32
    ).astype(jnp.bfloat16)
    returned = lax.all_to_all(rows_out, "expert", split_axis=0, concat_axis=0, tiled=True)
    rows_back = returned.reshape(experts_all * MOST, -1)[slot_index].reshape(tok_rows, top, -1)
    expert_out = jnp.einsum(
        "tk,tkd->td", gate_weight, rows_back.astype(jnp.float32), precision=TOP_PRECISION
    ).astype(jnp.bfloat16)
    return (mixer_out, expert_out, next_state[None])


def solution(mesh):
    placed = (
        P(("dp", "expert"), None),
        P(("dp", "expert"), None),
        P(("dp", "expert"), None),
        P(("dp", "expert"), None),
        P(("dp", "expert"), None),
        P(None, ("dp", "expert")),
        P(None, ("dp", "expert")),
        P(),
        P(),
        P(("dp", "expert"), None, None, None, None),
        P(("dp", "expert")),
        P(("dp", "expert")),
        P(("dp", "expert"), None),
        P(("dp", "expert"), None),
        P("expert", None, None),
        P("expert", None, None),
        P("expert", None, None),
    )
    return jax.shard_map(
        local,
        mesh=mesh,
        in_specs=placed,
        out_specs=(
            P(("dp", "expert"), None),
            P(("dp", "expert"), None),
            P(("dp", "expert"), None, None, None),
        ),
        check_vma=False,
    )
```

profile of v0, /device:TPU:16, one launch (start us, length us, event | category | flops | bytes accessed | tf_op | source)
XLA Modules:
  0.0 490.7 jit_solution(14651315032636866687)
XLA Ops:
  7.2 2.8 convert_element_type.68
  14.7 9.1 %reduce-window.6 = s32[32,10,128]{2,1,0:T(8,128)S(1)} reduce-window(s32[32,10,128]{2,1,0:T(8,128)S(1)} %fusion.45, s32[]{:T(128)} %constant.43.clone.1), window={size=1x1x128 pad=0_0x0_0x127_0}, to_apply=%region_6.7 | reduce-window | flops 5201920 | bytes 327684 | tf_op jit(solution)/shard_map/reduce-window
  24.5 5.5 %scatter_custom_fusion = s32[1792]{0:T(1024)S(1)} fusion(s32[1280]{0:T(1024)S(1)} %fusion.52, s32[1280]{0:T(1024)S(1)} %add_select_fusion, s32[]{:T(128)} %constant.25.clone.1), kind=kCustom, calls=%fused_computation.103 | custom fusion | bytes 7172 | tf_op jit(solution)/shard_map/scatter | solution.py:119
  33.0 1.2 copy.107
  35.8 1.6 broadcast_multiply_fusion
  37.3 2.8 convolution_multiply_fusion
  40.1 1.6 divide_bitcast_fusion.1
  45.6 1.3 convolution_add_fusion.5
  46.9 1.2 convolution_add_fusion.4
  48.1 1.4 fusion.60
  51.9 1.2 convolution_add_fusion.2
  56.6 2.4 fusion.36
  59.0 2.2 fusion.34
  61.2 4.2 convolution_multiply_fusion.1
  65.5 3.4 select_reduce_fusion
  68.9 2.5 fusion.25
  72.6 1.9 multiply_reduce_fusion
  74.5 1.3 multiply_multiply_fusion
  75.8 2.5 copy.112
  78.4 1.5 fusion.26
  80.1 8.0 %gather_fusion = bf16[1792,2048]{1,0:T(8,128)(2,1)} fusion(bf16[129,2048]{1,0:T(8,128)(2,1)S(1)} %concatenate.3, s32[2048]{0:T(1024)S(1)} %pad_clamp_fusion.1), kind=kCustom, calls=%fused_computation | custom fusion | bytes 14687232 | tf_op jit(solution)/shard_map/gather | solution.py:121
  88.1 163.7 %all_to_all.10 = bf16[8,4,56,2048]{3,2,1,0:T(8,128)(2,1)S(1)} all-to-all(bf16[8,4,56,2048]{3,2,1,0:T(8,128)(2,1)} %bitcast.136), channel_id=1, replica_groups=mesh['dp'=4,'expert'=8] {'expert'}, dimensions={0} | all-to-all | bytes 14680064 | tf_op jit(solution)/shard_map/all_to_all | solution.py:122
  251.8 3.0 copy-done.1
  254.8 8.2 %fusion.4 = f32[4,8,56,512]{3,2,1,0:T(8,128)} fusion(bf16[4,2048,512]{2,1,0:T(8,128)(2,1)} %param.31, bf16[8,4,56,2048]{3,2,1,0:T(8,128)(2,1)S(1)} %all_to_all.10), kind=kOutput, calls=%fused_computation.7 | convolution fusion | flops 3758096384 | bytes 19398656 | tf_op jit(solution)/shard_map/aemd,edf->aemf/dot_general | solution.py:123
  263.1 15.0 %convert_bitcast_fusion = bf16[8,4,56,2048]{3,2,0,1:T(8,128)(2,1)} fusion(bf16[4,512,2048]{2,1,0:T(8,128)(2,1)} %param.33, f32[4,8,56,512]{3,2,1,0:T(8,128)} %fusion.4, bf16[4,2048,512]{2,1,0:T(8,128)(2,1)} %param.32, bf16[8,4,56,2048]{3,2,1,0:T(8,128)(2,1)} %copy-done.1), kind=kOutput, calls=%fused_computation.10 | convolution fusion | flops 7525367808 | bytes 35127296 | tf_op jit(solution)/shard_map/aemf,efd->aemd/dot_general | solution.py:126
  278.1 7.5 %copy.120 = bf16[8,4,56,2048]{3,2,1,0:T(8,128)(2,1)} copy(bf16[8,4,56,2048]{3,2,0,1:T(8,128)(2,1)} %convert_bitcast_fusion) | data formatting | bytes 14680064 | tf_op jit(solution)/shard_map/convert_element_type | solution.py:128
  285.6 8.4 %all-to-all-start.1 = ((bf16[8,4,56,2048]{3,2,1,0:T(8,128)(2,1)}), bf16[8,4,56,2048]{3,2,1,0:T(8,128)(2,1)}, u32[]{:S(2)}, u32[]{:S(2)}) async-start(bf16[8,4,56,2048]{3,2,1,0:T(8,128)(2,1)} %copy.120), calls=%async_computation.1 | async-start | bytes 14680064 | tf_op jit(solution)/shard_map/all_to_all | solution.py:129
  294.3 4.3 fusion.23
  298.6 153.5 %all-to-all-done.1 = bf16[8,4,56,2048]{3,2,1,0:T(8,128)(2,1)} async-done(((bf16[8,4,56,2048]{3,2,1,0:T(8,128)(2,1)}), bf16[8,4,56,2048]{3,2,1,0:T(8,128)(2,1)}, u32[]{:S(2)}, u32[]{:S(2)}) %all-to-all-start.1) | async-done | bytes 7340064 | tf_op jit(solution)/shard_map/all_to_all | solution.py:129
  452.1 14.9 %gather_fusion.1 = bf16[1280,2048]{1,0:T(8,128)(2,1)} fusion(bf16[1792,2048]{1,0:T(8,128)(2,1)} %bitcast.23, s32[2048]{0:T(1024)S(1)} %pad_clamp_fusion), kind=kCustom, calls=%fused_computation.1 | custom fusion | bytes 10490880 | tf_op jit(solution)/shard_map/gather | solution.py:130
  467.0 9.5 %reshape.186 = bf16[128,10,2048]{2,1,0:T(8,128)(2,1)} reshape(bf16[1280,2048]{1,0:T(8,128)(2,1)} %gather_fusion.1) | data formatting | bytes 10485760 | tf_op jit(solution)/shard_map/reshape | solution.py:130
  476.6 6.0 %fusion.63 = bf16[128,1,2048]{2,1,0:T(2,128)(2,1)S(1)} fusion(bf16[128,10,2048]{2,1,0:T(8,128)(2,1)} %reshape.186, f32[128,10,1]{1,2,0:T(1,128)S(1)} %copy.128), kind=kOutput, calls=%fused_computation.119 | convolution fusion | flops 31457280 | bytes 5772288 | tf_op jit(solution)/shard_map/tk,tkd->td/dot_general | solution.py:131
  (97 shorter events, 21.0 us)
Async XLA Ops:
  7.2 22.8 %copy-start.8 = (bf16[128,2048]{1,0:T(8,128)(2,1)S(1)}, bf16[128,2048]{1,0:T(8,128)(2,1)}, u32[]{:S(2)}) copy-start(bf16[128,2048]{1,0:T(8,128)(2,1)} %param.18) | copy-start | bytes 1572868
  7.2 24.5 %copy-start.9 = (bf16[128,2048]{1,0:T(8,128)(2,1)S(1)}, bf16[128,2048]{1,0:T(8,128)(2,1)}, u32[]{:S(2)}) copy-start(bf16[128,2048]{1,0:T(8,128)(2,1)} %param.19) | copy-start | bytes 1572868
  7.2 58.3 %all-gather.2.cloned.1.call-start = ((), (), s32[]{:S(2)}) async-start(), calls=%async_computation.2 | async-start | bytes 5242880 | tf_op jit(solution)/shard_map/all_gather | solution.py:41
  10.0 22.4 %copy-start.13 = (f32[16,128]{1,0:T(8,128)S(1)}, f32[16,128]{1,0:T(8,128)}, u32[]{:S(2)}) copy-start(f32[16,128]{1,0:T(8,128)} %param.23) | copy-start | bytes 24580
  10.0 22.7 %copy-start.12 = (bf16[128,2048]{1,0:T(8,128)(2,1)S(1)}, bf16[128,2048]{1,0:T(8,128)(2,1)}, u32[]{:S(2)}) copy-start(bf16[128,2048]{1,0:T(8,128)(2,1)} %param.20) | copy-start | bytes 1572868
  23.8 10.7 %copy-start.10 = (bf16[128,2048]{1,0:T(8,128)(2,1)S(1)}, bf16[128,2048]{1,0:T(8,128)(2,1)}, u32[]{:S(2)}) copy-start(bf16[128,2048]{1,0:T(8,128)(2,1)} %param.21) | copy-start | bytes 1572868
  30.3 1.0 copy-start
  51.9 7.2 %copy-start.2 = (f32[128,16,128]{2,0,1:T(8,128)S(1)}, f32[128,16,128]{2,0,1:T(8,128)}, u32[]{:S(2)}) copy-start(f32[128,16,128]{2,0,1:T(8,128)} %copy.107) | copy-start | bytes 3145732
  65.5 9.1 %copy-start.16 = (f32[128]{0:T(128)S(1)}, f32[128]{0:T(128)}, u32[]{:S(2)}) copy-start(f32[128]{0:T(128)} %param.24) | copy-start | bytes 1540
  65.5 6.0 %copy-start.4 = (f32[16,128,128]{2,1,0:T(8,128)S(1)}, f32[16,128,128]{2,1,0:T(8,128)}, u32[]{:S(2)}) copy-start(f32[16,128,128]{2,1,0:T(8,128)} %fusion.36) | copy-start | bytes 3145732
  65.5 6.0 %copy-start.6 = (f32[16,128,128]{2,1,0:T(8,128)S(1)}, f32[16,128,128]{2,1,0:T(8,128)}, u32[]{:S(2)}) copy-start(f32[16,128,128]{2,1,0:T(8,128)} %fusion.34) | copy-start | bytes 3145732
  65.5 7.1 %copy-start.5 = (f32[16,128,128]{2,1,0:T(8,128)S(1)}, f32[16,128,128]{2,1,0:T(8,128)}, u32[]{:S(2)}) copy-start(f32[16,128,128]{2,1,0:T(8,128)} %convolution_multiply_fusion.1) | copy-start | bytes 3145732
  65.5 9.0 %copy-start.3 = (f32[128,2048]{0,1:T(8,128)S(1)}, f32[128,2048]{0,1:T(8,128)}, u32[]{:S(2)}) copy-start(f32[128,2048]{0,1:T(8,128)} %copy.111) | copy-start | bytes 3145732
  71.4 7.0 %copy-start.11 = (bf16[128,2048]{1,0:T(8,128)(2,1)S(1)}, bf16[128,2048]{1,0:T(8,128)(2,1)}, u32[]{:S(2)}) copy-start(bf16[128,2048]{1,0:T(8,128)(2,1)} %param.17) | copy-start | bytes 1572868
  71.4 8.4 %copy-start.14 = (f32[2048]{0:T(1024)S(1)}, f32[2048]{0:T(1024)}, u32[]{:S(2)}) copy-start(f32[2048]{0:T(1024)} %param.25) | copy-start | bytes 24580
  79.8 8.3 %copy-start.7 = (bf16[128,2048]{1,0:T(8,128)(2,1)}, bf16[128,2048]{1,0:T(8,128)(2,1)S(1)}, u32[]{:S(2)}) copy-start(bf16[128,2048]{1,0:T(8,128)(2,1)S(1)} %get-tuple-element.6) | copy-start | bytes 1572868
  251.8 3.0 copy-start.1
  285.6 8.4 %copy-start.15 = (f32[128,10]{0,1:T(8,128)S(1)}, f32[128,10]{0,1:T(8,128)}, u32[]{:S(2)}) copy-start(f32[128,10]{0,1:T(8,128)} %param.30) | copy-start | bytes 15364
  285.6 166.5 %all-to-all-start.1 = ((bf16[8,4,56,2048]{3,2,1,0:T(8,128)(2,1)}), bf16[8,4,56,2048]{3,2,1,0:T(8,128)(2,1)}, u32[]{:S(2)}, u32[]{:S(2)}) async-start(bf16[8,4,56,2048]{3,2,1,0:T(8,128)(2,1)} %copy.120), calls=%async_computation.1 | async-start | bytes 14680064 | tf_op jit(solution)/shard_map/all_to_all | solution.py:129
Sparse Core Ops, SparseCore 0:
  10.2 53.8 all-gather.1
where the time goes:
time: 499 us; the launch traced here: 491 us
  blocking collectives  164 us (33%)
  waiting for transfers between devices  153 us (31%)
  matrix products  65.1 us (13%)
  local copies, waits for them, and re-layouts  59 us (12%)
  other arithmetic  24.9 us (5%)
  between operations  16.1 us (3%)
  starting transfers between devices  8.44 us (2%)
    all_to_all x1, blocking collectives, local(): lax.all_to_all(outgoing, 'expert', split_axis=0, concat_axis=0, tiled=True)  164 us
    all_to_all x1, waiting for transfers between devices, local(): lax.all_to_all(rows_out, 'expert', split_axis=0, concat_axis=0, tiled=True)  153 us
    dot_general x1, matrix products, local(): jnp.einsum('aemf,efd->aemd', hidden_rows, w_down, preferred_element_type=...  15 us
    gather x1, local copies, waits for them, and re-layouts, local(): returned.reshape(experts_all * MOST, -1)[slot_index]  14.9 us
  transfers between devices with their start and end apart: 2, of which 1 were waited for; matrix products, arithmetic and copies ran while one was open for 12% of the time, Pallas kernels for 0%

commit v1 on v0

v1 whole, which is shorter than its diff:
```python
import jax
import jax.numpy as jnp
from jax import lax
from jax.experimental import pallas as pl
from jax.experimental.pallas import tpu as pltpu
from jax.sharding import PartitionSpec as P

MOST = 56
PAIR = 2 * MOST
EPS = 1e-06
HEADS_A_STEP = 4
STATE_CHUNKS = 4
RETURN_CHUNKS = 4
BF = jnp.bfloat16
F32 = jnp.float32
VMEM_BYTES = 60 * 1024 * 1024


def iota(shape, dim):
    return lax.broadcasted_iota(jnp.int32, shape, dim)


def mm(a, b):
    return jnp.dot(a, b, preferred_element_type=F32)


def silu(x):
    return x / (1.0 + jnp.exp(-x))


def prepare_kernel(q_ref, k_ref, lb_ref, lbt_ref, kq_ref, t_ref, mk_ref):
    rows = q_ref.shape[0]
    dk = 128
    at_row = iota((rows, rows), 0)
    at_col = iota((rows, rows), 1)
    strict = at_row > at_col
    inclusive = at_row >= at_col
    lower = inclusive.astype(F32)
    upper = (at_row <= at_col).astype(F32)
    top = lax.Precision.HIGHEST
    total_row = jnp.dot(lb_ref[0], upper, precision=top, preferred_element_type=F32)
    total_col = jnp.dot(lower, lbt_ref[0], precision=top, preferred_element_type=F32)
    solved = []
    mixes = []
    for i in range(HEADS_A_STEP):
        span = slice(i * dk, (i + 1) * dk)
        q = q_ref[:, span].astype(F32)
        k = k_ref[:, span].astype(F32)
        q = q / jnp.sqrt(jnp.sum(q * q, axis=-1, keepdims=True) + EPS)
        k = k / jnp.sqrt(jnp.sum(k * k, axis=-1, keepdims=True) + EPS)
        l_col = total_col[:, i : i + 1]
        l_row = total_row[i : i + 1, :]
        beta = lbt_ref[0][:, HEADS_A_STEP + i : HEADS_A_STEP + i + 1]
        ratio = jnp.where(inclusive, jnp.exp(jnp.where(inclusive, l_col - l_row, 0.0)), 0.0)
        kb = k.astype(BF)
        both = lax.dot_general(
            jnp.concatenate([kb, q.astype(BF)], axis=0),
            kb,
            (((1,), (1,)), ((), ())),
            preferred_element_type=F32,
        )
        mix = jnp.where(strict, beta * ratio * both[:rows], 0.0)
        growth = jnp.exp(l_col)
        trail = jnp.exp(l_col[rows - 1 : rows, :] - l_col)
        kq_ref[i] = jnp.concatenate([k * (beta * growth), q * growth], axis=0).astype(BF)
        mk_ref[i] = jnp.concatenate(
            [ratio * both[rows:], jnp.transpose(k * trail)], axis=0
        ).astype(BF)
        mixes.append(mix)
        first = (at_row // 2 == at_col // 2) & strict
        solved.append((at_row == at_col).astype(F32) - jnp.where(first, mix, 0.0))
    size = 2
    while size < rows:
        here = (
            (at_row // (2 * size) == at_col // (2 * size))
            & ((at_row // size) % 2 == 1)
            & ((at_col // size) % 2 == 0)
        )
        for i in range(HEADS_A_STEP):
            t = solved[i].astype(BF)
            block = jnp.where(here, mixes[i], 0.0).astype(BF)
            solved[i] = solved[i] - mm(t, mm(block, t).astype(BF))
        size *= 2
    for i in range(HEADS_A_STEP):
        t_ref[i] = solved[i].astype(BF)


def prepare(queries, keys_in, lb, lbt):
    rows = queries.shape[0]
    groups = lb.shape[0]
    heads = groups * HEADS_A_STEP
    wide = HEADS_A_STEP * 128
    return pl.pallas_call(
        prepare_kernel,
        grid=(groups,),
        in_specs=[
            pl.BlockSpec((rows, wide), lambda i: (0, i)),
            pl.BlockSpec((rows, wide), lambda i: (0, i)),
            pl.BlockSpec((1,) + lb.shape[1:], lambda i: (i, 0, 0)),
            pl.BlockSpec((1,) + lbt.shape[1:], lambda i: (i, 0, 0)),
        ],
        out_specs=[
            pl.BlockSpec((HEADS_A_STEP, 2 * rows, 128), lambda i: (i, 0, 0)),
            pl.BlockSpec((HEADS_A_STEP, rows, rows), lambda i: (i, 0, 0)),
            pl.BlockSpec((HEADS_A_STEP, rows + 128, rows), lambda i: (i, 0, 0)),
        ],
        out_shape=[
            jax.ShapeDtypeStruct((heads, 2 * rows, 128), BF),
            jax.ShapeDtypeStruct((heads, rows, rows), BF),
            jax.ShapeDtypeStruct((heads, rows + 128, rows), BF),
        ],
        compiler_params=pltpu.CompilerParams(vmem_limit_bytes=VMEM_BYTES),
        cost_estimate=pl.CostEstimate(flops=int(2e9), transcendentals=0, bytes_accessed=4000000),
        name="prepare",
    )(queries, keys_in, lb, lbt)


def resume_kernel(pick_ref, *refs, peers, first_head):
    cache_ref, got_refs, refs = refs[0], refs[1 : 1 + peers], refs[1 + peers :]
    kq_ref, t_ref, mk_ref, v_ref, lb_ref, lbt_ref, gate_ref, res_ref, gain_ref = refs[:9]
    out_ref, next_ref, own_buf, got_buf, sem_own, sem_got = refs[9:]
    heads, rows, _ = t_ref.shape
    place = pick_ref[0]
    slot = pick_ref[1]
    own = pltpu.make_async_copy(cache_ref.at[0, slot, pl.ds(first_head, heads)], own_buf, sem_own)
    own.start()
    for j in range(peers):

        @pl.when(place == j + 1)
        def _(j=j):
            copy = pltpu.make_async_copy(got_refs[j], got_buf, sem_got)
            copy.start()
            copy.wait()

    own.wait()
    here = place == 0
    for i in range(heads):
        span = slice(i * 128, (i + 1) * 128)
        state = jnp.where(here, own_buf[i], got_buf[i].astype(F32))
        beta = lbt_ref[0][:, HEADS_A_STEP + i : HEADS_A_STEP + i + 1]
        read = mm(kq_ref[i], state.astype(BF))
        rest = beta * v_ref[:, span].astype(F32) - read[:rows]
        fixed = mm(t_ref[i], rest.astype(BF)).astype(BF)
        added = mm(mk_ref[i], fixed)
        o = read[rows:] + added[:rows]
        last = jnp.exp(jnp.sum(lb_ref[0][i : i + 1, :], axis=-1, keepdims=True))
        next_ref[i] = last * state + added[rows:]
        scaled = o / jnp.sqrt(jnp.mean(o * o, axis=-1, keepdims=True) + EPS) * gain_ref[...]
        gated = scaled * silu(gate_ref[:, span].astype(F32))
        out_ref[:, span] = (res_ref[:, span].astype(F32) + gated).astype(BF)


def resume(pick, cache, got, kq, t, mk, values, lb, lbt, gate, residual, gain, group, heads):
    rows = values.shape[0]
    wide = heads * 128
    any_spec = pl.BlockSpec(memory_space=pl.ANY)
    cols = pl.BlockSpec((rows, wide), lambda i, p: (0, group))
    import_heads = lambda i, p: (group, 0, 0)
    return pl.pallas_call(
        lambda *refs: resume_kernel(*refs, peers=len(got), first_head=group * heads),
        grid_spec=pltpu.PrefetchScalarGridSpec(
            num_scalar_prefetch=1,
            grid=(1,),
            in_specs=[any_spec]
            + [any_spec] * len(got)
            + [
                pl.BlockSpec((heads,) + kq.shape[1:], import_heads),
                pl.BlockSpec((heads,) + t.shape[1:], import_heads),
                pl.BlockSpec((heads,) + mk.shape[1:], import_heads),
                cols,
                pl.BlockSpec((1,) + lb.shape[1:], import_heads),
                pl.BlockSpec((1,) + lbt.shape[1:], import_heads),
                cols,
                cols,
                pl.BlockSpec((1, 128), lambda i, p: (0, 0)),
            ],
            out_specs=[
                pl.BlockSpec((rows, wide), lambda i, p: (0, 0)),
                pl.BlockSpec((heads, 128, 128), lambda i, p: (0, 0, 0)),
            ],
            scratch_shapes=[
                pltpu.VMEM((heads, 128, 128), F32),
                pltpu.VMEM((heads, 128, 128), BF),
                pltpu.SemaphoreType.DMA,
                pltpu.SemaphoreType.DMA,
            ],
        ),
        out_shape=[
            jax.ShapeDtypeStruct((rows, wide), BF),
            jax.ShapeDtypeStruct((heads, 128, 128), F32),
        ],
        compiler_params=pltpu.CompilerParams(vmem_limit_bytes=VMEM_BYTES),
        cost_estimate=pl.CostEstimate(flops=int(1e9), transcendentals=0, bytes_accessed=3000000),
        name="resume",
    )(pick, cache, *got, kq, t, mk, values, lb, lbt, gate, residual, gain)


def hidden_kernel(*refs, blocks, parts, normed):
    count = 1 if normed else blocks * parts
    x_refs, refs = refs[:count], refs[count:]
    gain_ref, pos_ref, wt_ref, wg_ref, wu_ref, out_ref = refs[:6]
    if normed:
        all_ref = x_refs[0]
        chosen_ref = refs[6]
    else:
        all_ref, chosen_ref = refs[6:8]
        slab = 16

        @pl.when(pl.program_id(0) == 0)
        def _():
            gain = gain_ref[...]
            rows = x_refs[0].shape[0]
            for b in range(blocks):

                def step(s, carry, b=b):
                    at = pl.multiple_of(s * slab, slab)
                    x = jnp.concatenate(
                        [x_refs[b * parts + c][pl.ds(at, slab), :] for c in range(parts)], axis=1
                    ).astype(F32)
                    mean = jnp.mean(x * x, axis=-1, keepdims=True)
                    to = pl.multiple_of(b * rows + s * slab, slab)
                    all_ref[pl.ds(to, slab), :] = (x / jnp.sqrt(mean + EPS) * gain).astype(BF)
                    return carry

                lax.fori_loop(0, rows // slab, step, 0)

    pairs = pos_ref.shape[1]
    two = pos_ref.shape[3]
    weights = []
    for p in range(pairs):
        sel = iota((PAIR, two), 0) == pos_ref[0, p]
        weights.append(jnp.sum(jnp.where(sel, wt_ref[0, p], 0.0), axis=1, keepdims=True))
        chosen_ref[p * PAIR : (p + 1) * PAIR, :] = mm(
            sel.astype(F32).astype(BF), all_ref[p * two : (p + 1) * two, :]
        ).astype(BF)
    together = min(pairs, 4)
    for p in range(0, pairs, together):
        span = slice(p * PAIR, (p + together) * PAIR)
        x = chosen_ref[span, :]
        gate = mm(x, wg_ref[0])
        up = mm(x, wu_ref[0])
        weight = jnp.concatenate(weights[p : p + together], axis=0)
        out_ref[0, span, :] = (silu(gate) * up * weight).astype(BF)


def hidden(xs, parts, gain, pos, wt, w_gate, w_up, normed):
    experts, d, ff = w_gate.shape
    pairs, two = pos.shape[1], pos.shape[3]
    blocks = 2 * pairs
    one = pl.Buffered(1)
    scratch = [pltpu.VMEM((pairs * PAIR, d), BF)]
    if not normed:
        scratch = [pltpu.VMEM((pairs * two, d), BF)] + scratch
    return pl.pallas_call(
        lambda *refs: hidden_kernel(*refs, blocks=blocks, parts=parts, normed=normed),
        grid=(experts,),
        in_specs=[pl.BlockSpec(x.shape, lambda e: (0, 0), pipeline_mode=one) for x in xs]
        + [
            pl.BlockSpec((1, d), lambda e: (0, 0)),
            pl.BlockSpec((1, pairs, 1, two), lambda e: (e, 0, 0, 0)),
            pl.BlockSpec((1, pairs, 1, two), lambda e: (e, 0, 0, 0)),
            pl.BlockSpec((1, d, ff), lambda e: (e, 0, 0)),
            pl.BlockSpec((1, d, ff), lambda e: (e, 0, 0)),
        ],
        out_specs=pl.BlockSpec((1, pairs * PAIR, ff), lambda e: (e, 0, 0)),
        out_shape=jax.ShapeDtypeStruct((experts, pairs * PAIR, ff), BF),
        scratch_shapes=scratch,
        compiler_params=pltpu.CompilerParams(vmem_limit_bytes=VMEM_BYTES),
        cost_estimate=pl.CostEstimate(flops=int(9e9), transcendentals=0, bytes_accessed=24000000),
        name="hidden",
    )(*xs, gain, pos, wt, w_gate, w_up)


def down_kernel(pos_ref, h_ref, w_ref, own_ref, other_ref, sel_ref, rows_ref):
    experts = h_ref.shape[0]
    pairs, two, deep = sel_ref.shape
    half = two // 2

    @pl.when(pl.program_id(0) == 0)
    def _():
        lane = iota((two, deep), 1)
        for p in range(pairs):
            at = pos_ref[p * two : (p + 1) * two, :]
            hit = lane == at[:, 0:1]
            for e in range(1, experts):
                hit = hit | (lane == at[:, e : e + 1])
            sel_ref[p] = hit.astype(F32).astype(BF)

    for e in range(experts):
        rows = mm(h_ref[e], w_ref[e]).astype(BF)
        for p in range(pairs):
            rows_ref[p, e * PAIR : (e + 1) * PAIR, :] = rows[p * PAIR : (p + 1) * PAIR]
    for p in range(pairs):
        both = mm(sel_ref[p], rows_ref[p]).astype(BF)
        own_ref[p] = both[:half]
        other_ref[p] = both[half:]


def down(pos, h, w_down, chunk, chunks, two):
    experts, ff, d = w_down.shape
    pairs = h.shape[1] // PAIR
    wide = d // chunks
    tile = min(256, wide)
    steps = wide // tile
    out = jax.ShapeDtypeStruct((pairs, two // 2, wide), BF)
    out_spec = pl.BlockSpec((pairs, two // 2, tile), lambda n: (0, 0, n))
    return pl.pallas_call(
        down_kernel,
        grid=(steps,),
        in_specs=[
            pl.BlockSpec(pos.shape, lambda n: (0, 0)),
            pl.BlockSpec(h.shape, lambda n: (0, 0, 0)),
            pl.BlockSpec((experts, ff, tile), lambda n: (0, 0, chunk * steps + n)),
        ],
        out_specs=[out_spec, out_spec],
        out_shape=[out, out],
        scratch_shapes=[
            pltpu.VMEM((pairs, two, experts * PAIR), BF),
            pltpu.VMEM((pairs, experts * PAIR, tile), BF),
        ],
        compiler_params=pltpu.CompilerParams(vmem_limit_bytes=VMEM_BYTES),
        cost_estimate=pl.CostEstimate(
            flops=int(6e9) // chunks, transcendentals=0, bytes_accessed=12000000 // chunks
        ),
        name="down",
    )(pos, h, w_down)


def swap(x, axis, bits):
    size = lax.axis_size(axis)
    return lax.ppermute(x, axis, [(i, i ^ bits) for i in range(size)])


def local(
    residual_in,
    queries,
    keys_in,
    values_in,
    out_gate,
    log_decay,
    beta_rate,
    head_gain,
    moe_gain,
    state_cache,
    hit_holder,
    hit_slot,
    expert_ids,
    gate_weight,
    w_gate,
    w_up,
    w_down,
):
    rows, d = queries.shape
    head_count = log_decay.shape[0]
    holders = lax.axis_size("dp")
    group = lax.axis_size("expert")
    own_dp = lax.axis_index("dp")
    own_ep = lax.axis_index("expert")
    experts = w_gate.shape[0]
    pairs = group // 2
    heads = head_count // STATE_CHUNKS

    wish = jnp.concatenate([hit_holder, hit_slot])
    sends = []
    for j in range(1, holders):
        asked = swap(wish, "dp", j)
        sends.append(jnp.where(asked[0] == own_dp, asked[1], 0))
    got = []
    for g in range(STATE_CHUNKS):
        got.append([])
        for j in range(1, holders):
            piece = lax.dynamic_slice(
                state_cache, (0, sends[j - 1], g * heads, 0, 0), (1, 1, heads) + state_cache.shape[3:]
            )[0, 0].astype(BF)
            got[g].append(swap(piece, "dp", j))
    pick = jnp.stack([hit_holder[0] ^ own_dp, hit_slot[0]])

    all_experts = group * experts
    named = expert_ids.T[None] == jnp.arange(all_experts, dtype=jnp.int32)[:, None, None]
    dense = jnp.sum(jnp.where(named, gate_weight.T[None], 0.0), axis=1)
    spread = lax.all_gather(dense, "expert", axis=0).reshape(group, group, experts, rows)
    mine = lax.dynamic_index_in_dim(spread, own_ep, 1, False)
    order = jnp.arange(group, dtype=jnp.int32) ^ own_ep
    mine = mine[order]
    routed = mine > 0.0
    before = jnp.arange(rows)[:, None] < jnp.arange(rows)[None, :]
    rank = jnp.dot(
        routed.astype(F32).reshape(group * experts, rows), before.astype(F32)
    ).reshape(group, experts, rows)
    rank = rank.astype(jnp.int32) + (jnp.arange(group, dtype=jnp.int32) % 2 * MOST)[:, None, None]
    rank = jnp.where(routed, rank, -100000)
    pos_row = rank.transpose(1, 0, 2).reshape(experts, pairs, 1, 2 * rows)
    wt_row = mine.transpose(1, 0, 2).reshape(experts, pairs, 1, 2 * rows)
    pos_col = rank.transpose(0, 2, 1).reshape(group * rows, experts)
    pos_col = pos_col + jnp.arange(experts, dtype=jnp.int32)[None, :] * PAIR

    groups = head_count // HEADS_A_STEP
    lb = jnp.concatenate(
        [
            log_decay.reshape(groups, HEADS_A_STEP, rows),
            beta_rate.reshape(groups, HEADS_A_STEP, rows),
        ],
        axis=1,
    )
    lbt = lb.transpose(0, 2, 1)
    kq, t, mk = prepare(queries, keys_in, lb, lbt)
    mixed, states = [], []
    for g in range(STATE_CHUNKS):
        m, s = resume(
            pick, state_cache, got[g], kq, t, mk, values_in, lb, lbt, out_gate, residual_in,
            head_gain[None], g, heads,
        )
        mixed.append(m)
        states.append(s)

    mixer_out = jnp.concatenate(mixed, axis=1)

    gain = moe_gain[None]
    outs = []
    if group <= 8:
        blocks = [[None] * STATE_CHUNKS for _ in range(group)]
        for c in range(STATE_CHUNKS):
            for r in range(pairs):
                near = mixed[c] if r == 0 else swap(mixed[c], "expert", 2 * r)
                blocks[2 * r][c] = near
                blocks[2 * r + 1][c] = swap(near, "expert", 1)
        xs = [blocks[b][c] for b in range(group) for c in range(STATE_CHUNKS)]
        h = hidden(xs, STATE_CHUNKS, gain, pos_row, wt_row, w_gate, w_up, False)
        for c in range(RETURN_CHUNKS):
            own, other = down(pos_col, h, w_down, c, RETURN_CHUNKS, 2 * rows)
            came = swap(other, "expert", 1)
            total = own[0].astype(F32) + came[0].astype(F32)
            for r in range(1, pairs):
                chip = (own[r].astype(F32) + came[r].astype(F32)).astype(BF)
                total = total + swap(chip, "expert", 2 * r).astype(F32)
            outs.append(total.astype(BF))
    else:
        x = lax.all_gather(mixer_out, "expert", axis=0)[order].reshape(group * rows, d).astype(F32)
        x = (x / jnp.sqrt(jnp.mean(x * x, axis=-1, keepdims=True) + EPS) * gain).astype(BF)
        h = hidden([x], 1, gain, pos_row, wt_row, w_gate, w_up, True)
        for c in range(RETURN_CHUNKS):
            own, other = down(pos_col, h, w_down, c, RETURN_CHUNKS, 2 * rows)
            part = jnp.stack([own, other], axis=1).reshape(group, rows, -1)[order]
            outs.append(lax.psum_scatter(part, "expert", scatter_dimension=0))
    expert_out = jnp.concatenate(outs, axis=1)
    return (mixer_out, expert_out, jnp.concatenate(states, axis=0)[None])


def solution(mesh):
    both = ("dp", "expert")
    rows = P(both, None)
    placed = (
        rows,
        rows,
        rows,
        rows,
        rows,
        P(None, both),
        P(None, both),
        P(),
        P(),
        P(both, None, None, None, None),
        P(both),
        P(both),
        rows,
        rows,
        P("expert", None, None),
        P("expert", None, None),
        P("expert", None, None),
    )
    return jax.shard_map(
        local,
        mesh=mesh,
        in_specs=placed,
        out_specs=(rows, rows, P(both, None, None, None)),
        check_vma=False,
    )
```

time: 499 us -> 224 us (0.45); the launches traced: 491 us -> 223 us
  blocking collectives: 164 us -> 12.2 us
  waiting for transfers between devices: 153 us -> 48.8 us
  Pallas kernels: 0 us -> 76.5 us
  matrix products: 65.1 us -> 0.74 us
  starting transfers between devices: 8.44 us -> 62.2 us
  local copies, waits for them, and re-layouts: 59 us -> 6.12 us
  other arithmetic: 24.9 us -> 9.99 us
  between operations: 16.1 us -> 6.48 us
    all_to_all x1 -> x0, blocking collectives: 164 us -> none  [local(): lax.all_to_all(outgoing, 'expert', split_axis=0, concat_axis=0, tiled=True)]
    all_to_all x1 -> x0, waiting for transfers between devices: 153 us -> none  [local(): lax.all_to_all(rows_out, 'expert', split_axis=0, concat_axis=0, tiled=True)]
    pallas_call x0 -> x10, Pallas kernels: none -> 76.5 us  [the longest x4 24.2 us: down(): pl.pallas_call(down_kernel, grid=(steps,), in_specs=[pl.BlockSpec(pos.sha...]
    dot_general x23 -> x1, matrix products: 65.1 us -> 0.74 us  [local(): jnp.dot(routed.astype(F32).reshape(group * experts, rows), before.astype(...]
    ppermute x0 -> x59, starting transfers between devices: none -> 62.2 us  [swap(): return lax.ppermute(x, axis, [(i, i ^ bits) for i in range(size)])]
    ppermute x0 -> x59, waiting for transfers between devices: none -> 48.8 us  [swap(): return lax.ppermute(x, axis, [(i, i ^ bits) for i in range(size)])]
    gather x2, local copies, waits for them, and re-layouts: 22.9 us -> 1.3 us  [local(): mine = mine[order]]
    all_gather x0 -> x1, blocking collectives: none -> 12.2 us  [local(): lax.all_gather(dense, 'expert', axis=0).reshape(group, group, experts, rows)]
  transfers between devices with their start and end apart: 2 -> 59, of which waited for: 1 -> 12; matrix products, arithmetic and copies ran while one was open for 12% -> 6% of each run, Pallas kernels for 0% -> 21%
where the time goes in v1:
time: 224 us; the launch traced here: 223 us
  Pallas kernels  76.5 us (34%)
  starting transfers between devices  62.2 us (28%)
  waiting for transfers between devices  48.8 us (22%)
  blocking collectives  12.2 us (5%)
  other arithmetic  9.99 us (4%)
  between operations  6.48 us (3%)
  local copies, waits for them, and re-layouts  6.12 us (3%)
    ppermute x59, starting transfers between devices, swap(): return lax.ppermute(x, axis, [(i, i ^ bits) for i in range(size)])  62.2 us
    ppermute x59, waiting for transfers between devices, swap(): return lax.ppermute(x, axis, [(i, i ^ bits) for i in range(size)])  48.8 us
    pallas_call x4, Pallas kernels, down(): pl.pallas_call(down_kernel, grid=(steps,), in_specs=[pl.BlockSpec(pos.sha...  24.2 us
    pallas_call x1, Pallas kernels, hidden(): pl.pallas_call(lambda *refs: hidden_kernel(*refs, blocks=blocks, parts=pa...  23.1 us
    pallas_call x4, Pallas kernels, resume(): pl.pallas_call(lambda *refs: resume_kernel(*refs, peers=len(got), first_h...  18.3 us
    all_gather x1, blocking collectives, local(): lax.all_gather(dense, 'expert', axis=0).reshape(group, group, experts, rows)  12.2 us
    pallas_call x1, Pallas kernels, prepare(): pl.pallas_call(prepare_kernel, grid=(groups,), in_specs=[pl.BlockSpec((ro...  10.8 us
  transfers between devices with their start and end apart: 59, of which 12 were waited for; matrix products, arithmetic and copies ran while one was open for 6% of the time, Pallas kernels for 21%

profile of v1, /device:TPU:16, one launch (start us, length us, event | category | flops | bytes accessed | tf_op | source)
XLA Modules:
  0.0 223.1 jit_solution(10265471926121088268)
XLA Ops:
  3.7 1.5 collective-permute-start.2
  8.6 10.8 %prepare.1 = (bf16[16,256,128]{2,1,0:T(8,128)(2,1)}, bf16[16,128,128]{2,1,0:T(8,128)(2,1)}, bf16[16,256,128]{2,1,0:T(8,128)(2,1)}) custom-call(bf16[128,2048]{1,0:T(8,128)(2,1)} %q_ref.1, bf16[128,2048]{1,0:T(8,128)(2,1)} %k_ref.1, f32[4,8,128]{2,1,0:T(8,128)} %copy-done.1, f32[4,128,8]{2,1,0:T(8,128)} %bitcast.121), custom_call_target="tpu_custom_call" | custom-call | flops 2000000000 | bytes 4000000 | tf_op jit(solution)/shard_map/prepare/pallas_call | solution.py:93
  27.3 1.5 collective-permute-start.3
  30.7 1.5 collective-permute-start.7
  32.3 12.2 %all-gather = f32[256,128]{1,0:T(8,128)S(1)} all-gather(f32[32,128]{1,0:T(8,128)S(1)} %select_reduce_fusion), channel_id=2, replica_groups=mesh['dp'=4,'expert'=8] {'expert'}, dimensions={0}, use_global_device_ids=true | all-gather | bytes 147456 | tf_op jit(solution)/shard_map/all_gather | solution.py:381
  45.1 1.5 collective-permute-start.10
  50.7 4.5 %resume.4 = (bf16[128,512]{1,0:T(8,128)(2,1)}, f32[4,128,128]{2,1,0:T(8,128)}) custom-call(s32[2]{0:T(128)} %pad_add_fusion.refs_0_, f32[1,2,16,128,128]{4,3,2,1,0:T(8,128)} %refs_1_.7, bf16[4,128,128]{2,1,0:T(8,128)(2,1)} %copy-done.18, bf16[4,128,128]{2,1,0:T(8,128)(2,1)} %copy-done.19, bf16[4,128,128]{2,1,0:T(8,128)(2,1)} %copy-done.20, ...), custom_call_target="tpu_custom_call" | custom-call | flops 1000000000 | bytes 3000000 | tf_op jit(solution)/shard_map/resume/pallas_call | solution.py:159
  55.3 1.6 collective-permute-start.13
  57.4 3.3 %collective-permute-start.19 = (bf16[128,512]{1,0:T(8,128)(2,1)}, bf16[128,512]{1,0:T(8,128)(2,1)S(1)}, u32[]{:S(2)}, u32[]{:S(2)}) collective-permute-start(bf16[128,512]{1,0:T(8,128)(2,1)} %get-tuple-element.25.refs_0_), channel_id=1, source_target_pairs={{0,2},{1,3},{2,0},{3,1},{4,6},{5,7},{6,4},{7,5},{8,10},{9,11},{10,... | collective-permute-start | bytes 393224 | tf_op jit(solution)/shard_map/ppermute | solution.py:331
  63.0 4.6 %resume.5 = (bf16[128,512]{1,0:T(8,128)(2,1)}, f32[4,128,128]{2,1,0:T(8,128)}) custom-call(s32[2]{0:T(128)} %pad_add_fusion.refs_0_, f32[1,2,16,128,128]{4,3,2,1,0:T(8,128)} %refs_1_.7, bf16[4,128,128]{2,1,0:T(8,128)(2,1)} %copy-done.10, bf16[4,128,128]{2,1,0:T(8,128)(2,1)} %copy-done.12, bf16[4,128,128]{2,1,0:T(8,128)(2,1)} %copy-done.16, ...), custom_call_target="tpu_custom_call" | custom-call | flops 1000000000 | bytes 3000000 | tf_op jit(solution)/shard_map/resume/pallas_call | solution.py:159
  67.7 2.9 %collective-permute-start.20 = (bf16[128,512]{1,0:T(8,128)(2,1)}, bf16[128,512]{1,0:T(8,128)(2,1)S(1)}, u32[]{:S(2)}, u32[]{:S(2)}) collective-permute-start(bf16[128,512]{1,0:T(8,128)(2,1)} %get-tuple-element.26.refs_1_), channel_id=1, source_target_pairs={{0,2},{1,3},{2,0},{3,1},{4,6},{5,7},{6,4},{7,5},{8,10},{9,11},{10,... | collective-permute-start | bytes 393224 | tf_op jit(solution)/shard_map/ppermute | solution.py:331
  72.1 8.0 %collective-permute-done.35.refs_24_ = bf16[128,512]{1,0:T(8,128)(2,1)S(1)} collective-permute-done((bf16[128,512]{1,0:T(8,128)(2,1)}, bf16[128,512]{1,0:T(8,128)(2,1)S(1)}, u32[]{:S(2)}, u32[]{:S(2)}) %collective-permute-start.35) | collective-permute-done | bytes 131104 | tf_op jit(solution)/shard_map/ppermute | solution.py:331
  80.2 4.5 %resume.6 = (bf16[128,512]{1,0:T(8,128)(2,1)}, f32[4,128,128]{2,1,0:T(8,128)}) custom-call(s32[2]{0:T(128)} %pad_add_fusion.refs_0_, f32[1,2,16,128,128]{4,3,2,1,0:T(8,128)} %refs_1_.7, bf16[4,128,128]{2,1,0:T(8,128)(2,1)} %copy-done.14, bf16[4,128,128]{2,1,0:T(8,128)(2,1)} %copy-done.9, bf16[4,128,128]{2,1,0:T(8,128)(2,1)} %copy-done.11, ...), custom_call_target="tpu_custom_call" | custom-call | flops 1000000000 | bytes 3000000 | tf_op jit(solution)/shard_map/resume/pallas_call | solution.py:159
  84.8 4.7 %resume.7 = (bf16[128,512]{1,0:T(8,128)(2,1)}, f32[4,128,128]{2,1,0:T(8,128)}) custom-call(s32[2]{0:T(128)} %pad_add_fusion.refs_0_, f32[1,2,16,128,128]{4,3,2,1,0:T(8,128)} %refs_1_.7, bf16[4,128,128]{2,1,0:T(8,128)(2,1)} %copy-done.13, bf16[4,128,128]{2,1,0:T(8,128)(2,1)} %copy-done.15, bf16[4,128,128]{2,1,0:T(8,128)(2,1)} %copy-done.17, ...), custom_call_target="tpu_custom_call" | custom-call | flops 1000000000 | bytes 3000000 | tf_op jit(solution)/shard_map/resume/pallas_call | solution.py:159
  89.7 3.4 %collective-permute-start.37 = (bf16[128,512]{1,0:T(8,128)(2,1)}, bf16[128,512]{1,0:T(8,128)(2,1)S(1)}, u32[]{:S(2)}, u32[]{:S(2)}) collective-permute-start(bf16[128,512]{1,0:T(8,128)(2,1)} %get-tuple-element.27.refs_2_), channel_id=1, source_target_pairs={{0,6},{1,7},{2,4},{3,5},{4,2},{5,3},{6,0},{7,1},{8,14},{9,15},{10,... | collective-permute-start | bytes 393224 | tf_op jit(solution)/shard_map/ppermute | solution.py:331
  97.2 5.0 %collective-permute-start.38 = (bf16[128,512]{1,0:T(8,128)(2,1)}, bf16[128,512]{1,0:T(8,128)(2,1)S(1)}, u32[]{:S(2)}, u32[]{:S(2)}) collective-permute-start(bf16[128,512]{1,0:T(8,128)(2,1)} %get-tuple-element.28.refs_3_), channel_id=1, source_target_pairs={{0,6},{1,7},{2,4},{3,5},{4,2},{5,3},{6,0},{7,1},{8,14},{9,15},{10,... | collective-permute-start | bytes 393224 | tf_op jit(solution)/shard_map/ppermute | solution.py:331
  102.2 8.6 %collective-permute-done.37.refs_26_ = bf16[128,512]{1,0:T(8,128)(2,1)S(1)} collective-permute-done((bf16[128,512]{1,0:T(8,128)(2,1)}, bf16[128,512]{1,0:T(8,128)(2,1)S(1)}, u32[]{:S(2)}, u32[]{:S(2)}) %collective-permute-start.37) | collective-permute-done | bytes 131104 | tf_op jit(solution)/shard_map/ppermute | solution.py:331
  112.8 3.6 %collective-permute-done.38.refs_27_ = bf16[128,512]{1,0:T(8,128)(2,1)S(1)} collective-permute-done((bf16[128,512]{1,0:T(8,128)(2,1)}, bf16[128,512]{1,0:T(8,128)(2,1)S(1)}, u32[]{:S(2)}, u32[]{:S(2)}) %collective-permute-start.38) | collective-permute-done | bytes 131104 | tf_op jit(solution)/shard_map/ppermute | solution.py:331
  119.4 1.8 pad_maximum_fusion
  122.3 23.1 %hidden.1.h_ref = bf16[4,448,512]{2,1,0:T(8,128)(2,1)} custom-call(bf16[128,512]{1,0:T(8,128)(2,1)} %get-tuple-element.25.refs_0_, bf16[128,512]{1,0:T(8,128)(2,1)} %get-tuple-element.26.refs_1_, bf16[128,512]{1,0:T(8,128)(2,1)} %get-tuple-element.27.refs_2_, bf16[128,512]{1,0:T(8,128)(2,1)} %get-tuple-element.28.refs_3_, bf16[128,512]{1,0:T(8,128)(2,1)} %copy-done.27, ...), custom_call_target="tpu_custom_call" | custom-call | flops 8999999488 | bytes 24000000 | tf_op jit(solution)/shard_map/hidden/pallas_call | solution.py:254
  145.5 6.1 %down.4 = (bf16[4,128,512]{2,1,0:T(8,128)(2,1)}, bf16[4,128,512]{2,1,0:T(8,128)(2,1)}) custom-call(s32[1024,4]{1,0:T(8,128)} %bitcast_add_fusion.pos_ref, bf16[4,448,512]{2,1,0:T(8,128)(2,1)} %hidden.1.h_ref, bf16[4,512,2048]{2,1,0:T(8,128)(2,1)} %w_ref.7), custom_call_target="tpu_custom_call" | custom-call | flops 1500000000 | bytes 3000000 | tf_op jit(solution)/shard_map/down/pallas_call | solution.py:307
  152.0 6.0 %down.5 = (bf16[4,128,512]{2,1,0:T(8,128)(2,1)}, bf16[4,128,512]{2,1,0:T(8,128)(2,1)}) custom-call(s32[1024,4]{1,0:T(8,128)} %bitcast_add_fusion.pos_ref, bf16[4,448,512]{2,1,0:T(8,128)(2,1)} %hidden.1.h_ref, bf16[4,512,2048]{2,1,0:T(8,128)(2,1)} %w_ref.7), custom_call_target="tpu_custom_call" | custom-call | flops 1500000000 | bytes 3000000 | tf_op jit(solution)/shard_map/down/pallas_call | solution.py:307
  159.2 6.1 %down.6 = (bf16[4,128,512]{2,1,0:T(8,128)(2,1)}, bf16[4,128,512]{2,1,0:T(8,128)(2,1)}) custom-call(s32[1024,4]{1,0:T(8,128)} %bitcast_add_fusion.pos_ref, bf16[4,448,512]{2,1,0:T(8,128)(2,1)} %hidden.1.h_ref, bf16[4,512,2048]{2,1,0:T(8,128)(2,1)} %w_ref.7), custom_call_target="tpu_custom_call" | custom-call | flops 1500000000 | bytes 3000000 | tf_op jit(solution)/shard_map/down/pallas_call | solution.py:307
  165.7 6.0 %down.7 = (bf16[4,128,512]{2,1,0:T(8,128)(2,1)}, bf16[4,128,512]{2,1,0:T(8,128)(2,1)}) custom-call(s32[1024,4]{1,0:T(8,128)} %bitcast_add_fusion.pos_ref, bf16[4,448,512]{2,1,0:T(8,128)(2,1)} %hidden.1.h_ref, bf16[4,512,2048]{2,1,0:T(8,128)(2,1)} %w_ref.7), custom_call_target="tpu_custom_call" | custom-call | flops 1500000000 | bytes 3000000 | tf_op jit(solution)/shard_map/down/pallas_call | solution.py:307
  173.2 2.4 %collective-permute-start.46 = (bf16[128,512]{1,0:T(8,128)(2,1)S(1)}, bf16[128,512]{1,0:T(8,128)(2,1)S(1)}, u32[]{:S(2)}, u32[]{:S(2)}) collective-permute-start(bf16[128,512]{1,0:T(8,128)(2,1)S(1)} %get-tuple-element.54), channel_id=1, source_target_pairs={{0,6},{1,7},{2,4},{3,5},{4,2},{5,3},{6,0},{7,1},{8,14},{9,15},{10,... | collective-permute-start | bytes 393224 | tf_op jit(solution)/shard_map/ppermute | solution.py:331
  178.6 2.1 collective-permute-start.50
  180.6 6.3 %collective-permute-start.52 = (bf16[128,512]{1,0:T(8,128)(2,1)S(1)}, bf16[128,512]{1,0:T(8,128)(2,1)S(1)}, u32[]{:S(2)}, u32[]{:S(2)}) collective-permute-start(bf16[128,512]{1,0:T(8,128)(2,1)S(1)} %get-tuple-element.59), channel_id=1, source_target_pairs={{0,2},{1,3},{2,0},{3,1},{4,6},{5,7},{6,4},{7,5},{8,10},{9,11},{10,... | collective-permute-start | bytes 393224 | tf_op jit(solution)/shard_map/ppermute | solution.py:331
  187.0 6.6 %collective-permute-done.46 = bf16[128,512]{1,0:T(8,128)(2,1)S(1)} collective-permute-done((bf16[128,512]{1,0:T(8,128)(2,1)S(1)}, bf16[128,512]{1,0:T(8,128)(2,1)S(1)}, u32[]{:S(2)}, u32[]{:S(2)}) %collective-permute-start.46) | collective-permute-done | bytes 131104 | tf_op jit(solution)/shard_map/ppermute | solution.py:331
  193.8 7.9 %collective-permute-start.56 = (bf16[128,512]{1,0:T(8,128)(2,1)S(1)}, bf16[128,512]{1,0:T(8,128)(2,1)S(1)}, u32[]{:S(2)}, u32[]{:S(2)}) collective-permute-start(bf16[128,512]{1,0:T(8,128)(2,1)S(1)} %get-tuple-element.62), channel_id=1, source_target_pairs={{0,2},{1,3},{2,0},{3,1},{4,6},{5,7},{6,4},{7,5},{8,10},{9,11},{10,... | collective-permute-start | bytes 393224 | tf_op jit(solution)/shard_map/ppermute | solution.py:331
  201.8 3.1 %collective-permute-done.50 = bf16[128,512]{1,0:T(8,128)(2,1)S(1)} collective-permute-done((bf16[128,512]{1,0:T(8,128)(2,1)S(1)}, bf16[128,512]{1,0:T(8,128)(2,1)S(1)}, u32[]{:S(2)}, u32[]{:S(2)}) %collective-permute-start.50) | collective-permute-done | bytes 131104 | tf_op jit(solution)/shard_map/ppermute | solution.py:331
  206.3 9.8 %collective-permute-done.54 = bf16[128,512]{1,0:T(8,128)(2,1)S(1)} collective-permute-done((bf16[128,512]{1,0:T(8,128)(2,1)S(1)}, bf16[128,512]{1,0:T(8,128)(2,1)S(1)}, u32[]{:S(2)}, u32[]{:S(2)}) %collective-permute-start.54) | collective-permute-done | bytes 131104 | tf_op jit(solution)/shard_map/ppermute | solution.py:331
  216.3 4.9 %collective-permute-done.58 = bf16[128,512]{1,0:T(8,128)(2,1)S(1)} collective-permute-done((bf16[128,512]{1,0:T(8,128)(2,1)S(1)}, bf16[128,512]{1,0:T(8,128)(2,1)S(1)}, u32[]{:S(2)}, u32[]{:S(2)}) %collective-permute-start.58) | collective-permute-done | bytes 131104 | tf_op jit(solution)/shard_map/ppermute | solution.py:331
  (232 shorter events, 40.4 us)
Async XLA Ops:
  2.2 17.2 %collective-permute-start = (s32[2]{0:T(128)S(1)}, s32[2]{0:T(128)S(1)}, u32[]{:S(2)}, u32[]{:S(2)}) collective-permute-start(s32[2]{0:T(128)S(1)} %pad_add_fusion.1), channel_id=1, source_target_pairs={{0,8},{8,0},{16,24},{24,16},{1,9},{9,1},{17,25},{25,17},{2,10},{10... | collective-permute-start | bytes 32 | tf_op jit(solution)/shard_map/ppermute | solution.py:331
  3.7 17.5 %collective-permute-start.2 = (s32[2]{0:T(128)S(1)}, s32[2]{0:T(128)S(1)}, u32[]{:S(2)}, u32[]{:S(2)}) collective-permute-start(s32[2]{0:T(128)S(1)} %pad_add_fusion.1), channel_id=1, source_target_pairs={{0,16},{8,24},{16,0},{24,8},{1,17},{9,25},{17,1},{25,9},{2,18},{10... | collective-permute-start | bytes 32 | tf_op jit(solution)/shard_map/ppermute | solution.py:331
  5.2 17.8 %collective-permute-start.4 = (s32[2]{0:T(128)S(1)}, s32[2]{0:T(128)S(1)}, u32[]{:S(2)}, u32[]{:S(2)}) collective-permute-start(s32[2]{0:T(128)S(1)} %pad_add_fusion.1), channel_id=1, source_target_pairs={{0,24},{8,16},{16,8},{24,0},{1,25},{9,17},{17,9},{25,1},{2,26},{10... | collective-permute-start | bytes 32 | tf_op jit(solution)/shard_map/ppermute | solution.py:331
  25.8 18.8 %collective-permute-start.1 = (bf16[4,128,128]{2,1,0:T(8,128)(2,1)}, bf16[4,128,128]{2,1,0:T(8,128)(2,1)S(1)}, u32[]{:S(2)}, u32[]{:S(2)}) collective-permute-start(bf16[4,128,128]{2,1,0:T(8,128)(2,1)} %get-tuple-element.51), channel_id=1, source_target_pairs={{0,8},{8,0},{16,24},{24,16},{1,9},{9,1},{17,25},{25,17},{2,10},{10... | collective-permute-start | bytes 393224 | tf_op jit(solution)/shard_map/ppermute | solution.py:331
  27.3 17.8 %collective-permute-start.3 = (bf16[4,128,128]{2,1,0:T(8,128)(2,1)S(1)}, bf16[4,128,128]{2,1,0:T(8,128)(2,1)S(1)}, u32[]{:S(2)}, u32[]{:S(2)}) collective-permute-start(bf16[4,128,128]{2,1,0:T(8,128)(2,1)S(1)} %get-tuple-element.50), channel_id=1, source_target_pairs={{0,16},{8,24},{16,0},{24,8},{1,17},{9,25},{17,1},{25,9},{2,18},{10... | collective-permute-start | bytes 393224 | tf_op jit(solution)/shard_map/ppermute | solution.py:331
  28.8 17.8 %collective-permute-start.5 = (bf16[4,128,128]{2,1,0:T(8,128)(2,1)S(1)}, bf16[4,128,128]{2,1,0:T(8,128)(2,1)S(1)}, u32[]{:S(2)}, u32[]{:S(2)}) collective-permute-start(bf16[4,128,128]{2,1,0:T(8,128)(2,1)S(1)} %get-tuple-element.41), channel_id=1, source_target_pairs={{0,24},{8,16},{16,8},{24,0},{1,25},{9,17},{17,9},{25,1},{2,26},{10... | collective-permute-start | bytes 393224 | tf_op jit(solution)/shard_map/ppermute | solution.py:331
  29.3 18.8 %collective-permute-start.6 = (bf16[4,128,128]{2,1,0:T(8,128)(2,1)S(1)}, bf16[4,128,128]{2,1,0:T(8,128)(2,1)S(1)}, u32[]{:S(2)}, u32[]{:S(2)}) collective-permute-start(bf16[4,128,128]{2,1,0:T(8,128)(2,1)S(1)} %get-tuple-element.49), channel_id=1, source_target_pairs={{0,8},{8,0},{16,24},{24,16},{1,9},{9,1},{17,25},{25,17},{2,10},{10... | collective-permute-start | bytes 393224 | tf_op jit(solution)/shard_map/ppermute | solution.py:331
  30.7 17.8 %collective-permute-start.7 = (bf16[4,128,128]{2,1,0:T(8,128)(2,1)S(1)}, bf16[4,128,128]{2,1,0:T(8,128)(2,1)S(1)}, u32[]{:S(2)}, u32[]{:S(2)}) collective-permute-start(bf16[4,128,128]{2,1,0:T(8,128)(2,1)S(1)} %get-tuple-element.48), channel_id=1, source_target_pairs={{0,16},{8,24},{16,0},{24,8},{1,17},{9,25},{17,1},{25,9},{2,18},{10... | collective-permute-start | bytes 393224 | tf_op jit(solution)/shard_map/ppermute | solution.py:331
  48.0 12.6 %collective-permute-start.9 = (bf16[4,128,128]{2,1,0:T(8,128)(2,1)S(1)}, bf16[4,128,128]{2,1,0:T(8,128)(2,1)S(1)}, u32[]{:S(2)}, u32[]{:S(2)}) collective-permute-start(bf16[4,128,128]{2,1,0:T(8,128)(2,1)S(1)} %get-tuple-element.46), channel_id=1, source_target_pairs={{0,8},{8,0},{16,24},{24,16},{1,9},{9,1},{17,25},{25,17},{2,10},{10... | collective-permute-start | bytes 393224 | tf_op jit(solution)/shard_map/ppermute | solution.py:331
  57.4 13.2 %collective-permute-start.19 = (bf16[128,512]{1,0:T(8,128)(2,1)}, bf16[128,512]{1,0:T(8,128)(2,1)S(1)}, u32[]{:S(2)}, u32[]{:S(2)}) collective-permute-start(bf16[128,512]{1,0:T(8,128)(2,1)} %get-tuple-element.25.refs_0_), channel_id=1, source_target_pairs={{0,2},{1,3},{2,0},{3,1},{4,6},{5,7},{6,4},{7,5},{8,10},{9,11},{10,... | collective-permute-start | bytes 393224 | tf_op jit(solution)/shard_map/ppermute | solution.py:331
  61.2 19.0 %collective-permute-start.35 = (bf16[128,512]{1,0:T(8,128)(2,1)}, bf16[128,512]{1,0:T(8,128)(2,1)S(1)}, u32[]{:S(2)}, u32[]{:S(2)}) collective-permute-start(bf16[128,512]{1,0:T(8,128)(2,1)} %get-tuple-element.25.refs_0_), channel_id=1, source_target_pairs={{0,6},{1,7},{2,4},{3,5},{4,2},{5,3},{6,0},{7,1},{8,14},{9,15},{10,... | collective-permute-start | bytes 393224 | tf_op jit(solution)/shard_map/ppermute | solution.py:331
  67.6 21.9 %collective-permute-start.15 = (bf16[128,512]{1,0:T(8,128)(2,1)}, bf16[128,512]{1,0:T(8,128)(2,1)S(1)}, u32[]{:S(2)}, u32[]{:S(2)}) collective-permute-start(bf16[128,512]{1,0:T(8,128)(2,1)} %get-tuple-element.25.refs_0_), channel_id=1, source_target_pairs={{0,1},{1,0},{2,3},{3,2},{4,5},{5,4},{6,7},{7,6},{8,9},{9,8},{10,11... | collective-permute-start | bytes 393224 | tf_op jit(solution)/shard_map/ppermute | solution.py:331
  67.7 21.9 %collective-permute-start.20 = (bf16[128,512]{1,0:T(8,128)(2,1)}, bf16[128,512]{1,0:T(8,128)(2,1)S(1)}, u32[]{:S(2)}, u32[]{:S(2)}) collective-permute-start(bf16[128,512]{1,0:T(8,128)(2,1)} %get-tuple-element.26.refs_1_), channel_id=1, source_target_pairs={{0,2},{1,3},{2,0},{3,1},{4,6},{5,7},{6,4},{7,5},{8,10},{9,11},{10,... | collective-permute-start | bytes 393224 | tf_op jit(solution)/shard_map/ppermute | solution.py:331
  70.6 19.1 %collective-permute-start.28 = (bf16[128,512]{1,0:T(8,128)(2,1)}, bf16[128,512]{1,0:T(8,128)(2,1)S(1)}, u32[]{:S(2)}, u32[]{:S(2)}) collective-permute-start(bf16[128,512]{1,0:T(8,128)(2,1)} %get-tuple-element.26.refs_1_), channel_id=1, source_target_pairs={{0,4},{1,5},{2,6},{3,7},{4,0},{5,1},{6,2},{7,3},{8,12},{9,13},{10,... | collective-permute-start | bytes 393224 | tf_op jit(solution)/shard_map/ppermute | solution.py:331
  71.0 22.1 %collective-permute-start.36 = (bf16[128,512]{1,0:T(8,128)(2,1)}, bf16[128,512]{1,0:T(8,128)(2,1)S(1)}, u32[]{:S(2)}, u32[]{:S(2)}) collective-permute-start(bf16[128,512]{1,0:T(8,128)(2,1)} %get-tuple-element.26.refs_1_), channel_id=1, source_target_pairs={{0,6},{1,7},{2,4},{3,5},{4,2},{5,3},{6,0},{7,1},{8,14},{9,15},{10,... | collective-permute-start | bytes 393224 | tf_op jit(solution)/shard_map/ppermute | solution.py:331
  80.2 12.9 %collective-permute-start.16 = (bf16[128,512]{1,0:T(8,128)(2,1)}, bf16[128,512]{1,0:T(8,128)(2,1)S(1)}, u32[]{:S(2)}, u32[]{:S(2)}) collective-permute-start(bf16[128,512]{1,0:T(8,128)(2,1)} %get-tuple-element.26.refs_1_), channel_id=1, source_target_pairs={{0,1},{1,0},{2,3},{3,2},{4,5},{5,4},{6,7},{7,6},{8,9},{9,8},{10,11... | collective-permute-start | bytes 393224 | tf_op jit(solution)/shard_map/ppermute | solution.py:331
  89.7 21.1 %collective-permute-start.37 = (bf16[128,512]{1,0:T(8,128)(2,1)}, bf16[128,512]{1,0:T(8,128)(2,1)S(1)}, u32[]{:S(2)}, u32[]{:S(2)}) collective-permute-start(bf16[128,512]{1,0:T(8,128)(2,1)} %get-tuple-element.27.refs_2_), channel_id=1, source_target_pairs={{0,6},{1,7},{2,4},{3,5},{4,2},{5,3},{6,0},{7,1},{8,14},{9,15},{10,... | collective-permute-start | bytes 393224 | tf_op jit(solution)/shard_map/ppermute | solution.py:331
  93.1 17.8 %collective-permute-start.17 = (bf16[128,512]{1,0:T(8,128)(2,1)}, bf16[128,512]{1,0:T(8,128)(2,1)S(1)}, u32[]{:S(2)}, u32[]{:S(2)}) collective-permute-start(bf16[128,512]{1,0:T(8,128)(2,1)} %get-tuple-element.27.refs_2_), channel_id=1, source_target_pairs={{0,1},{1,0},{2,3},{3,2},{4,5},{5,4},{6,7},{7,6},{8,9},{9,8},{10,11... | collective-permute-start | bytes 393224 | tf_op jit(solution)/shard_map/ppermute | solution.py:331
  93.1 18.2 %collective-permute-start.22 = (bf16[128,512]{1,0:T(8,128)(2,1)}, bf16[128,512]{1,0:T(8,128)(2,1)S(1)}, u32[]{:S(2)}, u32[]{:S(2)}) collective-permute-start(bf16[128,512]{1,0:T(8,128)(2,1)} %get-tuple-element.28.refs_3_), channel_id=1, source_target_pairs={{0,2},{1,3},{2,0},{3,1},{4,6},{5,7},{6,4},{7,5},{8,10},{9,11},{10,... | collective-permute-start | bytes 393224 | tf_op jit(solution)/shard_map/ppermute | solution.py:331
  96.1 16.2 %collective-permute-start.30 = (bf16[128,512]{1,0:T(8,128)(2,1)}, bf16[128,512]{1,0:T(8,128)(2,1)S(1)}, u32[]{:S(2)}, u32[]{:S(2)}) collective-permute-start(bf16[128,512]{1,0:T(8,128)(2,1)} %get-tuple-element.28.refs_3_), channel_id=1, source_target_pairs={{0,4},{1,5},{2,6},{3,7},{4,0},{5,1},{6,2},{7,3},{8,12},{9,13},{10,... | collective-permute-start | bytes 393224 | tf_op jit(solution)/shard_map/ppermute | solution.py:331
  97.2 19.2 %collective-permute-start.38 = (bf16[128,512]{1,0:T(8,128)(2,1)}, bf16[128,512]{1,0:T(8,128)(2,1)S(1)}, u32[]{:S(2)}, u32[]{:S(2)}) collective-permute-start(bf16[128,512]{1,0:T(8,128)(2,1)} %get-tuple-element.28.refs_3_), channel_id=1, source_target_pairs={{0,6},{1,7},{2,4},{3,5},{4,2},{5,3},{6,0},{7,1},{8,14},{9,15},{10,... | collective-permute-start | bytes 393224 | tf_op jit(solution)/shard_map/ppermute | solution.py:331
  151.5 20.3 %collective-permute-start.43 = (bf16[4,128,512]{2,1,0:T(8,128)(2,1)}, bf16[4,128,512]{2,1,0:T(8,128)(2,1)S(1)}, u32[]{:S(2)}, u32[]{:S(2)}) collective-permute-start(bf16[4,128,512]{2,1,0:T(8,128)(2,1)} %get-tuple-element.30), channel_id=1, source_target_pairs={{0,1},{1,0},{2,3},{3,2},{4,5},{5,4},{6,7},{7,6},{8,9},{9,8},{10,11... | collective-permute-start | bytes 1572872 | tf_op jit(solution)/shard_map/ppermute | solution.py:331
  158.0 15.2 %collective-permute-start.47 = (bf16[4,128,512]{2,1,0:T(8,128)(2,1)}, bf16[4,128,512]{2,1,0:T(8,128)(2,1)S(1)}, u32[]{:S(2)}, u32[]{:S(2)}) collective-permute-start(bf16[4,128,512]{2,1,0:T(8,128)(2,1)} %get-tuple-element.32), channel_id=1, source_target_pairs={{0,1},{1,0},{2,3},{3,2},{4,5},{5,4},{6,7},{7,6},{8,9},{9,8},{10,11... | collective-permute-start | bytes 1572872 | tf_op jit(solution)/shard_map/ppermute | solution.py:331
  173.2 20.4 %collective-permute-start.46 = (bf16[128,512]{1,0:T(8,128)(2,1)S(1)}, bf16[128,512]{1,0:T(8,128)(2,1)S(1)}, u32[]{:S(2)}, u32[]{:S(2)}) collective-permute-start(bf16[128,512]{1,0:T(8,128)(2,1)S(1)} %get-tuple-element.54), channel_id=1, source_target_pairs={{0,6},{1,7},{2,4},{3,5},{4,2},{5,3},{6,0},{7,1},{8,14},{9,15},{10,... | collective-permute-start | bytes 393224 | tf_op jit(solution)/shard_map/ppermute | solution.py:331
  175.7 18.0 %collective-permute-start.48 = (bf16[128,512]{1,0:T(8,128)(2,1)S(1)}, bf16[128,512]{1,0:T(8,128)(2,1)S(1)}, u32[]{:S(2)}, u32[]{:S(2)}) collective-permute-start(bf16[128,512]{1,0:T(8,128)(2,1)S(1)} %get-tuple-element.56), channel_id=1, source_target_pairs={{0,2},{1,3},{2,0},{3,1},{4,6},{5,7},{6,4},{7,5},{8,10},{9,11},{10,... | collective-permute-start | bytes 393224 | tf_op jit(solution)/shard_map/ppermute | solution.py:331
  176.8 17.0 %collective-permute-start.49 = (bf16[128,512]{1,0:T(8,128)(2,1)S(1)}, bf16[128,512]{1,0:T(8,128)(2,1)S(1)}, u32[]{:S(2)}, u32[]{:S(2)}) collective-permute-start(bf16[128,512]{1,0:T(8,128)(2,1)S(1)} %get-tuple-element.58), channel_id=1, source_target_pairs={{0,4},{1,5},{2,6},{3,7},{4,0},{5,1},{6,2},{7,3},{8,12},{9,13},{10,... | collective-permute-start | bytes 393224 | tf_op jit(solution)/shard_map/ppermute | solution.py:331
  178.6 26.3 %collective-permute-start.50 = (bf16[128,512]{1,0:T(8,128)(2,1)S(1)}, bf16[128,512]{1,0:T(8,128)(2,1)S(1)}, u32[]{:S(2)}, u32[]{:S(2)}) collective-permute-start(bf16[128,512]{1,0:T(8,128)(2,1)S(1)} %get-tuple-element.57), channel_id=1, source_target_pairs={{0,6},{1,7},{2,4},{3,5},{4,2},{5,3},{6,0},{7,1},{8,14},{9,15},{10,... | collective-permute-start | bytes 393224 | tf_op jit(solution)/shard_map/ppermute | solution.py:331
  180.6 24.3 %collective-permute-start.52 = (bf16[128,512]{1,0:T(8,128)(2,1)S(1)}, bf16[128,512]{1,0:T(8,128)(2,1)S(1)}, u32[]{:S(2)}, u32[]{:S(2)}) collective-permute-start(bf16[128,512]{1,0:T(8,128)(2,1)S(1)} %get-tuple-element.59), channel_id=1, source_target_pairs={{0,2},{1,3},{2,0},{3,1},{4,6},{5,7},{6,4},{7,5},{8,10},{9,11},{10,... | collective-permute-start | bytes 393224 | tf_op jit(solution)/shard_map/ppermute | solution.py:331
  193.6 12.7 %collective-permute-start.53 = (bf16[128,512]{1,0:T(8,128)(2,1)S(1)}, bf16[128,512]{1,0:T(8,128)(2,1)S(1)}, u32[]{:S(2)}, u32[]{:S(2)}) collective-permute-start(bf16[128,512]{1,0:T(8,128)(2,1)S(1)} %get-tuple-element.61), channel_id=1, source_target_pairs={{0,4},{1,5},{2,6},{3,7},{4,0},{5,1},{6,2},{7,3},{8,12},{9,13},{10,... | collective-permute-start | bytes 393224 | tf_op jit(solution)/shard_map/ppermute | solution.py:331
  193.7 22.4 %collective-permute-start.54 = (bf16[128,512]{1,0:T(8,128)(2,1)S(1)}, bf16[128,512]{1,0:T(8,128)(2,1)S(1)}, u32[]{:S(2)}, u32[]{:S(2)}) collective-permute-start(bf16[128,512]{1,0:T(8,128)(2,1)S(1)} %get-tuple-element.60), channel_id=1, source_target_pairs={{0,6},{1,7},{2,4},{3,5},{4,2},{5,3},{6,0},{7,1},{8,14},{9,15},{10,... | collective-permute-start | bytes 393224 | tf_op jit(solution)/shard_map/ppermute | solution.py:331
  193.8 22.4 %collective-permute-start.56 = (bf16[128,512]{1,0:T(8,128)(2,1)S(1)}, bf16[128,512]{1,0:T(8,128)(2,1)S(1)}, u32[]{:S(2)}, u32[]{:S(2)}) collective-permute-start(bf16[128,512]{1,0:T(8,128)(2,1)S(1)} %get-tuple-element.62), channel_id=1, source_target_pairs={{0,2},{1,3},{2,0},{3,1},{4,6},{5,7},{6,4},{7,5},{8,10},{9,11},{10,... | collective-permute-start | bytes 393224 | tf_op jit(solution)/shard_map/ppermute | solution.py:331
  204.9 16.3 %collective-permute-start.58 = (bf16[128,512]{1,0:T(8,128)(2,1)S(1)}, bf16[128,512]{1,0:T(8,128)(2,1)S(1)}, u32[]{:S(2)}, u32[]{:S(2)}) collective-permute-start(bf16[128,512]{1,0:T(8,128)(2,1)S(1)} %get-tuple-element.63), channel_id=1, source_target_pairs={{0,6},{1,7},{2,4},{3,5},{4,2},{5,3},{6,0},{7,1},{8,14},{9,15},{10,... | collective-permute-start | bytes 393224 | tf_op jit(solution)/shard_map/ppermute | solution.py:331
  (79 other events, 1043.5 us)

commit v2 on v1

v2 whole, which is shorter than its diff:
```python
import jax
import jax.numpy as jnp
from jax import lax
from jax.experimental import pallas as pl
from jax.experimental.pallas import tpu as pltpu
from jax.sharding import PartitionSpec as P

MOST = 56
PAIR = 2 * MOST
EPS = 1e-06
HEADS_A_STEP = 4
HEAD_CHUNKS = (8, 8)
STAGES = ((0, 1), (2,), (3,))
LANES = 128
FAR = -100000.0
BF = jnp.bfloat16
F32 = jnp.float32
VMEM_BYTES = 60 * 1024 * 1024


def iota(shape, dim):
    return lax.broadcasted_iota(jnp.int32, shape, dim)


def mm(a, b):
    return jnp.dot(a, b, preferred_element_type=F32)


def silu(x):
    return x / (1.0 + jnp.exp(-x))


def prepare_kernel(q_ref, k_ref, lb_ref, lbt_ref, kq_ref, t_ref, mk_ref):
    rows = q_ref.shape[0]
    dk = 128
    at_row = iota((rows, rows), 0)
    at_col = iota((rows, rows), 1)
    strict = at_row > at_col
    inclusive = at_row >= at_col
    lower = inclusive.astype(F32)
    upper = (at_row <= at_col).astype(F32)
    top = lax.Precision.HIGHEST
    total_row = jnp.dot(lb_ref[0], upper, precision=top, preferred_element_type=F32)
    total_col = jnp.dot(lower, lbt_ref[0], precision=top, preferred_element_type=F32)
    solved = []
    mixes = []
    for i in range(HEADS_A_STEP):
        span = slice(i * dk, (i + 1) * dk)
        q = q_ref[:, span].astype(F32)
        k = k_ref[:, span].astype(F32)
        q = q / jnp.sqrt(jnp.sum(q * q, axis=-1, keepdims=True) + EPS)
        k = k / jnp.sqrt(jnp.sum(k * k, axis=-1, keepdims=True) + EPS)
        l_col = total_col[:, i : i + 1]
        l_row = total_row[i : i + 1, :]
        beta = lbt_ref[0][:, HEADS_A_STEP + i : HEADS_A_STEP + i + 1]
        ratio = jnp.where(inclusive, jnp.exp(jnp.where(inclusive, l_col - l_row, 0.0)), 0.0)
        kb = k.astype(BF)
        both = lax.dot_general(
            jnp.concatenate([kb, q.astype(BF)], axis=0),
            kb,
            (((1,), (1,)), ((), ())),
            preferred_element_type=F32,
        )
        mix = jnp.where(strict, beta * ratio * both[:rows], 0.0)
        growth = jnp.exp(l_col)
        trail = jnp.exp(l_col[rows - 1 : rows, :] - l_col)
        kq_ref[i] = jnp.concatenate([k * (beta * growth), q * growth], axis=0).astype(BF)
        mk_ref[i] = jnp.concatenate(
            [ratio * both[rows:], jnp.transpose(k * trail)], axis=0
        ).astype(BF)
        mixes.append(mix)
        first = (at_row // 2 == at_col // 2) & strict
        solved.append((at_row == at_col).astype(F32) - jnp.where(first, mix, 0.0))
    size = 2
    while size < rows:
        here = (
            (at_row // (2 * size) == at_col // (2 * size))
            & ((at_row // size) % 2 == 1)
            & ((at_col // size) % 2 == 0)
        )
        for i in range(HEADS_A_STEP):
            t = solved[i].astype(BF)
            block = jnp.where(here, mixes[i], 0.0).astype(BF)
            solved[i] = solved[i] - mm(t, mm(block, t).astype(BF))
        size *= 2
    for i in range(HEADS_A_STEP):
        t_ref[i] = solved[i].astype(BF)


def prepare(queries, keys_in, lb, lbt):
    rows = queries.shape[0]
    groups = lb.shape[0]
    heads = groups * HEADS_A_STEP
    wide = HEADS_A_STEP * 128
    return pl.pallas_call(
        prepare_kernel,
        grid=(groups,),
        in_specs=[
            pl.BlockSpec((rows, wide), lambda i: (0, i)),
            pl.BlockSpec((rows, wide), lambda i: (0, i)),
            pl.BlockSpec((1,) + lb.shape[1:], lambda i: (i, 0, 0)),
            pl.BlockSpec((1,) + lbt.shape[1:], lambda i: (i, 0, 0)),
        ],
        out_specs=[
            pl.BlockSpec((HEADS_A_STEP, 2 * rows, 128), lambda i: (i, 0, 0)),
            pl.BlockSpec((HEADS_A_STEP, rows, rows), lambda i: (i, 0, 0)),
            pl.BlockSpec((HEADS_A_STEP, rows + 128, rows), lambda i: (i, 0, 0)),
        ],
        out_shape=[
            jax.ShapeDtypeStruct((heads, 2 * rows, 128), BF),
            jax.ShapeDtypeStruct((heads, rows, rows), BF),
            jax.ShapeDtypeStruct((heads, rows + 128, rows), BF),
        ],
        compiler_params=pltpu.CompilerParams(vmem_limit_bytes=VMEM_BYTES),
        cost_estimate=pl.CostEstimate(flops=int(2e9), transcendentals=0, bytes_accessed=4000000),
        name="prepare",
    )(queries, keys_in, lb, lbt)


def resume_kernel(pick_ref, *refs, peers, first_head, experts):
    cache_ref, got_refs, refs = refs[0], refs[1 : 1 + peers], refs[1 + peers :]
    kq_ref, t_ref, mk_ref, v_ref, lb_ref, lbt_ref, gate_ref, res_ref, gain_ref = refs[:9]
    ids_ref, weight_ref = refs[9:11]
    out_ref, next_ref, own_buf, got_buf, sem_own, sem_got = refs[11:]
    heads, rows, _ = t_ref.shape
    steps = own_buf.shape[0] // heads
    at = pl.program_id(0)
    place = pick_ref[0]
    slot = pick_ref[1]

    def own_copy(s):
        return pltpu.make_async_copy(
            cache_ref.at[0, slot, pl.ds(first_head + s * heads, heads)],
            own_buf.at[pl.ds(s * heads, heads)],
            sem_own.at[s],
        )

    def got_copy(s, j):
        return pltpu.make_async_copy(
            got_refs[j].at[pl.ds(s * heads, heads)],
            got_buf.at[pl.ds(s * heads, heads)],
            sem_got.at[s],
        )

    @pl.when(at == 0)
    def _():
        for s in range(steps):
            own_copy(s).start()
            for j in range(peers):

                @pl.when(place == j + 1)
                def _(s=s, j=j):
                    got_copy(s, j).start()

        if experts:
            lane = iota((rows, LANES), 1)
            named = jnp.zeros((rows, LANES), F32)
            for k in range(ids_ref.shape[1]):
                hit = lane % experts == ids_ref[:, k : k + 1]
                named = jnp.where(hit, weight_ref[:, k : k + 1], named)
            coarse = named.astype(BF)
            fine = named - coarse.astype(F32)
            both = jnp.where(lane < experts, coarse.astype(F32), fine)
            both = jnp.where(lane < 2 * experts, both, 0.0)
            out_ref[:, out_ref.shape[1] - LANES :] = both.astype(BF)

    own_copy(at).wait()

    @pl.when(place > 0)
    def _():
        got_copy(at, 0).wait()

    here = place == 0
    for i in range(heads):
        span = slice(i * 128, (i + 1) * 128)
        head = at * heads + i
        state = jnp.where(here, own_buf[head], got_buf[head].astype(F32))
        beta = lbt_ref[0][:, HEADS_A_STEP + i : HEADS_A_STEP + i + 1]
        read = mm(kq_ref[i], state.astype(BF))
        rest = beta * v_ref[:, span].astype(F32) - read[:rows]
        fixed = mm(t_ref[i], rest.astype(BF)).astype(BF)
        added = mm(mk_ref[i], fixed)
        o = read[rows:] + added[:rows]
        last = jnp.exp(jnp.sum(lb_ref[0][i : i + 1, :], axis=-1, keepdims=True))
        next_ref[i] = last * state + added[rows:]
        scaled = o / jnp.sqrt(jnp.mean(o * o, axis=-1, keepdims=True) + EPS) * gain_ref[...]
        gated = scaled * silu(gate_ref[:, span].astype(F32))
        mixed = (res_ref[:, span].astype(F32) + gated).astype(BF)
        out_ref[:, pl.ds(pl.multiple_of(head * 128, 128), 128)] = mixed


def resume(
    pick, cache, got, kq, t, mk, values, lb, lbt, gate, residual, gain, ids, weight, first, heads,
    experts,
):
    rows = values.shape[0]
    step = HEADS_A_STEP
    wide = heads * 128 + (LANES if experts else 0)
    base = first // step
    any_spec = pl.BlockSpec(memory_space=pl.ANY)
    cols = pl.BlockSpec((rows, step * 128), lambda i, p: (0, base + i))
    group = lambda i, p: (base + i, 0, 0)
    whole = lambda i, p: (0, 0)
    return pl.pallas_call(
        lambda *refs: resume_kernel(*refs, peers=len(got), first_head=first, experts=experts),
        grid_spec=pltpu.PrefetchScalarGridSpec(
            num_scalar_prefetch=1,
            grid=(heads // step,),
            in_specs=[any_spec]
            + [any_spec] * len(got)
            + [
                pl.BlockSpec((step,) + kq.shape[1:], group),
                pl.BlockSpec((step,) + t.shape[1:], group),
                pl.BlockSpec((step,) + mk.shape[1:], group),
                cols,
                pl.BlockSpec((1,) + lb.shape[1:], group),
                pl.BlockSpec((1,) + lbt.shape[1:], group),
                cols,
                cols,
                pl.BlockSpec((1, 128), whole),
                pl.BlockSpec(ids.shape, whole),
                pl.BlockSpec(weight.shape, whole),
            ],
            out_specs=[
                pl.BlockSpec((rows, wide), whole),
                pl.BlockSpec((step, 128, 128), lambda i, p: (i, 0, 0)),
            ],
            scratch_shapes=[
                pltpu.VMEM((heads, 128, 128), F32),
                pltpu.VMEM((heads, 128, 128), BF),
                pltpu.SemaphoreType.DMA((heads // step,)),
                pltpu.SemaphoreType.DMA((heads // step,)),
            ],
        ),
        out_shape=[
            jax.ShapeDtypeStruct((rows, wide), BF),
            jax.ShapeDtypeStruct((heads, 128, 128), F32),
        ],
        compiler_params=pltpu.CompilerParams(vmem_limit_bytes=VMEM_BYTES),
        cost_estimate=pl.CostEstimate(flops=int(1e9), transcendentals=0, bytes_accessed=6000000),
        name="resume",
    )(pick, cache, *got, kq, t, mk, values, lb, lbt, gate, residual, gain, ids, weight)


def expert_kernel(first_ref, *refs, blocks, parts, experts, all_experts, halves):
    x_refs, refs = refs[: blocks * parts], refs[blocks * parts :]
    gain_ref, wg_ref, wu_ref, wd_ref, own_ref, other_ref = refs[:6]
    xs_ref, posr_ref, posc_ref, wr_ref, chosen_ref, slot_ref, acc_ref, rows_ref = refs[6:]
    step = pl.program_id(0)
    e = step // halves
    f = step % halves
    rows = x_refs[0].shape[0]
    d = xs_ref.shape[1]
    pairs = blocks // 2
    two = 2 * rows

    @pl.when(step == 0)
    def _():
        gain = gain_ref[...]
        slab = 16
        a, b = iota((LANES, LANES), 0), iota((LANES, LANES), 1)
        first = first_ref[0]
        mine = ((a == first + b) | (a == first + b + all_experts)) & (b < experts)
        mine = mine.astype(F32).astype(BF)
        before = (iota((rows, rows), 0) > iota((rows, rows), 1)).astype(F32).astype(BF)
        for n in range(blocks):
            last = x_refs[n * parts + parts - 1]
            weight = mm(last[:, last.shape[1] - LANES :], mine)
            routed = weight > 0.0
            rank = mm(before, routed.astype(F32).astype(BF)) + float(n % 2 * MOST)
            rank = jnp.where(routed, rank, FAR)
            posc_ref[n] = rank
            posr_ref[n] = jnp.transpose(rank)
            wr_ref[n] = jnp.transpose(weight)

            def norm(s, carry, n=n):
                at = pl.multiple_of(s * slab, slab)
                pieces = [x_refs[n * parts + c][pl.ds(at, slab), :] for c in range(parts)]
                pieces[-1] = pieces[-1][:, : pieces[-1].shape[1] - LANES]
                x = jnp.concatenate(pieces, axis=1).astype(F32)
                mean = jnp.mean(x * x, axis=-1, keepdims=True)
                to = pl.multiple_of(n * rows + s * slab, slab)
                xs_ref[pl.ds(to, slab), :] = (x / jnp.sqrt(mean + EPS) * gain).astype(BF)
                return carry

            lax.fori_loop(0, rows // slab, norm, 0, unroll=2)

    @pl.when(f == 0)
    def _():
        for p in range(pairs):
            pos = [posr_ref[2 * p + c, pl.ds(e, 1), :] for c in range(2)]
            weight = [wr_ref[2 * p + c, pl.ds(e, 1), :] for c in range(2)]
            sel = iota((PAIR, two), 0).astype(F32) == jnp.concatenate(pos, axis=1)
            span = slice(p * PAIR, (p + 1) * PAIR)
            slot_ref[span, :] = jnp.broadcast_to(
                jnp.sum(
                    jnp.where(sel, jnp.concatenate(weight, axis=1), 0.0), axis=1, keepdims=True
                ),
                (PAIR, LANES),
            )
            chosen_ref[span, :] = mm(
                sel.astype(F32).astype(BF), xs_ref[p * two : (p + 1) * two, :]
            ).astype(BF)

    x = chosen_ref[...]
    hidden = silu(mm(x, wg_ref[0])) * mm(x, wu_ref[0]) * slot_ref[:, 0:1]
    part = mm(hidden.astype(BF), wd_ref[0])

    @pl.when(f == 0)
    def _():
        acc_ref[...] = part

    @pl.when(f == halves - 1)
    def _():
        done = (part if halves == 1 else acc_ref[...] + part).astype(BF)
        to = pl.multiple_of(e * PAIR, 16)
        for p in range(pairs):
            rows_ref[p, pl.ds(to, PAIR), :] = done[p * PAIR : (p + 1) * PAIR]

    @pl.when(step == pl.num_programs(0) - 1)
    def _():
        lane = iota((two, experts * PAIR), 1).astype(F32)
        for p in range(pairs):
            at = jnp.concatenate([posc_ref[2 * p], posc_ref[2 * p + 1]], axis=0)
            hit = lane == at[:, 0:1]
            for n in range(1, experts):
                hit = hit | (lane == at[:, n : n + 1] + float(n * PAIR))
            both = mm(hit.astype(F32).astype(BF), rows_ref[p]).astype(BF)
            own_ref[p] = both[:rows]
            other_ref[p] = both[rows:]


def expert_stage(first, xs, parts, gain, w_gate, w_up, w_down, all_experts):
    experts, d, ff = w_gate.shape
    rows = xs[0].shape[0]
    blocks = len(xs) // parts
    pairs = blocks // 2
    halves = 2
    part = ff // halves
    one = pl.Buffered(1)
    out = jax.ShapeDtypeStruct((pairs, rows, d), BF)
    whole3 = lambda s, m: (0, 0, 0)
    return pl.pallas_call(
        lambda *refs: expert_kernel(
            *refs, blocks=blocks, parts=parts, experts=experts, all_experts=all_experts,
            halves=halves,
        ),
        grid_spec=pltpu.PrefetchScalarGridSpec(
            num_scalar_prefetch=1,
            grid=(experts * halves,),
            in_specs=[pl.BlockSpec(x.shape, lambda s, m: (0, 0), pipeline_mode=one) for x in xs]
            + [
                pl.BlockSpec((1, d), lambda s, m: (0, 0)),
                pl.BlockSpec((1, d, part), lambda s, m: (s // halves, 0, s % halves)),
                pl.BlockSpec((1, d, part), lambda s, m: (s // halves, 0, s % halves)),
                pl.BlockSpec((1, part, d), lambda s, m: (s // halves, s % halves, 0)),
            ],
            out_specs=[pl.BlockSpec(out.shape, whole3), pl.BlockSpec(out.shape, whole3)],
            scratch_shapes=[
                pltpu.VMEM((blocks * rows, d), BF),
                pltpu.VMEM((blocks, LANES, rows), F32),
                pltpu.VMEM((blocks, rows, LANES), F32),
                pltpu.VMEM((blocks, LANES, rows), F32),
                pltpu.VMEM((pairs * PAIR, d), BF),
                pltpu.VMEM((pairs * PAIR, LANES), F32),
                pltpu.VMEM((pairs * PAIR, d), F32),
                pltpu.VMEM((pairs, experts * PAIR, d), BF),
            ],
        ),
        out_shape=[out, out],
        compiler_params=pltpu.CompilerParams(vmem_limit_bytes=VMEM_BYTES),
        cost_estimate=pl.CostEstimate(
            flops=int(4e9) * pairs, transcendentals=0, bytes_accessed=30000000
        ),
        name="experts",
    )(first, *xs, gain, w_gate, w_up, w_down)


def swap(x, axis, bits):
    size = lax.axis_size(axis)
    return lax.ppermute(x, axis, [(i, i ^ bits) for i in range(size)])


def local(
    residual_in,
    queries,
    keys_in,
    values_in,
    out_gate,
    log_decay,
    beta_rate,
    head_gain,
    moe_gain,
    state_cache,
    hit_holder,
    hit_slot,
    expert_ids,
    gate_weight,
    w_gate,
    w_up,
    w_down,
):
    rows, d = queries.shape
    head_count = log_decay.shape[0]
    holders = lax.axis_size("dp")
    group = lax.axis_size("expert")
    own_dp = lax.axis_index("dp")
    own_ep = lax.axis_index("expert")
    experts = w_gate.shape[0]
    pairs = group // 2
    all_experts = group * experts
    chunks = HEAD_CHUNKS
    starts = [sum(chunks[:g]) for g in range(len(chunks))]

    wish = jnp.concatenate([hit_holder, hit_slot])
    sends = []
    for j in range(1, holders):
        asked = swap(wish, "dp", j)
        sends.append(jnp.where(asked[0] == own_dp, asked[1], 0))
    got = []
    for first, heads in zip(starts, chunks):
        got.append([])
        for j in range(1, holders):
            piece = lax.dynamic_slice(
                state_cache, (0, sends[j - 1], first, 0, 0), (1, 1, heads) + state_cache.shape[3:]
            )[0, 0].astype(BF)
            got[-1].append(swap(piece, "dp", j))
    pick = jnp.stack([hit_holder[0] ^ own_dp, hit_slot[0]])

    groups = head_count // HEADS_A_STEP
    lb = jnp.concatenate(
        [
            log_decay.reshape(groups, HEADS_A_STEP, rows),
            beta_rate.reshape(groups, HEADS_A_STEP, rows),
        ],
        axis=1,
    )
    lbt = lb.transpose(0, 2, 1)
    kq, t, mk = prepare(queries, keys_in, lb, lbt)
    mixed, states = [], []
    for g, (first, heads) in enumerate(zip(starts, chunks)):
        last = g == len(chunks) - 1
        m, s = resume(
            pick, state_cache, got[g], kq, t, mk, values_in, lb, lbt, out_gate, residual_in,
            head_gain[None], expert_ids, gate_weight, first, heads, all_experts if last else 0,
        )
        mixed.append(m)
        states.append(s)
    parts = len(chunks)
    mixer_out = jnp.concatenate(mixed[:-1] + [mixed[-1][:, :-LANES]], axis=1)

    gain = moe_gain[None]
    first_expert = (own_ep * experts)[None].astype(jnp.int32)
    weights = (w_gate, w_up, w_down)
    if group == 8:
        blocks = [[] for _ in range(group)]
        for c in range(parts):
            for r in (0, 2, 3, 1):
                near = mixed[c] if r == 0 else swap(mixed[c], "expert", 2 * r)
                blocks[2 * r].append(near)
                blocks[2 * r + 1].append(swap(near, "expert", 1))
        total = None
        for stage in STAGES:
            xs = [x for r in stage for x in blocks[2 * r] + blocks[2 * r + 1]]
            own, other = expert_stage(first_expert, xs, parts, gain, *weights, all_experts)
            came = swap(other, "expert", 1)
            for i, r in enumerate(stage):
                chip = own[i].astype(F32) + came[i].astype(F32)
                if r:
                    chip = swap(chip.astype(BF), "expert", 2 * r).astype(F32)
                total = chip if total is None else total + chip
        expert_out = total.astype(BF)
    else:
        order = jnp.arange(group, dtype=jnp.int32) ^ own_ep
        x = lax.all_gather(jnp.concatenate(mixed, axis=1), "expert", axis=0)[order]
        sums = []
        for p in range(0, group, 8):
            xs = [x[p + i] for i in range(8)]
            own, other = expert_stage(first_expert, xs, 1, gain, *weights, all_experts)
            sums.append(jnp.stack([own, other], axis=1).reshape(8, rows, d))
        part = jnp.concatenate(sums, axis=0)[order]
        expert_out = lax.psum_scatter(part, "expert", scatter_dimension=0)
    return (mixer_out, expert_out, jnp.concatenate(states, axis=0)[None])


def solution(mesh):
    both = ("dp", "expert")
    rows = P(both, None)
    placed = (
        rows,
        rows,
        rows,
        rows,
        rows,
        P(None, both),
        P(None, both),
        P(),
        P(),
        P(both, None, None, None, None),
        P(both),
        P(both),
        rows,
        rows,
        P("expert", None, None),
        P("expert", None, None),
        P("expert", None, None),
    )
    return jax.shard_map(
        local,
        mesh=mesh,
        in_specs=placed,
        out_specs=(rows, rows, P(both, None, None, None)),
        check_vma=False,
    )
```

time: 224 us -> 194 us (0.87)
  starting transfers between devices: 62.2 us -> 30.1 us
  blocking collectives: 12.2 us -> 0 us
  waiting for transfers between devices: 48.8 us -> 55.8 us
  local copies, waits for them, and re-layouts: 6.12 us -> 12.7 us
  Pallas kernels: 76.5 us -> 79.5 us
    ppermute x59 -> x29, starting transfers between devices: 62.2 us -> 30.1 us  [swap(): return lax.ppermute(x, axis, [(i, i ^ bits) for i in range(size)])]
    all_gather x1 -> x0, blocking collectives: 12.2 us -> none  [local(): lax.all_gather(dense, 'expert', axis=0).reshape(group, group, experts, rows)]
    pallas_call x5 -> x3, Pallas kernels: 47.4 us -> 57.2 us  [expert_stage(): pl.pallas_call(lambda *refs: expert_kernel(*refs, blocks=blocks, parts=pa...]
    ppermute x59 -> x29, waiting for transfers between devices: 48.8 us -> 55.8 us  [swap(): return lax.ppermute(x, axis, [(i, i ^ bits) for i in range(size)])]
    pallas_call x4 -> x2, Pallas kernels: 18.3 us -> 11.6 us  [resume(): pl.pallas_call(lambda *refs: resume_kernel(*refs, peers=len(got), first_h...]
    unnamed x104 -> x44, local copies, waits for them, and re-layouts: 0.97 us -> 6.78 us
  transfers between devices with their start and end apart: 59 -> 29, of which waited for: 12 -> 10; matrix products, arithmetic and copies ran while one was open for 6% -> 6% of each run, Pallas kernels for 21% -> 41%
where the time goes in v2:
time: 194 us; the launch traced here: 192 us
  Pallas kernels  79.5 us (41%)
  waiting for transfers between devices  55.8 us (29%)
  starting transfers between devices  30.1 us (16%)
  local copies, waits for them, and re-layouts  12.7 us (7%)
  other arithmetic  7.92 us (4%)
  between operations  6.1 us (3%)
    pallas_call x3, Pallas kernels, expert_stage(): pl.pallas_call(lambda *refs: expert_kernel(*refs, blocks=blocks, parts=pa...  57.2 us
    ppermute x29, waiting for transfers between devices, swap(): return lax.ppermute(x, axis, [(i, i ^ bits) for i in range(size)])  55.8 us
    ppermute x29, starting transfers between devices, swap(): return lax.ppermute(x, axis, [(i, i ^ bits) for i in range(size)])  30.1 us
    pallas_call x2, Pallas kernels, resume(): pl.pallas_call(lambda *refs: resume_kernel(*refs, peers=len(got), first_h...  11.6 us
    pallas_call x1, Pallas kernels, prepare(): pl.pallas_call(prepare_kernel, grid=(groups,), in_specs=[pl.BlockSpec((ro...  10.8 us
    unnamed x44, local copies, waits for them, and re-layouts  6.78 us
  transfers between devices with their start and end apart: 29, of which 10 were waited for; matrix products, arithmetic and copies ran while one was open for 6% of the time, Pallas kernels for 41%

profile of v2, /device:TPU:16, one launch (start us, length us, event | category | flops | bytes accessed | tf_op | source)
XLA Modules:
  0.0 192.2 jit_solution(14955451600655872677)
XLA Ops:
  2.0 1.5 collective-permute-start
  3.5 1.5 collective-permute-start.2
  11.4 2.3 %fusion.8 = (bf16[8,128,128]{2,1,0:T(8,128)(2,1)S(1)}, bf16[8,128,128]{2,1,0:T(8,128)(2,1)S(1)}, bf16[8,128,128]{2,1,0:T(8,128)(2,1)S(1)}, bf16[8,128,128]{2,1,0...) fusion(f32[1,2,16,128,128]{4,3,2,1,0:T(8,128)} %refs_1_.3, s32[]{:T(128)S(6)} %select_n.27, ...), kind=kLoop, calls=%fused_computation.20 | loop fusion | bytes 3145740 | tf_op jit(solution)/shard_map/convert_element_type | solution.py:426
  13.7 1.4 collective-permute-start.6
  16.7 1.4 copy.37.refs_14_
  18.1 1.4 copy.38.refs_15_
  19.6 1.5 collective-permute-start.7
  22.3 1.4 collective-permute-start.1
  23.6 1.5 collective-permute-start.3
  25.8 10.8 %prepare.1 = (bf16[16,256,128]{2,1,0:T(8,128)(2,1)}, bf16[16,128,128]{2,1,0:T(8,128)(2,1)}, bf16[16,256,128]{2,1,0:T(8,128)(2,1)}) custom-call(bf16[128,2048]{1,0:T(8,128)(2,1)} %q_ref.1, bf16[128,2048]{1,0:T(8,128)(2,1)} %k_ref.1, f32[4,8,128]{2,1,0:T(8,128)} %copy-done.8, f32[4,128,8]{2,1,0:T(8,128)} %bitcast.43), custom_call_target="tpu_custom_call" | custom-call | flops 2000000000 | bytes 4000000 | tf_op jit(solution)/shard_map/prepare/pallas_call | solution.py:95
  36.5 3.4 %collective-permute-done.7.refs_3_ = bf16[8,128,128]{2,1,0:T(8,128)(2,1)S(1)} collective-permute-done((bf16[8,128,128]{2,1,0:T(8,128)(2,1)S(1)}, bf16[8,128,128]{2,1,0:T(8,128)(2,1)S(1)}, u32[]{:S(2)}, u32[]{:S(2)}) %collective-permute-start.7) | collective-permute-done | bytes 262176 | tf_op jit(solution)/shard_map/ppermute | solution.py:381
  40.8 5.8 %resume.3 = (bf16[128,1152]{1,0:T(8,128)(2,1)}, f32[8,128,128]{2,1,0:T(8,128)}) custom-call(s32[2]{0:T(128)} %pad_add_fusion.refs_0_, f32[1,2,16,128,128]{4,3,2,1,0:T(8,128)} %refs_1_.3, bf16[8,128,128]{2,1,0:T(8,128)(2,1)} %copy-done.11, bf16[8,128,128]{2,1,0:T(8,128)(2,1)} %copy-done.13, bf16[8,128,128]{2,1,0:T(8,128)(2,1)} %copy-done.14, ...), custom_call_target="tpu_custom_call" | custom-call | flops 1000000000 | bytes 6000000 | tf_op jit(solution)/shard_map/resume/pallas_call | solution.py:204
  48.5 5.8 %resume.2 = (bf16[128,1024]{1,0:T(8,128)(2,1)}, f32[8,128,128]{2,1,0:T(8,128)}) custom-call(s32[2]{0:T(128)} %pad_add_fusion.refs_0_, f32[1,2,16,128,128]{4,3,2,1,0:T(8,128)} %refs_1_.3, bf16[8,128,128]{2,1,0:T(8,128)(2,1)} %copy-done.9, bf16[8,128,128]{2,1,0:T(8,128)(2,1)} %copy-done.10, bf16[8,128,128]{2,1,0:T(8,128)(2,1)} %copy-done.12, ...), custom_call_target="tpu_custom_call" | custom-call | flops 1000000000 | bytes 6000000 | tf_op jit(solution)/shard_map/resume/pallas_call | solution.py:204
  54.2 2.7 %collective-permute-start.17 = (bf16[128,1024]{1,0:T(8,128)(2,1)}, bf16[128,1024]{1,0:T(8,128)(2,1)S(1)}, u32[]{:S(2)}, u32[]{:S(2)}) collective-permute-start(bf16[128,1024]{1,0:T(8,128)(2,1)} %get-tuple-element.19.refs_1_), channel_id=1, source_target_pairs={{0,4},{1,5},{2,6},{3,7},{4,0},{5,1},{6,2},{7,3},{8,12},{9,13},{10,... | collective-permute-start | bytes 786440 | tf_op jit(solution)/shard_map/ppermute | solution.py:381
  56.9 1.5 collective-permute-start.12
  58.4 1.0 collective-permute-done.18.refs_2_
  59.5 8.1 %collective-permute-start.11 = (bf16[128,1024]{1,0:T(8,128)(2,1)}, bf16[128,1024]{1,0:T(8,128)(2,1)S(1)}, u32[]{:S(2)}, u32[]{:S(2)}) collective-permute-start(bf16[128,1024]{1,0:T(8,128)(2,1)} %get-tuple-element.19.refs_1_), channel_id=1, source_target_pairs={{0,2},{1,3},{2,0},{3,1},{4,6},{5,7},{6,4},{7,5},{8,10},{9,11},{10,... | collective-permute-start | bytes 786440 | tf_op jit(solution)/shard_map/ppermute | solution.py:381
  68.2 6.7 %collective-permute-done.11.refs_5_ = bf16[128,1024]{1,0:T(8,128)(2,1)S(1)} collective-permute-done((bf16[128,1024]{1,0:T(8,128)(2,1)}, bf16[128,1024]{1,0:T(8,128)(2,1)S(1)}, u32[]{:S(2)}, u32[]{:S(2)}) %collective-permute-start.11) | collective-permute-done | bytes 262176 | tf_op jit(solution)/shard_map/ppermute | solution.py:381
  74.9 2.0 %collective-permute-start.24 = (bf16[128,1152]{1,0:T(8,128)(2,1)}, bf16[128,1152]{1,0:T(8,128)(2,1)S(1)}, u32[]{:S(2)}, u32[]{:S(2)}) collective-permute-start(bf16[128,1152]{1,0:T(8,128)(2,1)} %get-tuple-element.20.refs_2_), channel_id=1, source_target_pairs={{0,6},{1,7},{2,4},{3,5},{4,2},{5,3},{6,0},{7,1},{8,14},{9,15},{10,... | collective-permute-start | bytes 884744 | tf_op jit(solution)/shard_map/ppermute | solution.py:381
  77.7 17.2 %experts.4 = (bf16[1,128,2048]{2,1,0:T(8,128)(2,1)}, bf16[1,128,2048]{2,1,0:T(8,128)(2,1)}) custom-call(s32[1]{0:T(128)} %bitcast.18.refs_0_, bf16[128,1024]{1,0:T(8,128)(2,1)} %copy-done.6, bf16[128,1152]{1,0:T(8,128)(2,1)} %copy-done.3, bf16[128,1024]{1,0:T(8,128)(2,1)} %copy-done.7, bf16[128,1152]{1,0:T(8,128)(2,1)} %copy-done.5, f32[1,2048]{1,0:T(1,128)} %bitcast.46, ...), custom_call_target="tpu_custom_call" | custom-call | flops 4000000000 | bytes 30000000 | tf_op jit(solution)/shard_map/experts/pallas_call | solution.py:343
  94.9 1.3 collective-permute-done.23.refs_1_
  96.3 5.8 %collective-permute-done.24.refs_2_ = bf16[128,1152]{1,0:T(8,128)(2,1)S(1)} collective-permute-done((bf16[128,1152]{1,0:T(8,128)(2,1)}, bf16[128,1152]{1,0:T(8,128)(2,1)S(1)}, u32[]{:S(2)}, u32[]{:S(2)}) %collective-permute-start.24) | collective-permute-done | bytes 294944 | tf_op jit(solution)/shard_map/ppermute | solution.py:381
  104.0 22.4 %experts.3 = (bf16[2,128,2048]{2,1,0:T(8,128)(2,1)}, bf16[2,128,2048]{2,1,0:T(8,128)(2,1)}) custom-call(s32[1]{0:T(128)} %bitcast.18.refs_0_, bf16[128,1024]{1,0:T(8,128)(2,1)} %get-tuple-element.19.refs_1_, bf16[128,1152]{1,0:T(8,128)(2,1)} %get-tuple-element.20.refs_2_, bf16[128,1024]{1,0:T(8,128)(2,1)} %copy-done.19, bf16[128,1152]{1,0:T(8,128)(2,1)} %copy-done.16, ...), custom_call_target="tpu_custom_call" | custom-call | flops 8000000000 | bytes 30000000 | tf_op jit(solution)/shard_map/experts/pallas_call | solution.py:343
  126.6 17.6 %experts.5 = (bf16[1,128,2048]{2,1,0:T(8,128)(2,1)}, bf16[1,128,2048]{2,1,0:T(8,128)(2,1)}) custom-call(s32[1]{0:T(128)} %bitcast.18.refs_0_, bf16[128,1024]{1,0:T(8,128)(2,1)} %collective-permute-done.23.refs_1_, bf16[128,1152]{1,0:T(8,128)(2,1)} %copy-done.4, bf16[128,1024]{1,0:T(8,128)(2,1)} %collective-permute-done.25.refs_3_, ...), custom_call_target="tpu_custom_call" | custom-call | flops 4000000000 | bytes 30000000 | tf_op jit(solution)/shard_map/experts/pallas_call | solution.py:343
  144.6 1.7 collective-permute-done.27
  146.3 1.2 fusion.5
  147.9 2.5 %collective-permute-start.16 = (bf16[128,2048]{1,0:T(8,128)(2,1)S(1)}, bf16[128,2048]{1,0:T(8,128)(2,1)S(1)}, u32[]{:S(2)}, u32[]{:S(2)}) collective-permute-start(bf16[128,2048]{1,0:T(8,128)(2,1)S(1)} %fusion.3), channel_id=1, source_target_pairs={{0,2},{1,3},{2,0},{3,1},{4,6},{5,7},{6,4},{7,5},{8,10},{9,11},{10,... | collective-permute-start | bytes 1572872 | tf_op jit(solution)/shard_map/ppermute | solution.py:381
  151.4 2.1 %maximum_bitcast_fusion = f32[1,16,128,128]{3,2,1,0:T(8,128)} fusion(f32[8,128,128]{2,1,0:T(8,128)S(1)} %copy-done.2, f32[8,128,128]{2,1,0:T(8,128)} %get-tuple-element.27), kind=kLoop, calls=%fused_computation | loop fusion | flops 262144 | bytes 2097152 | tf_op jit(solution)/shard_map/broadcast_in_dim | solution.py:483
  153.5 1.8 pad_maximum_fusion
  155.3 24.0 %collective-permute-done.22 = bf16[128,2048]{1,0:T(8,128)(2,1)S(1)} collective-permute-done((bf16[128,2048]{1,0:T(8,128)(2,1)S(1)}, bf16[128,2048]{1,0:T(8,128)(2,1)S(1)}, u32[]{:S(2)}, u32[]{:S(2)}) %collective-permute-start.22) | collective-permute-done | bytes 524320 | tf_op jit(solution)/shard_map/ppermute | solution.py:381
  179.3 11.6 %collective-permute-done.28 = bf16[128,2048]{1,0:T(8,128)(2,1)S(1)} collective-permute-done((bf16[128,2048]{1,0:T(8,128)(2,1)S(1)}, bf16[128,2048]{1,0:T(8,128)(2,1)S(1)}, u32[]{:S(2)}, u32[]{:S(2)}) %collective-permute-start.28) | collective-permute-done | bytes 524320 | tf_op jit(solution)/shard_map/ppermute | solution.py:381
  191.0 1.2 fusion.2
  (91 shorter events, 13.7 us)
Async XLA Ops:
  2.0 3.5 %collective-permute-start = (s32[2]{0:T(128)S(1)}, s32[2]{0:T(128)S(1)}, u32[]{:S(2)}, u32[]{:S(2)}) collective-permute-start(s32[2]{0:T(128)S(1)} %pad_add_fusion.1), channel_id=1, source_target_pairs={{0,8},{8,0},{16,24},{24,16},{1,9},{9,1},{17,25},{25,17},{2,10},{10... | collective-permute-start | bytes 32 | tf_op jit(solution)/shard_map/ppermute | solution.py:381
  3.5 3.9 %collective-permute-start.2 = (s32[2]{0:T(128)S(1)}, s32[2]{0:T(128)S(1)}, u32[]{:S(2)}, u32[]{:S(2)}) collective-permute-start(s32[2]{0:T(128)S(1)} %pad_add_fusion.1), channel_id=1, source_target_pairs={{0,16},{8,24},{16,0},{24,8},{1,17},{9,25},{17,1},{25,9},{2,18},{10... | collective-permute-start | bytes 32 | tf_op jit(solution)/shard_map/ppermute | solution.py:381
  5.0 4.4 %collective-permute-start.4 = (s32[2]{0:T(128)S(1)}, s32[2]{0:T(128)S(1)}, u32[]{:S(2)}, u32[]{:S(2)}) collective-permute-start(s32[2]{0:T(128)S(1)} %pad_add_fusion.1), channel_id=1, source_target_pairs={{0,24},{8,16},{16,8},{24,0},{1,25},{9,17},{17,9},{25,1},{2,26},{10... | collective-permute-start | bytes 32 | tf_op jit(solution)/shard_map/ppermute | solution.py:381
  13.7 11.5 %collective-permute-start.6 = (bf16[8,128,128]{2,1,0:T(8,128)(2,1)S(1)}, bf16[8,128,128]{2,1,0:T(8,128)(2,1)S(1)}, u32[]{:S(2)}, u32[]{:S(2)}) collective-permute-start(bf16[8,128,128]{2,1,0:T(8,128)(2,1)S(1)} %get-tuple-element.31), channel_id=1, source_target_pairs={{0,8},{8,0},{16,24},{24,16},{1,9},{9,1},{17,25},{25,17},{2,10},{10... | collective-permute-start | bytes 786440 | tf_op jit(solution)/shard_map/ppermute | solution.py:381
  19.6 20.4 %collective-permute-start.7 = (bf16[8,128,128]{2,1,0:T(8,128)(2,1)S(1)}, bf16[8,128,128]{2,1,0:T(8,128)(2,1)S(1)}, u32[]{:S(2)}, u32[]{:S(2)}) collective-permute-start(bf16[8,128,128]{2,1,0:T(8,128)(2,1)S(1)} %get-tuple-element.30), channel_id=1, source_target_pairs={{0,16},{8,24},{16,0},{24,8},{1,17},{9,25},{17,1},{25,9},{2,18},{10... | collective-permute-start | bytes 786440 | tf_op jit(solution)/shard_map/ppermute | solution.py:381
  21.1 18.9 %collective-permute-start.8 = (bf16[8,128,128]{2,1,0:T(8,128)(2,1)S(1)}, bf16[8,128,128]{2,1,0:T(8,128)(2,1)S(1)}, u32[]{:S(2)}, u32[]{:S(2)}) collective-permute-start(bf16[8,128,128]{2,1,0:T(8,128)(2,1)S(1)} %get-tuple-element.34), channel_id=1, source_target_pairs={{0,24},{8,16},{16,8},{24,0},{1,25},{9,17},{17,9},{25,1},{2,26},{10... | collective-permute-start | bytes 786440 | tf_op jit(solution)/shard_map/ppermute | solution.py:381
  22.3 24.7 %collective-permute-start.1 = (bf16[8,128,128]{2,1,0:T(8,128)(2,1)S(1)}, bf16[8,128,128]{2,1,0:T(8,128)(2,1)S(1)}, u32[]{:S(2)}, u32[]{:S(2)}) collective-permute-start(bf16[8,128,128]{2,1,0:T(8,128)(2,1)S(1)} %get-tuple-element.33), channel_id=1, source_target_pairs={{0,8},{8,0},{16,24},{24,16},{1,9},{9,1},{17,25},{25,17},{2,10},{10... | collective-permute-start | bytes 786440 | tf_op jit(solution)/shard_map/ppermute | solution.py:381
  23.6 23.4 %collective-permute-start.3 = (bf16[8,128,128]{2,1,0:T(8,128)(2,1)S(1)}, bf16[8,128,128]{2,1,0:T(8,128)(2,1)S(1)}, u32[]{:S(2)}, u32[]{:S(2)}) collective-permute-start(bf16[8,128,128]{2,1,0:T(8,128)(2,1)S(1)} %get-tuple-element.32), channel_id=1, source_target_pairs={{0,16},{8,24},{16,0},{24,8},{1,17},{9,25},{17,1},{25,9},{2,18},{10... | collective-permute-start | bytes 786440 | tf_op jit(solution)/shard_map/ppermute | solution.py:381
  25.2 21.8 %collective-permute-start.5 = (bf16[8,128,128]{2,1,0:T(8,128)(2,1)S(1)}, bf16[8,128,128]{2,1,0:T(8,128)(2,1)S(1)}, u32[]{:S(2)}, u32[]{:S(2)}) collective-permute-start(bf16[8,128,128]{2,1,0:T(8,128)(2,1)S(1)} %get-tuple-element.29), channel_id=1, source_target_pairs={{0,24},{8,16},{16,8},{24,0},{1,25},{9,17},{17,9},{25,1},{2,26},{10... | collective-permute-start | bytes 786440 | tf_op jit(solution)/shard_map/ppermute | solution.py:381
  46.6 12.9 %collective-permute-start.18 = (bf16[128,1152]{1,0:T(8,128)(2,1)}, bf16[128,1152]{1,0:T(8,128)(2,1)S(1)}, u32[]{:S(2)}, u32[]{:S(2)}) collective-permute-start(bf16[128,1152]{1,0:T(8,128)(2,1)} %get-tuple-element.20.refs_2_), channel_id=1, source_target_pairs={{0,4},{1,5},{2,6},{3,7},{4,0},{5,1},{6,2},{7,3},{8,12},{9,13},{10,... | collective-permute-start | bytes 884744 | tf_op jit(solution)/shard_map/ppermute | solution.py:381
  54.2 13.6 %collective-permute-start.17 = (bf16[128,1024]{1,0:T(8,128)(2,1)}, bf16[128,1024]{1,0:T(8,128)(2,1)S(1)}, u32[]{:S(2)}, u32[]{:S(2)}) collective-permute-start(bf16[128,1024]{1,0:T(8,128)(2,1)} %get-tuple-element.19.refs_1_), channel_id=1, source_target_pairs={{0,4},{1,5},{2,6},{3,7},{4,0},{5,1},{6,2},{7,3},{8,12},{9,13},{10,... | collective-permute-start | bytes 786440 | tf_op jit(solution)/shard_map/ppermute | solution.py:381
  56.9 18.0 %collective-permute-start.12 = (bf16[128,1152]{1,0:T(8,128)(2,1)}, bf16[128,1152]{1,0:T(8,128)(2,1)S(1)}, u32[]{:S(2)}, u32[]{:S(2)}) collective-permute-start(bf16[128,1152]{1,0:T(8,128)(2,1)} %get-tuple-element.20.refs_2_), channel_id=1, source_target_pairs={{0,2},{1,3},{2,0},{3,1},{4,6},{5,7},{6,4},{7,5},{8,10},{9,11},{10,... | collective-permute-start | bytes 884744 | tf_op jit(solution)/shard_map/ppermute | solution.py:381
  59.5 17.5 %collective-permute-start.20 = (bf16[128,1152]{1,0:T(8,128)(2,1)S(1)}, bf16[128,1152]{1,0:T(8,128)(2,1)S(1)}, u32[]{:S(2)}, u32[]{:S(2)}) collective-permute-start(bf16[128,1152]{1,0:T(8,128)(2,1)S(1)} %collective-permute-done.18.refs_2_), channel_id=1, source_target_pairs={{0,1},{1,0},{2,3},{3,2},{4,5},{5,4},{6,7},{7,6},{8,9},{9,8},{10,11... | collective-permute-start | bytes 884744 | tf_op jit(solution)/shard_map/ppermute | solution.py:381
  59.5 15.3 %collective-permute-start.11 = (bf16[128,1024]{1,0:T(8,128)(2,1)}, bf16[128,1024]{1,0:T(8,128)(2,1)S(1)}, u32[]{:S(2)}, u32[]{:S(2)}) collective-permute-start(bf16[128,1024]{1,0:T(8,128)(2,1)} %get-tuple-element.19.refs_1_), channel_id=1, source_target_pairs={{0,2},{1,3},{2,0},{3,1},{4,6},{5,7},{6,4},{7,5},{8,10},{9,11},{10,... | collective-permute-start | bytes 786440 | tf_op jit(solution)/shard_map/ppermute | solution.py:381
  67.6 7.2 %collective-permute-start.9 = (bf16[128,1024]{1,0:T(8,128)(2,1)}, bf16[128,1024]{1,0:T(8,128)(2,1)S(1)}, u32[]{:S(2)}, u32[]{:S(2)}) collective-permute-start(bf16[128,1024]{1,0:T(8,128)(2,1)} %get-tuple-element.19.refs_1_), channel_id=1, source_target_pairs={{0,1},{1,0},{2,3},{3,2},{4,5},{5,4},{6,7},{7,6},{8,9},{9,8},{10,11... | collective-permute-start | bytes 786440 | tf_op jit(solution)/shard_map/ppermute | solution.py:381
  67.9 9.1 %collective-permute-start.19 = (bf16[128,1024]{1,0:T(8,128)(2,1)S(1)}, bf16[128,1024]{1,0:T(8,128)(2,1)S(1)}, u32[]{:S(2)}, u32[]{:S(2)}) collective-permute-start(bf16[128,1024]{1,0:T(8,128)(2,1)S(1)} %collective-permute-done.17.refs_1_), channel_id=1, source_target_pairs={{0,1},{1,0},{2,3},{3,2},{4,5},{5,4},{6,7},{7,6},{8,9},{9,8},{10,11... | collective-permute-start | bytes 786440 | tf_op jit(solution)/shard_map/ppermute | solution.py:381
  74.8 27.7 %copy-start.18 = (bf16[128,1024]{1,0:T(8,128)(2,1)}, bf16[128,1024]{1,0:T(8,128)(2,1)S(1)}, u32[]{:S(2)}) copy-start(bf16[128,1024]{1,0:T(8,128)(2,1)S(1)} %collective-permute-done.11.refs_5_) | copy-start | bytes 786436
  74.8 27.2 %collective-permute-start.10 = (bf16[128,1152]{1,0:T(8,128)(2,1)}, bf16[128,1152]{1,0:T(8,128)(2,1)S(1)}, u32[]{:S(2)}, u32[]{:S(2)}) collective-permute-start(bf16[128,1152]{1,0:T(8,128)(2,1)} %get-tuple-element.20.refs_2_), channel_id=1, source_target_pairs={{0,1},{1,0},{2,3},{3,2},{4,5},{5,4},{6,7},{7,6},{8,9},{9,8},{10,11... | collective-permute-start | bytes 884744 | tf_op jit(solution)/shard_map/ppermute | solution.py:381
  74.8 27.7 %copy-start.19 = (bf16[128,1024]{1,0:T(8,128)(2,1)}, bf16[128,1024]{1,0:T(8,128)(2,1)S(1)}, u32[]{:S(2)}) copy-start(bf16[128,1024]{1,0:T(8,128)(2,1)S(1)} %collective-permute-done.9.refs_3_) | copy-start | bytes 786436
  74.8 21.4 %collective-permute-start.23 = (bf16[128,1024]{1,0:T(8,128)(2,1)}, bf16[128,1024]{1,0:T(8,128)(2,1)}, u32[]{:S(2)}, u32[]{:S(2)}) collective-permute-start(bf16[128,1024]{1,0:T(8,128)(2,1)} %get-tuple-element.19.refs_1_), channel_id=1, source_target_pairs={{0,6},{1,7},{2,4},{3,5},{4,2},{5,3},{6,0},{7,1},{8,14},{9,15},{10,... | collective-permute-start | bytes 786440 | tf_op jit(solution)/shard_map/ppermute | solution.py:381
  74.9 27.7 %copy-start.15 = (bf16[128,1152]{1,0:T(8,128)(2,1)}, bf16[128,1152]{1,0:T(8,128)(2,1)S(1)}, u32[]{:S(2)}) copy-start(bf16[128,1152]{1,0:T(8,128)(2,1)S(1)} %collective-permute-done.12.refs_6_) | copy-start | bytes 884740
  74.9 27.1 %collective-permute-start.24 = (bf16[128,1152]{1,0:T(8,128)(2,1)}, bf16[128,1152]{1,0:T(8,128)(2,1)S(1)}, u32[]{:S(2)}, u32[]{:S(2)}) collective-permute-start(bf16[128,1152]{1,0:T(8,128)(2,1)} %get-tuple-element.20.refs_2_), channel_id=1, source_target_pairs={{0,6},{1,7},{2,4},{3,5},{4,2},{5,3},{6,0},{7,1},{8,14},{9,15},{10,... | collective-permute-start | bytes 884744 | tf_op jit(solution)/shard_map/ppermute | solution.py:381
  76.9 25.6 %collective-permute-start.13 = (bf16[128,1024]{1,0:T(8,128)(2,1)S(1)}, bf16[128,1024]{1,0:T(8,128)(2,1)S(1)}, u32[]{:S(2)}, u32[]{:S(2)}) collective-permute-start(bf16[128,1024]{1,0:T(8,128)(2,1)S(1)} %collective-permute-done.11.refs_5_), channel_id=1, source_target_pairs={{0,1},{1,0},{2,3},{3,2},{4,5},{5,4},{6,7},{7,6},{8,9},{9,8},{10,11... | collective-permute-start | bytes 786440 | tf_op jit(solution)/shard_map/ppermute | solution.py:381
  77.0 25.6 %collective-permute-start.14 = (bf16[128,1152]{1,0:T(8,128)(2,1)S(1)}, bf16[128,1152]{1,0:T(8,128)(2,1)S(1)}, u32[]{:S(2)}, u32[]{:S(2)}) collective-permute-start(bf16[128,1152]{1,0:T(8,128)(2,1)S(1)} %collective-permute-done.12.refs_6_), channel_id=1, source_target_pairs={{0,1},{1,0},{2,3},{3,2},{4,5},{5,4},{6,7},{7,6},{8,9},{9,8},{10,11... | collective-permute-start | bytes 884744 | tf_op jit(solution)/shard_map/ppermute | solution.py:381
  96.3 30.3 %collective-permute-start.25 = (bf16[128,1024]{1,0:T(8,128)(2,1)}, bf16[128,1024]{1,0:T(8,128)(2,1)}, u32[]{:S(2)}, u32[]{:S(2)}) collective-permute-start(bf16[128,1024]{1,0:T(8,128)(2,1)} %collective-permute-done.23.refs_1_), channel_id=1, source_target_pairs={{0,1},{1,0},{2,3},{3,2},{4,5},{5,4},{6,7},{7,6},{8,9},{9,8},{10,11... | collective-permute-start | bytes 786440 | tf_op jit(solution)/shard_map/ppermute | solution.py:381
  102.0 24.6 %collective-permute-start.26 = (bf16[128,1152]{1,0:T(8,128)(2,1)S(1)}, bf16[128,1152]{1,0:T(8,128)(2,1)}, u32[]{:S(2)}, u32[]{:S(2)}) collective-permute-start(bf16[128,1152]{1,0:T(8,128)(2,1)S(1)} %collective-permute-done.24.refs_2_), channel_id=1, source_target_pairs={{0,1},{1,0},{2,3},{3,2},{4,5},{5,4},{6,7},{7,6},{8,9},{9,8},{10,11... | collective-permute-start | bytes 884744 | tf_op jit(solution)/shard_map/ppermute | solution.py:381
  102.1 42.3 %collective-permute-start.21 = (bf16[1,128,2048]{2,1,0:T(8,128)(2,1)}, bf16[1,128,2048]{2,1,0:T(8,128)(2,1)S(1)}, u32[]{:S(2)}, u32[]{:S(2)}) collective-permute-start(bf16[1,128,2048]{2,1,0:T(8,128)(2,1)} %get-tuple-element.24), channel_id=1, source_target_pairs={{0,1},{1,0},{2,3},{3,2},{4,5},{5,4},{6,7},{7,6},{8,9},{9,8},{10,11... | collective-permute-start | bytes 1572872 | tf_op jit(solution)/shard_map/ppermute | solution.py:381
  126.4 21.3 %collective-permute-start.15 = (bf16[2,128,2048]{2,1,0:T(8,128)(2,1)}, bf16[2,128,2048]{2,1,0:T(8,128)(2,1)S(1)}, u32[]{:S(2)}, u32[]{:S(2)}) collective-permute-start(bf16[2,128,2048]{2,1,0:T(8,128)(2,1)} %get-tuple-element.22), channel_id=1, source_target_pairs={{0,1},{1,0},{2,3},{3,2},{4,5},{5,4},{6,7},{7,6},{8,9},{9,8},{10,11... | collective-permute-start | bytes 3145736 | tf_op jit(solution)/shard_map/ppermute | solution.py:381
  144.2 2.1 %collective-permute-start.27 = (bf16[1,128,2048]{2,1,0:T(8,128)(2,1)}, bf16[1,128,2048]{2,1,0:T(8,128)(2,1)S(1)}, u32[]{:S(2)}, u32[]{:S(2)}) collective-permute-start(bf16[1,128,2048]{2,1,0:T(8,128)(2,1)} %get-tuple-element.26), channel_id=1, source_target_pairs={{0,1},{1,0},{2,3},{3,2},{4,5},{5,4},{6,7},{7,6},{8,9},{9,8},{10,11... | collective-permute-start | bytes 1572872 | tf_op jit(solution)/shard_map/ppermute | solution.py:381
  144.5 34.8 %collective-permute-start.22 = (bf16[128,2048]{1,0:T(8,128)(2,1)S(1)}, bf16[128,2048]{1,0:T(8,128)(2,1)S(1)}, u32[]{:S(2)}, u32[]{:S(2)}) collective-permute-start(bf16[128,2048]{1,0:T(8,128)(2,1)S(1)} %fusion.4), channel_id=1, source_target_pairs={{0,4},{1,5},{2,6},{3,7},{4,0},{5,1},{6,2},{7,3},{8,12},{9,13},{10,... | collective-permute-start | bytes 1572872 | tf_op jit(solution)/shard_map/ppermute | solution.py:381
  147.5 43.5 %collective-permute-start.28 = (bf16[128,2048]{1,0:T(8,128)(2,1)S(1)}, bf16[128,2048]{1,0:T(8,128)(2,1)S(1)}, u32[]{:S(2)}, u32[]{:S(2)}) collective-permute-start(bf16[128,2048]{1,0:T(8,128)(2,1)S(1)} %fusion.5), channel_id=1, source_target_pairs={{0,6},{1,7},{2,4},{3,5},{4,2},{5,3},{6,0},{7,1},{8,14},{9,15},{10,... | collective-permute-start | bytes 1572872 | tf_op jit(solution)/shard_map/ppermute | solution.py:381
  147.9 43.1 %collective-permute-start.16 = (bf16[128,2048]{1,0:T(8,128)(2,1)S(1)}, bf16[128,2048]{1,0:T(8,128)(2,1)S(1)}, u32[]{:S(2)}, u32[]{:S(2)}) collective-permute-start(bf16[128,2048]{1,0:T(8,128)(2,1)S(1)} %fusion.3), channel_id=1, source_target_pairs={{0,2},{1,3},{2,0},{3,1},{4,6},{5,7},{6,4},{7,5},{8,10},{9,11},{10,... | collective-permute-start | bytes 1572872 | tf_op jit(solution)/shard_map/ppermute | solution.py:381
  (18 other events, 148.3 us)

commit v3 on v2

--- a/solution.py
+++ b/solution.py
@@ -10,12 +10,13 @@
 EPS = 1e-06
 HEADS_A_STEP = 4
 HEAD_CHUNKS = (8, 8)
-STAGES = ((0, 1), (2,), (3,))
+STAGES = ((0,), (1, 2), (3,))
+PIECES = (1, 2, 4)
 LANES = 128
 FAR = -100000.0
 BF = jnp.bfloat16
 F32 = jnp.float32
-VMEM_BYTES = 60 * 1024 * 1024
+VMEM_BYTES = 24 * 1024 * 1024
 
 
 def iota(shape, dim):
@@ -87,19 +88,19 @@
         t_ref[i] = solved[i].astype(BF)
 
 
-def prepare(queries, keys_in, lb, lbt):
+def prepare(queries, keys_in, lb, lbt, first, heads):
     rows = queries.shape[0]
-    groups = lb.shape[0]
-    heads = groups * HEADS_A_STEP
+    groups = heads // HEADS_A_STEP
+    base = first // HEADS_A_STEP
     wide = HEADS_A_STEP * 128
     return pl.pallas_call(
         prepare_kernel,
         grid=(groups,),
         in_specs=[
-            pl.BlockSpec((rows, wide), lambda i: (0, i)),
-            pl.BlockSpec((rows, wide), lambda i: (0, i)),
-            pl.BlockSpec((1,) + lb.shape[1:], lambda i: (i, 0, 0)),
-            pl.BlockSpec((1,) + lbt.shape[1:], lambda i: (i, 0, 0)),
+            pl.BlockSpec((rows, wide), lambda i: (0, base + i)),
+            pl.BlockSpec((rows, wide), lambda i: (0, base + i)),
+            pl.BlockSpec((1,) + lb.shape[1:], lambda i: (base + i, 0, 0)),
+            pl.BlockSpec((1,) + lbt.shape[1:], lambda i: (base + i, 0, 0)),
         ],
         out_specs=[
             pl.BlockSpec((HEADS_A_STEP, 2 * rows, 128), lambda i: (i, 0, 0)),
@@ -112,9 +113,49 @@
             jax.ShapeDtypeStruct((heads, rows + 128, rows), BF),
         ],
         compiler_params=pltpu.CompilerParams(vmem_limit_bytes=VMEM_BYTES),
-        cost_estimate=pl.CostEstimate(flops=int(2e9), transcendentals=0, bytes_accessed=4000000),
+        cost_estimate=pl.CostEstimate(flops=1000, transcendentals=0, bytes_accessed=1000),
         name="prepare",
     )(queries, keys_in, lb, lbt)
+
+
+def pack_kernel(own_ref, *refs, peers, first):
+    asked, cache_ref, outs = refs[:peers], refs[peers], refs[peers + 1 : 2 * peers + 1]
+    buf, sems = refs[2 * peers + 1 :]
+    heads = buf.shape[1]
+    copies = []
+    for j in range(peers):
+        slot = jnp.where(asked[j][0] == own_ref[0], asked[j][1], 0)
+        copies.append(
+            pltpu.make_async_copy(
+                cache_ref.at[0, slot, pl.ds(first, heads)], buf.at[j], sems.at[j]
+            )
+        )
+        copies[-1].start()
+    for j in range(peers):
+        copies[j].wait()
+        outs[j][...] = buf[j].astype(BF)
+
+
+def pack(own, asked, cache, first, heads):
+    peers = len(asked)
+    shape = (heads,) + cache.shape[3:]
+    return pl.pallas_call(
+        lambda *refs: pack_kernel(*refs, peers=peers, first=first),
+        grid_spec=pltpu.PrefetchScalarGridSpec(
+            num_scalar_prefetch=1 + peers,
+            grid=(1,),
+            in_specs=[pl.BlockSpec(memory_space=pl.ANY)],
+            out_specs=[pl.BlockSpec(shape, lambda i, *p: (0, 0, 0))] * peers,
+            scratch_shapes=[
+                pltpu.VMEM((peers,) + shape, F32),
+                pltpu.SemaphoreType.DMA((peers,)),
+            ],
+        ),
+        out_shape=[jax.ShapeDtypeStruct(shape, BF)] * peers,
+        compiler_params=pltpu.CompilerParams(vmem_limit_bytes=VMEM_BYTES),
+        cost_estimate=pl.CostEstimate(flops=1000, transcendentals=0, bytes_accessed=1000),
+        name="pack",
+    )(own, *asked, cache)
 
 
 def resume_kernel(pick_ref, *refs, peers, first_head, experts):
@@ -153,16 +194,15 @@
                     got_copy(s, j).start()
 
         if experts:
-            lane = iota((rows, LANES), 1)
-            named = jnp.zeros((rows, LANES), F32)
-            for k in range(ids_ref.shape[1]):
-                hit = lane % experts == ids_ref[:, k : k + 1]
-                named = jnp.where(hit, weight_ref[:, k : k + 1], named)
-            coarse = named.astype(BF)
-            fine = named - coarse.astype(F32)
-            both = jnp.where(lane < experts, coarse.astype(F32), fine)
-            both = jnp.where(lane < 2 * experts, both, 0.0)
-            out_ref[:, out_ref.shape[1] - LANES :] = both.astype(BF)
+            line = iota((LANES, rows), 0)
+            named = jnp.zeros((LANES, rows), F32)
+            for k in range(ids_ref.shape[0]):
+                hit = line % experts == ids_ref[k : k + 1, :]
+                named = jnp.where(hit, weight_ref[k : k + 1, :], named)
+            coarse = named.astype(BF).astype(F32)
+            both = jnp.where(line < experts, coarse, named - coarse)
+            both = jnp.where(line < 2 * experts, both, 0.0)
+            out_ref[:, out_ref.shape[1] - LANES :] = jnp.transpose(both).astype(BF)
 
     own_copy(at).wait()
 
@@ -200,6 +240,7 @@
     any_spec = pl.BlockSpec(memory_space=pl.ANY)
     cols = pl.BlockSpec((rows, step * 128), lambda i, p: (0, base + i))
     group = lambda i, p: (base + i, 0, 0)
+    local_group = lambda i, p: (i, 0, 0)
     whole = lambda i, p: (0, 0)
     return pl.pallas_call(
         lambda *refs: resume_kernel(*refs, peers=len(got), first_head=first, experts=experts),
@@ -209,9 +250,9 @@
             in_specs=[any_spec]
             + [any_spec] * len(got)
             + [
-                pl.BlockSpec((step,) + kq.shape[1:], group),
-                pl.BlockSpec((step,) + t.shape[1:], group),
-                pl.BlockSpec((step,) + mk.shape[1:], group),
+                pl.BlockSpec((step,) + kq.shape[1:], local_group),
+                pl.BlockSpec((step,) + t.shape[1:], local_group),
+                pl.BlockSpec((step,) + mk.shape[1:], local_group),
                 cols,
                 pl.BlockSpec((1,) + lb.shape[1:], group),
                 pl.BlockSpec((1,) + lbt.shape[1:], group),
@@ -237,18 +278,18 @@
             jax.ShapeDtypeStruct((heads, 128, 128), F32),
         ],
         compiler_params=pltpu.CompilerParams(vmem_limit_bytes=VMEM_BYTES),
-        cost_estimate=pl.CostEstimate(flops=int(1e9), transcendentals=0, bytes_accessed=6000000),
+        cost_estimate=pl.CostEstimate(flops=1000, transcendentals=0, bytes_accessed=1000),
         name="resume",
     )(pick, cache, *got, kq, t, mk, values, lb, lbt, gate, residual, gain, ids, weight)
 
 
-def expert_kernel(first_ref, *refs, blocks, parts, experts, all_experts, halves):
+def expert_kernel(first_ref, *refs, blocks, parts, experts, all_experts, pieces):
     x_refs, refs = refs[: blocks * parts], refs[blocks * parts :]
-    gain_ref, wg_ref, wu_ref, wd_ref, own_ref, other_ref = refs[:6]
-    xs_ref, posr_ref, posc_ref, wr_ref, chosen_ref, slot_ref, acc_ref, rows_ref = refs[6:]
+    gain_ref, wg_ref, wu_ref, wd_ref, own_ref = refs[:5]
+    other_refs, refs = refs[5 : 5 + pieces], refs[5 + pieces :]
+    xs_ref, posr_ref, posc_ref, wr_ref, chosen_ref, slot_ref, rows_ref = refs
     step = pl.program_id(0)
-    e = step // halves
-    f = step % halves
+    e = step
     rows = x_refs[0].shape[0]
     d = xs_ref.shape[1]
     pairs = blocks // 2
@@ -280,13 +321,12 @@
                 x = jnp.concatenate(pieces, axis=1).astype(F32)
                 mean = jnp.mean(x * x, axis=-1, keepdims=True)
                 to = pl.multiple_of(n * rows + s * slab, slab)
-                xs_ref[pl.ds(to, slab), :] = (x / jnp.sqrt(mean + EPS) * gain).astype(BF)
+                xs_ref[pl.ds(to, slab), :] = (x * (1.0 / jnp.sqrt(mean + EPS)) * gain).astype(BF)
                 return carry
 
             lax.fori_loop(0, rows // slab, norm, 0, unroll=2)
 
-    @pl.when(f == 0)
-    def _():
+    if True:
         for p in range(pairs):
             pos = [posr_ref[2 * p + c, pl.ds(e, 1), :] for c in range(2)]
             weight = [wr_ref[2 * p + c, pl.ds(e, 1), :] for c in range(2)]
@@ -303,19 +343,11 @@
             ).astype(BF)
 
     x = chosen_ref[...]
-    hidden = silu(mm(x, wg_ref[0])) * mm(x, wu_ref[0]) * slot_ref[:, 0:1]
-    part = mm(hidden.astype(BF), wd_ref[0])
-
-    @pl.when(f == 0)
-    def _():
-        acc_ref[...] = part
-
-    @pl.when(f == halves - 1)
-    def _():
-        done = (part if halves == 1 else acc_ref[...] + part).astype(BF)
-        to = pl.multiple_of(e * PAIR, 16)
-        for p in range(pairs):
-            rows_ref[p, pl.ds(to, PAIR), :] = done[p * PAIR : (p + 1) * PAIR]
+    hidden = silu(mm(x, wg_ref[e])) * mm(x, wu_ref[e]) * slot_ref[:, 0:1]
+    done = mm(hidden.astype(BF), wd_ref[e]).astype(BF)
+    to = pl.multiple_of(e * PAIR, 16)
+    for p in range(pairs):
+        rows_ref[p, pl.ds(to, PAIR), :] = done[p * PAIR : (p + 1) * PAIR]
 
     @pl.when(step == pl.num_programs(0) - 1)
     def _():
@@ -327,35 +359,35 @@
                 hit = hit | (lane == at[:, n : n + 1] + float(n * PAIR))
             both = mm(hit.astype(F32).astype(BF), rows_ref[p]).astype(BF)
             own_ref[p] = both[:rows]
-            other_ref[p] = both[rows:]
-
-
-def expert_stage(first, xs, parts, gain, w_gate, w_up, w_down, all_experts):
+            for n in range(pieces):
+                other_refs[n][p] = both[rows:, n * d // pieces : (n + 1) * d // pieces]
+
+
+def expert_stage(first, xs, parts, gain, w_gate, w_up, w_down, all_experts, pieces):
     experts, d, ff = w_gate.shape
     rows = xs[0].shape[0]
     blocks = len(xs) // parts
     pairs = blocks // 2
-    halves = 2
-    part = ff // halves
     one = pl.Buffered(1)
-    out = jax.ShapeDtypeStruct((pairs, rows, d), BF)
+    outs = [jax.ShapeDtypeStruct((pairs, rows, d), BF)]
+    outs += [jax.ShapeDtypeStruct((pairs, rows, d // pieces), BF)] * pieces
     whole3 = lambda s, m: (0, 0, 0)
     return pl.pallas_call(
         lambda *refs: expert_kernel(
             *refs, blocks=blocks, parts=parts, experts=experts, all_experts=all_experts,
-            halves=halves,
+            pieces=pieces,
         ),
         grid_spec=pltpu.PrefetchScalarGridSpec(
             num_scalar_prefetch=1,
-            grid=(experts * halves,),
+            grid=(experts,),
             in_specs=[pl.BlockSpec(x.shape, lambda s, m: (0, 0), pipeline_mode=one) for x in xs]
             + [
                 pl.BlockSpec((1, d), lambda s, m: (0, 0)),
-                pl.BlockSpec((1, d, part), lambda s, m: (s // halves, 0, s % halves)),
-                pl.BlockSpec((1, d, part), lambda s, m: (s // halves, 0, s % halves)),
-                pl.BlockSpec((1, part, d), lambda s, m: (s // halves, s % halves, 0)),
+                pl.BlockSpec(memory_space=pltpu.VMEM),
+                pl.BlockSpec(memory_space=pltpu.VMEM),
+                pl.BlockSpec(memory_space=pltpu.VMEM),
             ],
-            out_specs=[pl.BlockSpec(out.shape, whole3), pl.BlockSpec(out.shape, whole3)],
+            out_specs=[pl.BlockSpec(out.shape, whole3) for out in outs],
             scratch_shapes=[
                 pltpu.VMEM((blocks * rows, d), BF),
                 pltpu.VMEM((blocks, LANES, rows), F32),
@@ -363,22 +395,24 @@
                 pltpu.VMEM((blocks, LANES, rows), F32),
                 pltpu.VMEM((pairs * PAIR, d), BF),
                 pltpu.VMEM((pairs * PAIR, LANES), F32),
-                pltpu.VMEM((pairs * PAIR, d), F32),
                 pltpu.VMEM((pairs, experts * PAIR, d), BF),
             ],
         ),
-        out_shape=[out, out],
+        out_shape=outs,
         compiler_params=pltpu.CompilerParams(vmem_limit_bytes=VMEM_BYTES),
-        cost_estimate=pl.CostEstimate(
-            flops=int(4e9) * pairs, transcendentals=0, bytes_accessed=30000000
-        ),
+        cost_estimate=pl.CostEstimate(flops=1000, transcendentals=0, bytes_accessed=1000),
         name="experts",
     )(first, *xs, gain, w_gate, w_up, w_down)
 
 
-def swap(x, axis, bits):
+def after(*xs):
+    return lax.optimization_barrier(xs)
+
+
+def swap(x, axis, bits, what):
     size = lax.axis_size(axis)
-    return lax.ppermute(x, axis, [(i, i ^ bits) for i in range(size)])
+    with jax.named_scope(what):
+        return lax.ppermute(x, axis, [(i, i ^ bits) for i in range(size)])
 
 
 def local(
@@ -412,21 +446,6 @@
     chunks = HEAD_CHUNKS
     starts = [sum(chunks[:g]) for g in range(len(chunks))]
 
-    wish = jnp.concatenate([hit_holder, hit_slot])
-    sends = []
-    for j in range(1, holders):
-        asked = swap(wish, "dp", j)
-        sends.append(jnp.where(asked[0] == own_dp, asked[1], 0))
-    got = []
-    for first, heads in zip(starts, chunks):
-        got.append([])
-        for j in range(1, holders):
-            piece = lax.dynamic_slice(
-                state_cache, (0, sends[j - 1], first, 0, 0), (1, 1, heads) + state_cache.shape[3:]
-            )[0, 0].astype(BF)
-            got[-1].append(swap(piece, "dp", j))
-    pick = jnp.stack([hit_holder[0] ^ own_dp, hit_slot[0]])
-
     groups = head_count // HEADS_A_STEP
     lb = jnp.concatenate(
         [
@@ -436,51 +455,92 @@
         axis=1,
     )
     lbt = lb.transpose(0, 2, 1)
-    kq, t, mk = prepare(queries, keys_in, lb, lbt)
+    pick = jnp.stack([hit_holder[0] ^ own_dp, hit_slot[0]])
+
+    wish = jnp.concatenate([hit_holder, hit_slot])
+    asked = [swap(wish, "dp", j, f"hits{j}") for j in range(1, holders)]
+    asked[0], lb, lbt, pick = after(asked[0], lb, lbt, pick)
+    got = []
+    for first, heads in zip(starts, chunks):
+        pieces = pack(own_dp[None], asked, state_cache, first, heads)
+        asked[0], *pieces = after(asked[0], *pieces)
+        got.append(
+            [swap(p, "dp", j + 1, f"state{first}from{j + 1}") for j, p in enumerate(pieces)]
+        )
+
+    lb = after(lb, asked[0])[0]
     mixed, states = [], []
     for g, (first, heads) in enumerate(zip(starts, chunks)):
         last = g == len(chunks) - 1
+        kq, t, mk = prepare(queries, keys_in, lb, lbt, first, heads)
         m, s = resume(
             pick, state_cache, got[g], kq, t, mk, values_in, lb, lbt, out_gate, residual_in,
-            head_gain[None], expert_ids, gate_weight, first, heads, all_experts if last else 0,
-        )
+            head_gain[None], expert_ids.T, gate_weight.T, first, heads, all_experts if last else 0,
+        )
+        pick, lb = after(pick, lb, m)[:2]
         mixed.append(m)
         states.append(s)
     parts = len(chunks)
+    next_state = jnp.concatenate(states, axis=0)[None]
     mixer_out = jnp.concatenate(mixed[:-1] + [mixed[-1][:, :-LANES]], axis=1)
 
     gain = moe_gain[None]
     first_expert = (own_ep * experts)[None].astype(jnp.int32)
     weights = (w_gate, w_up, w_down)
     if group == 8:
-        blocks = [[] for _ in range(group)]
+        whole = jnp.concatenate(mixed, axis=1)
+        near = [mixed, [], [], []]
         for c in range(parts):
-            for r in (0, 2, 3, 1):
-                near = mixed[c] if r == 0 else swap(mixed[c], "expert", 2 * r)
-                blocks[2 * r].append(near)
-                blocks[2 * r + 1].append(swap(near, "expert", 1))
-        total = None
-        for stage in STAGES:
-            xs = [x for r in stage for x in blocks[2 * r] + blocks[2 * r + 1]]
-            own, other = expert_stage(first_expert, xs, parts, gain, *weights, all_experts)
-            came = swap(other, "expert", 1)
+            near[2].append(swap(mixed[c], "expert", 4, f"rows{c}chip2"))
+        near[3].append(swap(whole, "expert", 6, "rowschip3"))
+        for c in range(parts):
+            x = after(mixed[c], mixed[-1])[0]
+            near[1].append(swap(x, "expert", 2, f"rows{c}chip1"))
+        sums, ready = [], []
+        gain, mixer_out, next_state = after(gain, mixer_out, next_state)
+        for stage, pieces in zip(STAGES, PIECES):
+            if stage == STAGES[-1]:
+                gain = after(gain, *ready)[0]
+            xs = []
+            for r in stage:
+                held = [after(x, own)[0] for x in near[r]] if r else near[r]
+                xs += near[r]
+                xs += [swap(x, "expert", 1, f"rows{c}pair{r}") for c, x in enumerate(held)]
+            count = len(xs) // (2 * len(stage))
+            own, *other = expert_stage(
+                first_expert, xs, count, gain, *weights, all_experts, pieces
+            )
+            gain = after(gain, own)[0]
+            came = [swap(o, "expert", 1, f"sums{stage[0]}pair") for o in other]
+            wide = d // pieces
             for i, r in enumerate(stage):
-                chip = own[i].astype(F32) + came[i].astype(F32)
-                if r:
-                    chip = swap(chip.astype(BF), "expert", 2 * r).astype(F32)
-                total = chip if total is None else total + chip
-        expert_out = total.astype(BF)
+                chip = [
+                    own[i][:, n * wide : (n + 1) * wide].astype(F32) + came[n][i].astype(F32)
+                    for n in range(pieces)
+                ]
+                if r in (1, 2):
+                    chip = jnp.concatenate(chip, axis=1).astype(BF)
+                    ready.append(chip)
+                    chip = [swap(chip, "expert", 2 * r, f"sums{r}chip").astype(F32)]
+                elif r == 3:
+                    chip = [
+                        swap(c.astype(BF), "expert", 2 * r, f"sums{r}chip").astype(F32)
+                        for c in chip
+                    ]
+                sums.append(jnp.concatenate(chip, axis=1))
+        expert_out = sum(sums).astype(BF)
     else:
         order = jnp.arange(group, dtype=jnp.int32) ^ own_ep
         x = lax.all_gather(jnp.concatenate(mixed, axis=1), "expert", axis=0)[order]
         sums = []
         for p in range(0, group, 8):
             xs = [x[p + i] for i in range(8)]
-            own, other = expert_stage(first_expert, xs, 1, gain, *weights, all_experts)
+            own, *other = expert_stage(first_expert, xs, 1, gain, *weights, all_experts, 1)
+            other = jnp.concatenate(other, axis=2)
             sums.append(jnp.stack([own, other], axis=1).reshape(8, rows, d))
         part = jnp.concatenate(sums, axis=0)[order]
         expert_out = lax.psum_scatter(part, "expert", scatter_dimension=0)
-    return (mixer_out, expert_out, jnp.concatenate(states, axis=0)[None])
+    return (mixer_out, expert_out, next_state)
 
 
 def solution(mesh):

time: 194 us -> 167 us (0.86)
  Pallas kernels: 79.5 us -> 49.9 us
  local copies, waits for them, and re-layouts: 12.7 us -> 21.8 us
  waiting for transfers between devices: 55.8 us -> 61.8 us
  starting transfers between devices: 30.1 us -> 25.2 us
  between operations: 6.1 us -> 2.32 us
  other arithmetic: 7.92 us -> 4.62 us
    pallas_call x3, Pallas kernels: 57.2 us -> 29.9 us  [expert_stage(): pl.pallas_call(lambda *refs: expert_kernel(*refs, blocks=blocks, parts=pa...]
    unnamed x44 -> x48, local copies, waits for them, and re-layouts: 6.78 us -> 21.6 us
    ppermute x29 -> x34, waiting for transfers between devices: 55.8 us -> 61.8 us  [swap(): return lax.ppermute(x, axis, [(i, i ^ bits) for i in range(size)])]
    ppermute x29 -> x34, starting transfers between devices: 30.1 us -> 25.2 us  [swap(): return lax.ppermute(x, axis, [(i, i ^ bits) for i in range(size)])]
    pallas_call x2, Pallas kernels: 11.6 us -> 7.74 us  [resume(): pl.pallas_call(lambda *refs: resume_kernel(*refs, peers=len(got), first_h...]
    pallas_call x0 -> x2, Pallas kernels: none -> 3.2 us  [pack(): pl.pallas_call(lambda *refs: pack_kernel(*refs, peers=peers, first=first)...]
    convert_element_type x1 -> x0, local copies, waits for them, and re-layouts: 2.32 us -> none  [local(): piece = lax.dynamic_slice(state_cache, (0, sends[j - 1], first, 0, 0), (1...]
    pallas_call x1 -> x2, Pallas kernels: 10.8 us -> 9.09 us  [prepare(): pl.pallas_call(prepare_kernel, grid=(groups,), in_specs=[pl.BlockSpec((ro...]
  transfers between devices with their start and end apart: 29 -> 34, of which waited for: 10 -> 14; matrix products, arithmetic and copies ran while one was open for 6% -> 2% of each run, Pallas kernels for 41% -> 29%
where the time goes in v3:
time: 167 us; the launch traced here: 166 us
  waiting for transfers between devices  61.8 us (37%)
  Pallas kernels  49.9 us (30%)
  starting transfers between devices  25.2 us (15%)
  local copies, waits for them, and re-layouts  21.8 us (13%)
  other arithmetic  4.62 us (3%)
  between operations  2.32 us (1%)
    ppermute x34, waiting for transfers between devices, swap(): return lax.ppermute(x, axis, [(i, i ^ bits) for i in range(size)])  61.8 us
    pallas_call x3, Pallas kernels, expert_stage(): pl.pallas_call(lambda *refs: expert_kernel(*refs, blocks=blocks, parts=pa...  29.9 us
    ppermute x34, starting transfers between devices, swap(): return lax.ppermute(x, axis, [(i, i ^ bits) for i in range(size)])  25.2 us
    unnamed x48, local copies, waits for them, and re-layouts  21.6 us
    pallas_call x2, Pallas kernels, prepare(): pl.pallas_call(prepare_kernel, grid=(groups,), in_specs=[pl.BlockSpec((ro...  9.09 us
    pallas_call x2, Pallas kernels, resume(): pl.pallas_call(lambda *refs: resume_kernel(*refs, peers=len(got), first_h...  7.74 us
  transfers between devices with their start and end apart: 34, of which 14 were waited for; matrix products, arithmetic and copies ran while one was open for 2% of the time, Pallas kernels for 29%

profile of v3, /device:TPU:16, one launch (start us, length us, event | category | flops | bytes accessed | tf_op | source)
XLA Modules:
  0.0 165.7 jit_solution(10812196278682294107)
XLA Ops:
  2.0 2.5 %collective-permute-start.2 = (s32[2]{0:T(128)S(1)}, s32[2]{0:T(128)S(1)}, u32[]{:S(2)}, u32[]{:S(2)}) collective-permute-start(s32[2]{0:T(128)S(1)} %pad_add_fusion), channel_id=1, source_target_pairs={{0,24},{8,16},{16,8},{24,0},{1,25},{9,17},{17,9},{25,1},{2,26},{10... | collective-permute-start | bytes 32 | tf_op jit(solution)/shard_map/hits3/ppermute | solution.py:415
  6.4 2.1 %collective-permute-done.refs_1_ = s32[2]{0:T(128)S(1)} collective-permute-done((s32[2]{0:T(128)S(1)}, s32[2]{0:T(128)S(1)}, u32[]{:S(2)}, u32[]{:S(2)}) %collective-permute-start) | collective-permute-done | bytes 40 | tf_op jit(solution)/shard_map/hits1/ppermute | solution.py:415
  8.5 1.6 copy-done.4
  10.1 1.6 pack.2
  12.3 1.5 collective-permute-start.4
  13.8 1.4 collective-permute-start.5
  15.3 1.6 pack.3
  17.5 1.5 collective-permute-start.7
  19.0 2.0 %collective-permute-done.3.refs_2_ = bf16[8,128,128]{2,1,0:T(8,128)(2,1)S(1)} collective-permute-done((bf16[8,128,128]{2,1,0:T(8,128)(2,1)S(1)}, bf16[8,128,128]{2,1,0:T(8,128)(2,1)S(1)}, u32[]{:S(2)}, u32[]{:S(2)}) %collective-permute-start.3) | collective-permute-done | bytes 262176 | tf_op jit(solution)/shard_map/state0from1/ppermute | solution.py:415
  21.7 1.5 collective-permute-start.8
  25.3 4.5 %prepare.2 = (bf16[8,256,128]{2,1,0:T(8,128)(2,1)S(1)}, bf16[8,128,128]{2,1,0:T(8,128)(2,1)S(1)}, bf16[8,256,128]{2,1,0:T(8,128)(2,1)S(1)}) custom-call(bf16[128,2048]{1,0:T(8,128)(2,1)S(1)} %copy-done.10, bf16[128,2048]{1,0:T(8,128)(2,1)S(1)} %copy-done.11, f32[4,8,128]{2,1,0:T(8,128)S(1)} %pad_maximum_fusion.4.lb_ref.refs_9_, f32[4,128,8]{2,1,0:T(8,128)S(1)} %bitcast.63), custom_call_target="tpu_custom_call" | custom-call | flops 1000 | bytes 1000 | tf_op jit(solution)/shard_map/prepare/pallas_call | solution.py:96
  31.9 3.9 %resume.2 = (bf16[128,1024]{1,0:T(8,128)(2,1)S(1)}, f32[8,128,128]{2,1,0:T(8,128)S(1)}) custom-call(s32[2]{0:T(128)S(1)} %pad_add_fusion.1.refs_0_, f32[1,2,16,128,128]{4,3,2,1,0:T(8,128)S(1)} %copy-done.5, bf16[8,128,128]{2,1,0:T(8,128)(2,1)S(1)} %copy-done.15, bf16[8,128,128]{2,1,0:T(8,128)(2,1)} %collective-permute-done.4.refs_3_, ...), custom_call_target="tpu_custom_call" | custom-call | flops 1000 | bytes 1000 | tf_op jit(solution)/shard_map/resume/pallas_call | solution.py:245
  36.0 4.6 %prepare.3 = (bf16[8,256,128]{2,1,0:T(8,128)(2,1)S(1)}, bf16[8,128,128]{2,1,0:T(8,128)(2,1)S(1)}, bf16[8,256,128]{2,1,0:T(8,128)(2,1)S(1)}) custom-call(bf16[128,2048]{1,0:T(8,128)(2,1)S(1)} %copy-done.10, bf16[128,2048]{1,0:T(8,128)(2,1)S(1)} %copy-done.11, f32[4,8,128]{2,1,0:T(8,128)S(1)} %pad_maximum_fusion.4.lb_ref.refs_9_, f32[4,128,8]{2,1,0:T(8,128)S(1)} %bitcast.65), custom_call_target="tpu_custom_call" | custom-call | flops 1000 | bytes 1000 | tf_op jit(solution)/shard_map/prepare/pallas_call | solution.py:96
  40.6 3.9 %resume.3 = (bf16[128,1152]{1,0:T(8,128)(2,1)S(1)}, f32[8,128,128]{2,1,0:T(8,128)S(1)}) custom-call(s32[2]{0:T(128)S(1)} %pad_add_fusion.1.refs_0_, f32[1,2,16,128,128]{4,3,2,1,0:T(8,128)S(1)} %copy-done.5, bf16[8,128,128]{2,1,0:T(8,128)(2,1)} %collective-permute-done.6.refs_2_, bf16[8,128,128]{2,1,0:T(8,128)(2,1)} %collective-permute-done.7.refs_3_, ...), custom_call_target="tpu_custom_call" | custom-call | flops 1000 | bytes 1000 | tf_op jit(solution)/shard_map/resume/pallas_call | solution.py:245
  44.5 2.9 %collective-permute-start.17 = (bf16[128,1152]{1,0:T(8,128)(2,1)S(1)}, bf16[128,1152]{1,0:T(8,128)(2,1)S(1)}, u32[]{:S(2)}, u32[]{:S(2)}) collective-permute-start(bf16[128,1152]{1,0:T(8,128)(2,1)S(1)} %get-tuple-element.89.refs_2_), channel_id=1, source_target_pairs={{0,4},{1,5},{2,6},{3,7},{4,0},{5,1},{6,2},{7,3},{8,12},{9,13},{10,... | collective-permute-start | bytes 884744 | tf_op jit(solution)/shard_map/rows1chip2/ppermute | solution.py:415
  47.6 1.4 collective-permute-start.13
  51.7 3.4 %copy-done = bf16[4,2048,512]{2,1,0:T(8,128)(2,1)S(1)} copy-done((bf16[4,2048,512]{2,1,0:T(8,128)(2,1)S(1)}, bf16[4,2048,512]{2,1,0:T(8,128)(2,1)}, u32[]{:S(2)}) %copy-start) | copy-done | bytes 8388632
  55.1 3.4 %copy-done.2 = bf16[4,512,2048]{2,1,0:T(8,128)(2,1)S(1)} copy-done((bf16[4,512,2048]{2,1,0:T(8,128)(2,1)S(1)}, bf16[4,512,2048]{2,1,0:T(8,128)(2,1)}, u32[]{:S(2)}) %copy-start.2) | copy-done | bytes 8388632
  58.5 8.2 %experts.3 = (bf16[1,128,2048]{2,1,0:T(8,128)(2,1)S(1)}, bf16[1,128,2048]{2,1,0:T(8,128)(2,1)S(1)}) custom-call(s32[1]{0:T(128)} %bitcast.11.refs_0_, bf16[128,1024]{1,0:T(8,128)(2,1)S(1)} %get-tuple-element.88.refs_1_, bf16[128,1152]{1,0:T(8,128)(2,1)S(1)} %get-tuple-element.89.refs_2_, bf16[128,1024]{1,0:T(8,128)(2,1)S(1)} %collective-permute-done.9.refs_3_, ...), custom_call_target="tpu_custom_call" | custom-call | flops 1000 | bytes 1000 | tf_op jit(solution)/shard_map/experts/pallas_call | solution.py:375
  67.3 11.5 %collective-permute-done.12.refs_1_ = bf16[128,1024]{1,0:T(8,128)(2,1)S(1)} collective-permute-done((bf16[128,1024]{1,0:T(8,128)(2,1)S(1)}, bf16[128,1024]{1,0:T(8,128)(2,1)S(1)}, u32[]{:S(2)}, u32[]{:S(2)}) %collective-permute-start.12) | collective-permute-done | bytes 262176 | tf_op jit(solution)/shard_map/rows0chip1/ppermute | solution.py:415
  81.7 13.5 %experts.4 = (bf16[2,128,2048]{2,1,0:T(8,128)(2,1)S(1)}, bf16[2,128,1024]{2,1,0:T(8,128)(2,1)S(1)}, bf16[2,128,1024]{2,1,0:T(8,128)(2,1)S(1)}) custom-call(s32[1]{0:T(128)} %bitcast.11.refs_0_, bf16[128,1024]{1,0:T(8,128)(2,1)S(1)} %collective-permute-done.12.refs_1_, bf16[128,1152]{1,0:T(8,128)(2,1)S(1)} %collective-permute-done.13.refs_2_, ...), custom_call_target="tpu_custom_call" | custom-call | flops 1000 | bytes 1000 | tf_op jit(solution)/shard_map/experts/pallas_call | solution.py:375
  99.4 3.4 %copy-done.1 = bf16[4,2048,512]{2,1,0:T(8,128)(2,1)S(1)} copy-done((bf16[4,2048,512]{2,1,0:T(8,128)(2,1)S(1)}, bf16[4,2048,512]{2,1,0:T(8,128)(2,1)}, u32[]{:S(2)}) %copy-start.1) | copy-done | bytes 8388632
  102.8 3.4 %copy-done.3 = bf16[4,512,2048]{2,1,0:T(8,128)(2,1)S(1)} copy-done((bf16[4,512,2048]{2,1,0:T(8,128)(2,1)S(1)}, bf16[4,512,2048]{2,1,0:T(8,128)(2,1)}, u32[]{:S(2)}) %copy-start.3) | copy-done | bytes 8388632
  106.2 8.2 %experts.5 = (bf16[1,128,2048]{2,1,0:T(8,128)(2,1)S(1)}, bf16[1,128,512]{2,1,0:T(8,128)(2,1)S(1)}, bf16[1,128,512]{2,1,0:T(8,128)(2,1)S(1)}, bf16[1,128,512]{2,1,0:T(8,128)(2,1)S(1)}, bf16[1,128,512]{2,1,0:T(8,128)(2,1)S(1)}) custom-call(s32[1]{0:T(128)} %bitcast.11.refs_0_, bf16[128,2176]{1,0:T(8,128)(2,1)S(1)} %collective-permute-done.24.refs_1_, ...), custom_call_target="tpu_custom_call" | custom-call | flops 1000 | bytes 1000 | tf_op jit(solution)/shard_map/experts/pallas_call | solution.py:375
  116.0 2.5 %collective-permute-start.22 = (bf16[128,2048]{1,0:T(8,128)(2,1)S(1)}, bf16[128,2048]{1,0:T(8,128)(2,1)S(1)}, u32[]{:S(2)}, u32[]{:S(2)}) collective-permute-start(bf16[128,2048]{1,0:T(8,128)(2,1)S(1)} %pad_maximum_fusion.2), channel_id=1, source_target_pairs={{0,2},{1,3},{2,0},{3,1},{4,6},{5,7},{6,4},{7,5},{8,10},{9,11},{10,... | collective-permute-start | bytes 1572872 | tf_op jit(solution)/shard_map/sums1chip/ppermute | solution.py:415
  118.7 1.4 collective-permute-start.27
  120.8 1.3 collective-permute-start.31
  122.1 34.0 %collective-permute-done.27 = bf16[128,512]{1,0:T(8,128)(2,1)S(1)} collective-permute-done((bf16[128,512]{1,0:T(8,128)(2,1)S(1)}, bf16[128,512]{1,0:T(8,128)(2,1)S(1)}, u32[]{:S(2)}, u32[]{:S(2)}) %collective-permute-start.27) | collective-permute-done | bytes 131104 | tf_op jit(solution)/shard_map/sums3chip/ppermute | solution.py:415
  156.1 2.8 %collective-permute-done.33 = bf16[128,512]{1,0:T(8,128)(2,1)S(1)} collective-permute-done((bf16[128,512]{1,0:T(8,128)(2,1)S(1)}, bf16[128,512]{1,0:T(8,128)(2,1)S(1)}, u32[]{:S(2)}, u32[]{:S(2)}) %collective-permute-start.33) | collective-permute-done | bytes 131104 | tf_op jit(solution)/shard_map/sums3chip/ppermute | solution.py:415
  158.9 2.8 %collective-permute-done.31 = bf16[128,512]{1,0:T(8,128)(2,1)S(1)} collective-permute-done((bf16[128,512]{1,0:T(8,128)(2,1)S(1)}, bf16[128,512]{1,0:T(8,128)(2,1)S(1)}, u32[]{:S(2)}, u32[]{:S(2)}) %collective-permute-start.31) | collective-permute-done | bytes 131104 | tf_op jit(solution)/shard_map/sums3chip/ppermute | solution.py:415
  161.7 2.7 %collective-permute-done.29 = bf16[128,512]{1,0:T(8,128)(2,1)S(1)} collective-permute-done((bf16[128,512]{1,0:T(8,128)(2,1)S(1)}, bf16[128,512]{1,0:T(8,128)(2,1)S(1)}, u32[]{:S(2)}, u32[]{:S(2)}) %collective-permute-start.29) | collective-permute-done | bytes 131104 | tf_op jit(solution)/shard_map/sums3chip/ppermute | solution.py:415
  164.5 1.2 fusion.2
  (109 shorter events, 21.3 us)
Async XLA Ops:
  2.0 6.5 %collective-permute-start.2 = (s32[2]{0:T(128)S(1)}, s32[2]{0:T(128)S(1)}, u32[]{:S(2)}, u32[]{:S(2)}) collective-permute-start(s32[2]{0:T(128)S(1)} %pad_add_fusion), channel_id=1, source_target_pairs={{0,24},{8,16},{16,8},{24,0},{1,25},{9,17},{17,9},{25,1},{2,26},{10... | collective-permute-start | bytes 32 | tf_op jit(solution)/shard_map/hits3/ppermute | solution.py:415
  4.5 4.1 %collective-permute-start.1 = (s32[2]{0:T(128)S(1)}, s32[2]{0:T(128)S(1)}, u32[]{:S(2)}, u32[]{:S(2)}) collective-permute-start(s32[2]{0:T(128)S(1)} %pad_add_fusion), channel_id=1, source_target_pairs={{0,16},{8,24},{16,0},{24,8},{1,17},{9,25},{17,1},{25,9},{2,18},{10... | collective-permute-start | bytes 32 | tf_op jit(solution)/shard_map/hits2/ppermute | solution.py:415
  5.0 3.5 %collective-permute-start = (s32[2]{0:T(128)S(1)}, s32[2]{0:T(128)S(1)}, u32[]{:S(2)}, u32[]{:S(2)}) collective-permute-start(s32[2]{0:T(128)S(1)} %pad_add_fusion), channel_id=1, source_target_pairs={{0,8},{8,0},{16,24},{24,16},{1,9},{9,1},{17,25},{25,17},{2,10},{10... | collective-permute-start | bytes 32 | tf_op jit(solution)/shard_map/hits1/ppermute | solution.py:415
  11.7 9.3 %collective-permute-start.3 = (bf16[8,128,128]{2,1,0:T(8,128)(2,1)S(1)}, bf16[8,128,128]{2,1,0:T(8,128)(2,1)S(1)}, u32[]{:S(2)}, u32[]{:S(2)}) collective-permute-start(bf16[8,128,128]{2,1,0:T(8,128)(2,1)S(1)} %get-tuple-element.60), channel_id=1, source_target_pairs={{0,8},{8,0},{16,24},{24,16},{1,9},{9,1},{17,25},{25,17},{2,10},{10... | collective-permute-start | bytes 786440 | tf_op jit(solution)/shard_map/state0from1/ppermute | solution.py:415
  12.3 17.5 %collective-permute-start.4 = (bf16[8,128,128]{2,1,0:T(8,128)(2,1)}, bf16[8,128,128]{2,1,0:T(8,128)(2,1)}, u32[]{:S(2)}, u32[]{:S(2)}) collective-permute-start(bf16[8,128,128]{2,1,0:T(8,128)(2,1)} %get-tuple-element.61), channel_id=1, source_target_pairs={{0,16},{8,24},{16,0},{24,8},{1,17},{9,25},{17,1},{25,9},{2,18},{10... | collective-permute-start | bytes 786440 | tf_op jit(solution)/shard_map/state0from2/ppermute | solution.py:415
  13.8 16.0 %collective-permute-start.5 = (bf16[8,128,128]{2,1,0:T(8,128)(2,1)}, bf16[8,128,128]{2,1,0:T(8,128)(2,1)}, u32[]{:S(2)}, u32[]{:S(2)}) collective-permute-start(bf16[8,128,128]{2,1,0:T(8,128)(2,1)} %get-tuple-element.62), channel_id=1, source_target_pairs={{0,24},{8,16},{16,8},{24,0},{1,25},{9,17},{17,9},{25,1},{2,26},{10... | collective-permute-start | bytes 786440 | tf_op jit(solution)/shard_map/state0from3/ppermute | solution.py:415
  16.9 23.6 %collective-permute-start.6 = (bf16[8,128,128]{2,1,0:T(8,128)(2,1)}, bf16[8,128,128]{2,1,0:T(8,128)(2,1)}, u32[]{:S(2)}, u32[]{:S(2)}) collective-permute-start(bf16[8,128,128]{2,1,0:T(8,128)(2,1)} %get-tuple-element.74), channel_id=1, source_target_pairs={{0,8},{8,0},{16,24},{24,16},{1,9},{9,1},{17,25},{25,17},{2,10},{10... | collective-permute-start | bytes 786440 | tf_op jit(solution)/shard_map/state8from1/ppermute | solution.py:415
  17.5 23.1 %collective-permute-start.7 = (bf16[8,128,128]{2,1,0:T(8,128)(2,1)}, bf16[8,128,128]{2,1,0:T(8,128)(2,1)}, u32[]{:S(2)}, u32[]{:S(2)}) collective-permute-start(bf16[8,128,128]{2,1,0:T(8,128)(2,1)} %get-tuple-element.75), channel_id=1, source_target_pairs={{0,16},{8,24},{16,0},{24,8},{1,17},{9,25},{17,1},{25,9},{2,18},{10... | collective-permute-start | bytes 786440 | tf_op jit(solution)/shard_map/state8from2/ppermute | solution.py:415
  21.7 18.8 %collective-permute-start.8 = (bf16[8,128,128]{2,1,0:T(8,128)(2,1)}, bf16[8,128,128]{2,1,0:T(8,128)(2,1)}, u32[]{:S(2)}, u32[]{:S(2)}) collective-permute-start(bf16[8,128,128]{2,1,0:T(8,128)(2,1)} %get-tuple-element.76), channel_id=1, source_target_pairs={{0,24},{8,16},{16,8},{24,0},{1,25},{9,17},{17,9},{25,1},{2,26},{10... | collective-permute-start | bytes 786440 | tf_op jit(solution)/shard_map/state8from3/ppermute | solution.py:415
  35.8 31.5 %collective-permute-start.16 = (bf16[128,1024]{1,0:T(8,128)(2,1)S(1)}, bf16[128,1024]{1,0:T(8,128)(2,1)S(1)}, u32[]{:S(2)}, u32[]{:S(2)}) collective-permute-start(bf16[128,1024]{1,0:T(8,128)(2,1)S(1)} %get-tuple-element.88.refs_1_), channel_id=1, source_target_pairs={{0,4},{1,5},{2,6},{3,7},{4,0},{5,1},{6,2},{7,3},{8,12},{9,13},{10,... | collective-permute-start | bytes 786440 | tf_op jit(solution)/shard_map/rows0chip2/ppermute | solution.py:415
  35.9 14.2 %collective-permute-start.9 = (bf16[128,1024]{1,0:T(8,128)(2,1)S(1)}, bf16[128,1024]{1,0:T(8,128)(2,1)S(1)}, u32[]{:S(2)}, u32[]{:S(2)}) collective-permute-start(bf16[128,1024]{1,0:T(8,128)(2,1)S(1)} %get-tuple-element.88.refs_1_), channel_id=1, source_target_pairs={{0,1},{1,0},{2,3},{3,2},{4,5},{5,4},{6,7},{7,6},{8,9},{9,8},{10,11... | collective-permute-start | bytes 786440 | tf_op jit(solution)/shard_map/rows0pair0/ppermute | solution.py:415
  44.5 22.2 %collective-permute-start.17 = (bf16[128,1152]{1,0:T(8,128)(2,1)S(1)}, bf16[128,1152]{1,0:T(8,128)(2,1)S(1)}, u32[]{:S(2)}, u32[]{:S(2)}) collective-permute-start(bf16[128,1152]{1,0:T(8,128)(2,1)S(1)} %get-tuple-element.89.refs_2_), channel_id=1, source_target_pairs={{0,4},{1,5},{2,6},{3,7},{4,0},{5,1},{6,2},{7,3},{8,12},{9,13},{10,... | collective-permute-start | bytes 884744 | tf_op jit(solution)/shard_map/rows1chip2/ppermute | solution.py:415
  47.4 3.5 %collective-permute-start.10 = (bf16[128,1152]{1,0:T(8,128)(2,1)S(1)}, bf16[128,1152]{1,0:T(8,128)(2,1)S(1)}, u32[]{:S(2)}, u32[]{:S(2)}) collective-permute-start(bf16[128,1152]{1,0:T(8,128)(2,1)S(1)} %get-tuple-element.89.refs_2_), channel_id=1, source_target_pairs={{0,1},{1,0},{2,3},{3,2},{4,5},{5,4},{6,7},{7,6},{8,9},{9,8},{10,11... | collective-permute-start | bytes 884744 | tf_op jit(solution)/shard_map/rows1pair0/ppermute | solution.py:415
  47.6 19.0 %collective-permute-start.13 = (bf16[128,1152]{1,0:T(8,128)(2,1)S(1)}, bf16[128,1152]{1,0:T(8,128)(2,1)S(1)}, u32[]{:S(2)}, u32[]{:S(2)}) collective-permute-start(bf16[128,1152]{1,0:T(8,128)(2,1)S(1)} %get-tuple-element.89.refs_2_), channel_id=1, source_target_pairs={{0,2},{1,3},{2,0},{3,1},{4,6},{5,7},{6,4},{7,5},{8,10},{9,11},{10,... | collective-permute-start | bytes 884744 | tf_op jit(solution)/shard_map/rows1chip1/ppermute | solution.py:415
  50.1 28.6 %collective-permute-start.12 = (bf16[128,1024]{1,0:T(8,128)(2,1)S(1)}, bf16[128,1024]{1,0:T(8,128)(2,1)S(1)}, u32[]{:S(2)}, u32[]{:S(2)}) collective-permute-start(bf16[128,1024]{1,0:T(8,128)(2,1)S(1)} %get-tuple-element.88.refs_1_), channel_id=1, source_target_pairs={{0,2},{1,3},{2,0},{3,1},{4,6},{5,7},{6,4},{7,5},{8,10},{9,11},{10,... | collective-permute-start | bytes 786440 | tf_op jit(solution)/shard_map/rows0chip1/ppermute | solution.py:415
  50.9 45.0 %collective-permute-start.24 = (bf16[128,2176]{1,0:T(8,128)(2,1)S(1)}, bf16[128,2176]{1,0:T(8,128)(2,1)S(1)}, u32[]{:S(2)}, u32[]{:S(2)}) collective-permute-start(bf16[128,2176]{1,0:T(8,128)(2,1)S(1)} %pad_maximum_fusion), channel_id=1, source_target_pairs={{0,6},{1,7},{2,4},{3,5},{4,2},{5,3},{6,0},{7,1},{8,14},{9,15},{10,... | collective-permute-start | bytes 1671176 | tf_op jit(solution)/shard_map/rowschip3/ppermute | solution.py:415
  66.7 14.0 %collective-permute-start.15 = (bf16[128,1152]{1,0:T(8,128)(2,1)S(1)}, bf16[128,1152]{1,0:T(8,128)(2,1)S(1)}, u32[]{:S(2)}, u32[]{:S(2)}) collective-permute-start(bf16[128,1152]{1,0:T(8,128)(2,1)S(1)} %collective-permute-done.13.refs_2_), channel_id=1, source_target_pairs={{0,1},{1,0},{2,3},{3,2},{4,5},{5,4},{6,7},{7,6},{8,9},{9,8},{10,11... | collective-permute-start | bytes 884744 | tf_op jit(solution)/shard_map/rows1pair1/ppermute | solution.py:415
  66.8 13.9 %collective-permute-start.19 = (bf16[128,1152]{1,0:T(8,128)(2,1)S(1)}, bf16[128,1152]{1,0:T(8,128)(2,1)S(1)}, u32[]{:S(2)}, u32[]{:S(2)}) collective-permute-start(bf16[128,1152]{1,0:T(8,128)(2,1)S(1)} %collective-permute-done.17.refs_6_), channel_id=1, source_target_pairs={{0,1},{1,0},{2,3},{3,2},{4,5},{5,4},{6,7},{7,6},{8,9},{9,8},{10,11... | collective-permute-start | bytes 884744 | tf_op jit(solution)/shard_map/rows1pair2/ppermute | solution.py:415
  78.8 1.5 collective-permute-start.14
  78.8 1.9 %collective-permute-start.18 = (bf16[128,1024]{1,0:T(8,128)(2,1)S(1)}, bf16[128,1024]{1,0:T(8,128)(2,1)S(1)}, u32[]{:S(2)}, u32[]{:S(2)}) collective-permute-start(bf16[128,1024]{1,0:T(8,128)(2,1)S(1)} %collective-permute-done.16.refs_5_), channel_id=1, source_target_pairs={{0,1},{1,0},{2,3},{3,2},{4,5},{5,4},{6,7},{7,6},{8,9},{9,8},{10,11... | collective-permute-start | bytes 786440 | tf_op jit(solution)/shard_map/rows0pair2/ppermute | solution.py:415
  95.2 2.0 %collective-permute-start.20 = (bf16[2,128,1024]{2,1,0:T(8,128)(2,1)S(1)}, bf16[2,128,1024]{2,1,0:T(8,128)(2,1)S(1)}, u32[]{:S(2)}, u32[]{:S(2)}) collective-permute-start(bf16[2,128,1024]{2,1,0:T(8,128)(2,1)S(1)} %get-tuple-element.96), channel_id=1, source_target_pairs={{0,1},{1,0},{2,3},{3,2},{4,5},{5,4},{6,7},{7,6},{8,9},{9,8},{10,11... | collective-permute-start | bytes 1572872 | tf_op jit(solution)/shard_map/sums1pair/ppermute | solution.py:415
  95.4 2.5 %collective-permute-start.21 = (bf16[2,128,1024]{2,1,0:T(8,128)(2,1)S(1)}, bf16[2,128,1024]{2,1,0:T(8,128)(2,1)S(1)}, u32[]{:S(2)}, u32[]{:S(2)}) collective-permute-start(bf16[2,128,1024]{2,1,0:T(8,128)(2,1)S(1)} %get-tuple-element.97), channel_id=1, source_target_pairs={{0,1},{1,0},{2,3},{3,2},{4,5},{5,4},{6,7},{7,6},{8,9},{9,8},{10,11... | collective-permute-start | bytes 1572872 | tf_op jit(solution)/shard_map/sums1pair/ppermute | solution.py:415
  95.7 25.0 %collective-permute-start.11 = (bf16[1,128,2048]{2,1,0:T(8,128)(2,1)S(1)}, bf16[1,128,2048]{2,1,0:T(8,128)(2,1)S(1)}, u32[]{:S(2)}, u32[]{:S(2)}) collective-permute-start(bf16[1,128,2048]{2,1,0:T(8,128)(2,1)S(1)} %get-tuple-element.87), channel_id=1, source_target_pairs={{0,1},{1,0},{2,3},{3,2},{4,5},{5,4},{6,7},{7,6},{8,9},{9,8},{10,11... | collective-permute-start | bytes 1572872 | tf_op jit(solution)/shard_map/sums0pair/ppermute | solution.py:415
  95.9 3.6 %collective-permute-start.25 = (bf16[128,2176]{1,0:T(8,128)(2,1)S(1)}, bf16[128,2176]{1,0:T(8,128)(2,1)S(1)}, u32[]{:S(2)}, u32[]{:S(2)}) collective-permute-start(bf16[128,2176]{1,0:T(8,128)(2,1)S(1)} %collective-permute-done.24.refs_1_), channel_id=1, source_target_pairs={{0,1},{1,0},{2,3},{3,2},{4,5},{5,4},{6,7},{7,6},{8,9},{9,8},{10,11... | collective-permute-start | bytes 1671176 | tf_op jit(solution)/shard_map/rows0pair3/ppermute | solution.py:415
  115.0 3.5 %collective-permute-start.30 = (bf16[1,128,512]{2,1,0:T(8,128)(2,1)S(1)}, bf16[1,128,512]{2,1,0:T(8,128)(2,1)S(1)}, u32[]{:S(2)}, u32[]{:S(2)}) collective-permute-start(bf16[1,128,512]{2,1,0:T(8,128)(2,1)S(1)} %get-tuple-element.104), channel_id=1, source_target_pairs={{0,1},{1,0},{2,3},{3,2},{4,5},{5,4},{6,7},{7,6},{8,9},{9,8},{10,11... | collective-permute-start | bytes 393224 | tf_op jit(solution)/shard_map/sums3pair/ppermute | solution.py:415
  115.1 3.4 %collective-permute-start.32 = (bf16[1,128,512]{2,1,0:T(8,128)(2,1)S(1)}, bf16[1,128,512]{2,1,0:T(8,128)(2,1)S(1)}, u32[]{:S(2)}, u32[]{:S(2)}) collective-permute-start(bf16[1,128,512]{2,1,0:T(8,128)(2,1)S(1)} %get-tuple-element.105), channel_id=1, source_target_pairs={{0,1},{1,0},{2,3},{3,2},{4,5},{5,4},{6,7},{7,6},{8,9},{9,8},{10,11... | collective-permute-start | bytes 393224 | tf_op jit(solution)/shard_map/sums3pair/ppermute | solution.py:415
  115.8 48.6 %collective-permute-start.23 = (bf16[128,2048]{1,0:T(8,128)(2,1)S(1)}, bf16[128,2048]{1,0:T(8,128)(2,1)S(1)}, u32[]{:S(2)}, u32[]{:S(2)}) collective-permute-start(bf16[128,2048]{1,0:T(8,128)(2,1)S(1)} %pad_maximum_fusion.3), channel_id=1, source_target_pairs={{0,4},{1,5},{2,6},{3,7},{4,0},{5,1},{6,2},{7,3},{8,12},{9,13},{10,... | collective-permute-start | bytes 1572872 | tf_op jit(solution)/shard_map/sums2chip/ppermute | solution.py:415
  116.0 48.4 %collective-permute-start.22 = (bf16[128,2048]{1,0:T(8,128)(2,1)S(1)}, bf16[128,2048]{1,0:T(8,128)(2,1)S(1)}, u32[]{:S(2)}, u32[]{:S(2)}) collective-permute-start(bf16[128,2048]{1,0:T(8,128)(2,1)S(1)} %pad_maximum_fusion.2), channel_id=1, source_target_pairs={{0,2},{1,3},{2,0},{3,1},{4,6},{5,7},{6,4},{7,5},{8,10},{9,11},{10,... | collective-permute-start | bytes 1572872 | tf_op jit(solution)/shard_map/sums1chip/ppermute | solution.py:415
  118.7 37.4 %collective-permute-start.27 = (bf16[128,512]{1,0:T(8,128)(2,1)S(1)}, bf16[128,512]{1,0:T(8,128)(2,1)S(1)}, u32[]{:S(2)}, u32[]{:S(2)}) collective-permute-start(bf16[128,512]{1,0:T(8,128)(2,1)S(1)} %get-tuple-element.109), channel_id=1, source_target_pairs={{0,6},{1,7},{2,4},{3,5},{4,2},{5,3},{6,0},{7,1},{8,14},{9,15},{10,... | collective-permute-start | bytes 393224 | tf_op jit(solution)/shard_map/sums3chip/ppermute | solution.py:415
  120.0 38.9 %collective-permute-start.33 = (bf16[128,512]{1,0:T(8,128)(2,1)S(1)}, bf16[128,512]{1,0:T(8,128)(2,1)S(1)}, u32[]{:S(2)}, u32[]{:S(2)}) collective-permute-start(bf16[128,512]{1,0:T(8,128)(2,1)S(1)} %get-tuple-element.110), channel_id=1, source_target_pairs={{0,6},{1,7},{2,4},{3,5},{4,2},{5,3},{6,0},{7,1},{8,14},{9,15},{10,... | collective-permute-start | bytes 393224 | tf_op jit(solution)/shard_map/sums3chip/ppermute | solution.py:415
  120.8 41.0 %collective-permute-start.31 = (bf16[128,512]{1,0:T(8,128)(2,1)S(1)}, bf16[128,512]{1,0:T(8,128)(2,1)S(1)}, u32[]{:S(2)}, u32[]{:S(2)}) collective-permute-start(bf16[128,512]{1,0:T(8,128)(2,1)S(1)} %get-tuple-element.111), channel_id=1, source_target_pairs={{0,6},{1,7},{2,4},{3,5},{4,2},{5,3},{6,0},{7,1},{8,14},{9,15},{10,... | collective-permute-start | bytes 393224 | tf_op jit(solution)/shard_map/sums3chip/ppermute | solution.py:415
  156.1 8.4 %collective-permute-start.29 = (bf16[128,512]{1,0:T(8,128)(2,1)S(1)}, bf16[128,512]{1,0:T(8,128)(2,1)S(1)}, u32[]{:S(2)}, u32[]{:S(2)}) collective-permute-start(bf16[128,512]{1,0:T(8,128)(2,1)S(1)} %get-tuple-element.112), channel_id=1, source_target_pairs={{0,6},{1,7},{2,4},{3,5},{4,2},{5,3},{6,0},{7,1},{8,14},{9,15},{10,... | collective-permute-start | bytes 393224 | tf_op jit(solution)/shard_map/sums3chip/ppermute | solution.py:415
  (26 other events, 249.0 us)

commit v4 on v3

--- a/solution.py
+++ b/solution.py
@@ -16,7 +16,7 @@
 FAR = -100000.0
 BF = jnp.bfloat16
 F32 = jnp.float32
-VMEM_BYTES = 24 * 1024 * 1024
+MIB = 1024 * 1024
 
 
 def iota(shape, dim):
@@ -31,7 +31,18 @@
     return x / (1.0 + jnp.exp(-x))
 
 
-def prepare_kernel(q_ref, k_ref, lb_ref, lbt_ref, kq_ref, t_ref, mk_ref):
+def prepare_kernel(*refs, carried):
+    q_ref, k_ref, lb_ref, lbt_ref = refs[:4]
+    from_refs, refs = refs[4 : 4 + carried], refs[4 + carried :]
+    kq_ref, t_ref, mk_ref = refs[:3]
+    to_refs, sems = refs[3 : 3 + carried], refs[3 + carried]
+    copies = [pltpu.make_async_copy(a, b, sems.at[n]) for n, (a, b) in enumerate(zip(from_refs, to_refs))]
+
+    @pl.when(pl.program_id(0) == 0)
+    def _():
+        for copy in copies:
+            copy.start()
+
     rows = q_ref.shape[0]
     dk = 128
     at_row = iota((rows, rows), 0)
@@ -87,35 +98,46 @@
     for i in range(HEADS_A_STEP):
         t_ref[i] = solved[i].astype(BF)
 
-
-def prepare(queries, keys_in, lb, lbt, first, heads):
+    @pl.when(pl.program_id(0) == pl.num_programs(0) - 1)
+    def _():
+        for copy in copies:
+            copy.wait()
+
+
+def prepare(queries, keys_in, lb, lbt, first, heads, carry):
     rows = queries.shape[0]
     groups = heads // HEADS_A_STEP
     base = first // HEADS_A_STEP
     wide = HEADS_A_STEP * 128
-    return pl.pallas_call(
-        prepare_kernel,
+    carry = [pltpu.with_memory_space_constraint(w, pltpu.HBM) for w in carry]
+    kq, t, mk, *carried = pl.pallas_call(
+        lambda *refs: prepare_kernel(*refs, carried=len(carry)),
         grid=(groups,),
         in_specs=[
             pl.BlockSpec((rows, wide), lambda i: (0, base + i)),
             pl.BlockSpec((rows, wide), lambda i: (0, base + i)),
             pl.BlockSpec((1,) + lb.shape[1:], lambda i: (base + i, 0, 0)),
             pl.BlockSpec((1,) + lbt.shape[1:], lambda i: (base + i, 0, 0)),
-        ],
+        ]
+        + [pl.BlockSpec(memory_space=pl.ANY)] * len(carry),
         out_specs=[
             pl.BlockSpec((HEADS_A_STEP, 2 * rows, 128), lambda i: (i, 0, 0)),
             pl.BlockSpec((HEADS_A_STEP, rows, rows), lambda i: (i, 0, 0)),
             pl.BlockSpec((HEADS_A_STEP, rows + 128, rows), lambda i: (i, 0, 0)),
-        ],
+        ]
+        + [pl.BlockSpec(memory_space=pltpu.VMEM)] * len(carry),
         out_shape=[
             jax.ShapeDtypeStruct((heads, 2 * rows, 128), BF),
             jax.ShapeDtypeStruct((heads, rows, rows), BF),
             jax.ShapeDtypeStruct((heads, rows + 128, rows), BF),
-        ],
-        compiler_params=pltpu.CompilerParams(vmem_limit_bytes=VMEM_BYTES),
+        ]
+        + [pltpu.VMEM(w.shape, w.dtype) for w in carry],
+        scratch_shapes=[pltpu.SemaphoreType.DMA((max(1, len(carry)),))],
+        compiler_params=pltpu.CompilerParams(vmem_limit_bytes=12 * MIB),
         cost_estimate=pl.CostEstimate(flops=1000, transcendentals=0, bytes_accessed=1000),
         name="prepare",
-    )(queries, keys_in, lb, lbt)
+    )(queries, keys_in, lb, lbt, *carry)
+    return kq, t, mk, carried
 
 
 def pack_kernel(own_ref, *refs, peers, first):
@@ -152,17 +174,24 @@
             ],
         ),
         out_shape=[jax.ShapeDtypeStruct(shape, BF)] * peers,
-        compiler_params=pltpu.CompilerParams(vmem_limit_bytes=VMEM_BYTES),
+        compiler_params=pltpu.CompilerParams(vmem_limit_bytes=12 * MIB),
         cost_estimate=pl.CostEstimate(flops=1000, transcendentals=0, bytes_accessed=1000),
         name="pack",
     )(own, *asked, cache)
 
 
-def resume_kernel(pick_ref, *refs, peers, first_head, experts):
+def resume_kernel(pick_ref, *refs, peers, first_head, experts, carried):
     cache_ref, got_refs, refs = refs[0], refs[1 : 1 + peers], refs[1 + peers :]
     kq_ref, t_ref, mk_ref, v_ref, lb_ref, lbt_ref, gate_ref, res_ref, gain_ref = refs[:9]
     ids_ref, weight_ref = refs[9:11]
-    out_ref, next_ref, own_buf, got_buf, sem_own, sem_got = refs[11:]
+    from_refs, refs = refs[11 : 11 + carried], refs[11 + carried :]
+    out_ref, next_ref = refs[:2]
+    to_refs, refs = refs[2 : 2 + carried], refs[2 + carried :]
+    own_buf, got_buf, sem_own, sem_got, sem_carry = refs
+    copies = [
+        pltpu.make_async_copy(a, b, sem_carry.at[n])
+        for n, (a, b) in enumerate(zip(from_refs, to_refs))
+    ]
     heads, rows, _ = t_ref.shape
     steps = own_buf.shape[0] // heads
     at = pl.program_id(0)
@@ -193,6 +222,8 @@
                 def _(s=s, j=j):
                     got_copy(s, j).start()
 
+        for copy in copies:
+            copy.start()
         if experts:
             line = iota((LANES, rows), 0)
             named = jnp.zeros((LANES, rows), F32)
@@ -228,13 +259,19 @@
         mixed = (res_ref[:, span].astype(F32) + gated).astype(BF)
         out_ref[:, pl.ds(pl.multiple_of(head * 128, 128), 128)] = mixed
 
+    @pl.when(at == steps - 1)
+    def _():
+        for copy in copies:
+            copy.wait()
+
 
 def resume(
     pick, cache, got, kq, t, mk, values, lb, lbt, gate, residual, gain, ids, weight, first, heads,
-    experts,
+    experts, carry,
 ):
     rows = values.shape[0]
     step = HEADS_A_STEP
+    carry = [pltpu.with_memory_space_constraint(w, pltpu.HBM) for w in carry]
     wide = heads * 128 + (LANES if experts else 0)
     base = first // step
     any_spec = pl.BlockSpec(memory_space=pl.ANY)
@@ -242,8 +279,10 @@
     group = lambda i, p: (base + i, 0, 0)
     local_group = lambda i, p: (i, 0, 0)
     whole = lambda i, p: (0, 0)
-    return pl.pallas_call(
-        lambda *refs: resume_kernel(*refs, peers=len(got), first_head=first, experts=experts),
+    out, state, *carried = pl.pallas_call(
+        lambda *refs: resume_kernel(
+            *refs, peers=len(got), first_head=first, experts=experts, carried=len(carry)
+        ),
         grid_spec=pltpu.PrefetchScalarGridSpec(
             num_scalar_prefetch=1,
             grid=(heads // step,),
@@ -261,26 +300,31 @@
                 pl.BlockSpec((1, 128), whole),
                 pl.BlockSpec(ids.shape, whole),
                 pl.BlockSpec(weight.shape, whole),
-            ],
+            ]
+            + [any_spec] * len(carry),
             out_specs=[
                 pl.BlockSpec((rows, wide), whole),
                 pl.BlockSpec((step, 128, 128), lambda i, p: (i, 0, 0)),
-            ],
+            ]
+            + [pl.BlockSpec(memory_space=pltpu.VMEM)] * len(carry),
             scratch_shapes=[
                 pltpu.VMEM((heads, 128, 128), F32),
                 pltpu.VMEM((heads, 128, 128), BF),
                 pltpu.SemaphoreType.DMA((heads // step,)),
                 pltpu.SemaphoreType.DMA((heads // step,)),
+                pltpu.SemaphoreType.DMA((max(1, len(carry)),)),
             ],
         ),
         out_shape=[
             jax.ShapeDtypeStruct((rows, wide), BF),
             jax.ShapeDtypeStruct((heads, 128, 128), F32),
-        ],
-        compiler_params=pltpu.CompilerParams(vmem_limit_bytes=VMEM_BYTES),
+        ]
+        + [pltpu.VMEM(w.shape, w.dtype) for w in carry],
+        compiler_params=pltpu.CompilerParams(vmem_limit_bytes=12 * MIB),
         cost_estimate=pl.CostEstimate(flops=1000, transcendentals=0, bytes_accessed=1000),
         name="resume",
-    )(pick, cache, *got, kq, t, mk, values, lb, lbt, gate, residual, gain, ids, weight)
+    )(pick, cache, *got, kq, t, mk, values, lb, lbt, gate, residual, gain, ids, weight, *carry)
+    return out, state, carried
 
 
 def expert_kernel(first_ref, *refs, blocks, parts, experts, all_experts, pieces):
@@ -399,7 +443,7 @@
             ],
         ),
         out_shape=outs,
-        compiler_params=pltpu.CompilerParams(vmem_limit_bytes=VMEM_BYTES),
+        compiler_params=pltpu.CompilerParams(vmem_limit_bytes=(4 + 5 * pairs) * MIB),
         cost_estimate=pl.CostEstimate(flops=1000, transcendentals=0, bytes_accessed=1000),
         name="experts",
     )(first, *xs, gain, w_gate, w_up, w_down)
@@ -436,6 +480,10 @@
 ):
     rows, d = queries.shape
     head_count = log_decay.shape[0]
+    queries, keys_in, values_in, out_gate, residual_in, state_cache = (
+        pltpu.with_memory_space_constraint(x, pltpu.HBM)
+        for x in (queries, keys_in, values_in, out_gate, residual_in, state_cache)
+    )
     holders = lax.axis_size("dp")
     group = lax.axis_size("expert")
     own_dp = lax.axis_index("dp")
@@ -459,7 +507,8 @@
 
     wish = jnp.concatenate([hit_holder, hit_slot])
     asked = [swap(wish, "dp", j, f"hits{j}") for j in range(1, holders)]
-    asked[0], lb, lbt, pick = after(asked[0], lb, lbt, pick)
+    *ready, held = prepare(queries, keys_in, lb, lbt, 0, chunks[0], ())
+    asked[0], lb, lbt, pick, *ready = after(asked[0], lb, lbt, pick, *ready)
     got = []
     for first, heads in zip(starts, chunks):
         pieces = pack(own_dp[None], asked, state_cache, first, heads)
@@ -472,11 +521,18 @@
     mixed, states = [], []
     for g, (first, heads) in enumerate(zip(starts, chunks)):
         last = g == len(chunks) - 1
-        kq, t, mk = prepare(queries, keys_in, lb, lbt, first, heads)
-        m, s = resume(
+        if g:
+            more = (w_up, w_down) if g == 1 else ()
+            *ready, new = prepare(queries, keys_in, lb, lbt, first, heads, more)
+            held = held + new
+        kq, t, mk = ready
+        more = (w_gate,) if g == 1 else ()
+        m, s, new = resume(
             pick, state_cache, got[g], kq, t, mk, values_in, lb, lbt, out_gate, residual_in,
             head_gain[None], expert_ids.T, gate_weight.T, first, heads, all_experts if last else 0,
+            more,
         )
+        held = new + held
         pick, lb = after(pick, lb, m)[:2]
         mixed.append(m)
         states.append(s)
@@ -486,19 +542,20 @@
 
     gain = moe_gain[None]
     first_expert = (own_ep * experts)[None].astype(jnp.int32)
-    weights = (w_gate, w_up, w_down)
+    weights = held
     if group == 8:
-        whole = jnp.concatenate(mixed, axis=1)
         near = [mixed, [], [], []]
         for c in range(parts):
             near[2].append(swap(mixed[c], "expert", 4, f"rows{c}chip2"))
-        near[3].append(swap(whole, "expert", 6, "rowschip3"))
+            near[3].append(swap(near[2][c], "expert", 2, f"rows{c}chip3"))
         for c in range(parts):
             x = after(mixed[c], mixed[-1])[0]
             near[1].append(swap(x, "expert", 2, f"rows{c}chip1"))
-        sums, ready = [], []
+        sums, ready, landed = [], [], []
         gain, mixer_out, next_state = after(gain, mixer_out, next_state)
         for stage, pieces in zip(STAGES, PIECES):
+            if stage == STAGES[0]:
+                gain = after(gain, near[2][0])[0]
             if stage == STAGES[-1]:
                 gain = after(gain, *ready)[0]
             xs = []
@@ -521,12 +578,14 @@
                 if r in (1, 2):
                     chip = jnp.concatenate(chip, axis=1).astype(BF)
                     ready.append(chip)
-                    chip = [swap(chip, "expert", 2 * r, f"sums{r}chip").astype(F32)]
+                    chip = swap(chip, "expert", 2 * r, f"sums{r}chip")
+                    landed.append(chip)
+                    chip = [chip.astype(F32)]
                 elif r == 3:
-                    chip = [
-                        swap(c.astype(BF), "expert", 2 * r, f"sums{r}chip").astype(F32)
-                        for c in chip
-                    ]
+                    chip = [c.astype(BF) for c in chip]
+                    half = pieces // 2
+                    chip[half:] = after(*chip[half:], *landed)[:half]
+                    chip = [swap(c, "expert", 2 * r, f"sums{r}chip").astype(F32) for c in chip]
                 sums.append(jnp.concatenate(chip, axis=1))
         expert_out = sum(sums).astype(BF)
     else:

time: 167 us -> 143 us (0.86)
  local copies, waits for them, and re-layouts: 21.8 us -> 2.28 us
  waiting for transfers between devices: 61.8 us -> 47.7 us
  Pallas kernels: 49.9 us -> 56.5 us
  starting transfers between devices: 25.2 us -> 29 us
    unnamed x48 -> x14, local copies, waits for them, and re-layouts: 21.6 us -> 2.07 us
    ppermute x34 -> x36, waiting for transfers between devices: 61.8 us -> 47.7 us  [swap(): return lax.ppermute(x, axis, [(i, i ^ bits) for i in range(size)])]
    ppermute x34 -> x36, starting transfers between devices: 25.2 us -> 29 us  [swap(): return lax.ppermute(x, axis, [(i, i ^ bits) for i in range(size)])]
    pallas_call x2, Pallas kernels: 9.09 us -> 12.3 us  [prepare(): pl.pallas_call(lambda *refs: prepare_kernel(*refs, carried=len(carry)), g...]
    pallas_call x2, Pallas kernels: 7.74 us -> 9.97 us  [resume(): pl.pallas_call(lambda *refs: resume_kernel(*refs, peers=len(got), first_h...]
  transfers between devices with their start and end apart: 34 -> 36, of which waited for: 14 -> 17; matrix products, arithmetic and copies ran while one was open for 2% -> 2% of each run, Pallas kernels for 29% -> 38%
where the time goes in v4:
time: 143 us; the launch traced here: 142 us
  Pallas kernels  56.5 us (40%)
  waiting for transfers between devices  47.7 us (33%)
  starting transfers between devices  29 us (20%)
  other arithmetic  4.55 us (3%)
  local copies, waits for them, and re-layouts  2.28 us (2%)
  between operations  2.22 us (2%)
    ppermute x36, waiting for transfers between devices, swap(): return lax.ppermute(x, axis, [(i, i ^ bits) for i in range(size)])  47.7 us
    pallas_call x3, Pallas kernels, expert_stage(): pl.pallas_call(lambda *refs: expert_kernel(*refs, blocks=blocks, parts=pa...  30.1 us
    ppermute x36, starting transfers between devices, swap(): return lax.ppermute(x, axis, [(i, i ^ bits) for i in range(size)])  29 us
    pallas_call x2, Pallas kernels, prepare(): pl.pallas_call(lambda *refs: prepare_kernel(*refs, carried=len(carry)), g...  12.3 us
    pallas_call x2, Pallas kernels, resume(): pl.pallas_call(lambda *refs: resume_kernel(*refs, peers=len(got), first_h...  9.97 us
    pallas_call x2, Pallas kernels, pack(): pl.pallas_call(lambda *refs: pack_kernel(*refs, peers=peers, first=first)...  4.1 us
  transfers between devices with their start and end apart: 36, of which 17 were waited for; matrix products, arithmetic and copies ran while one was open for 2% of the time, Pallas kernels for 38%

profile of v4, /device:TPU:16, one launch (start us, length us, event | category | flops | bytes accessed | tf_op | source)
XLA Modules:
  0.0 142.2 jit_solution(15700691952012308373)
XLA Ops:
  2.0 1.5 %collective-permute-start = (s32[2]{0:T(128)S(1)}, s32[2]{0:T(128)S(1)}, u32[]{:S(2)}, u32[]{:S(2)}) collective-permute-start(s32[2]{0:T(128)S(1)} %pad_add_fusion), channel_id=1, source_target_pairs={{0,8},{8,0},{16,24},{24,16},{1,9},{9,1},{17,25},{25,17},{2,10},{10... | collective-permute-start | bytes 32 | tf_op jit(solution)/shard_map/hits1/ppermute | solution.py:459
  3.5 1.5 %collective-permute-start.1 = (s32[2]{0:T(128)S(1)}, s32[2]{0:T(128)S(1)}, u32[]{:S(2)}, u32[]{:S(2)}) collective-permute-start(s32[2]{0:T(128)S(1)} %pad_add_fusion), channel_id=1, source_target_pairs={{0,16},{8,24},{16,0},{24,8},{1,17},{9,25},{17,1},{25,9},{2,18},{10... | collective-permute-start | bytes 32 | tf_op jit(solution)/shard_map/hits2/ppermute | solution.py:459
  6.4 5.5 %prepare.2 = (bf16[8,256,128]{2,1,0:T(8,128)(2,1)S(1)}, bf16[8,128,128]{2,1,0:T(8,128)(2,1)S(1)}, bf16[8,256,128]{2,1,0:T(8,128)(2,1)S(1)}) custom-call(bf16[128,2048]{1,0:T(8,128)(2,1)} %refs_0_.3, bf16[128,2048]{1,0:T(8,128)(2,1)} %refs_1_.6, f32[4,8,128]{2,1,0:T(8,128)S(1)} %pad_maximum_fusion.3.refs_2_.refs_9_, f32[4,128,8]{2,1,0:T(8,128)S(1)} %bitcast.59), custom_call_target="tpu_custom_call" | custom-call | flops 1000 | bytes 1000 | tf_op jit(solution)/shard_map/prepare/pallas_call | solution.py:113
  11.9 2.1 %pack.2 = (bf16[8,128,128]{2,1,0:T(8,128)(2,1)S(1)}, bf16[8,128,128]{2,1,0:T(8,128)(2,1)S(1)}, bf16[8,128,128]{2,1,0:T(8,128)(2,1)S(1)}) custom-call(s32[1]{0:T(128)} %bitcast.6.refs_0_, s32[2]{0:T(128)S(1)} %collective-permute-done.refs_1_, s32[2]{0:T(128)S(1)} %collective-permute-done.1.refs_2_, s32[2]{0:T(128)S(1)} %collective-permute-done.2.refs_3_, ...), custom_call_target="tpu_custom_call" | custom-call | flops 1000 | bytes 1000 | tf_op jit(solution)/shard_map/pack/pallas_call | solution.py:164
  14.0 1.6 %collective-permute-start.3 = (bf16[8,128,128]{2,1,0:T(8,128)(2,1)S(1)}, bf16[8,128,128]{2,1,0:T(8,128)(2,1)S(1)}, u32[]{:S(2)}, u32[]{:S(2)}) collective-permute-start(bf16[8,128,128]{2,1,0:T(8,128)(2,1)S(1)} %get-tuple-element.73), channel_id=1, source_target_pairs={{0,8},{8,0},{16,24},{24,16},{1,9},{9,1},{17,25},{25,17},{2,10},{10... | collective-permute-start | bytes 786440 | tf_op jit(solution)/shard_map/state0from1/ppermute | solution.py:459
  15.6 1.5 %collective-permute-start.4 = (bf16[8,128,128]{2,1,0:T(8,128)(2,1)S(1)}, bf16[8,128,128]{2,1,0:T(8,128)(2,1)S(1)}, u32[]{:S(2)}, u32[]{:S(2)}) collective-permute-start(bf16[8,128,128]{2,1,0:T(8,128)(2,1)S(1)} %get-tuple-element.74), channel_id=1, source_target_pairs={{0,16},{8,24},{16,0},{24,8},{1,17},{9,25},{17,1},{25,9},{2,18},{10... | collective-permute-start | bytes 786440 | tf_op jit(solution)/shard_map/state0from2/ppermute | solution.py:459
  17.6 2.0 %pack.3 = (bf16[8,128,128]{2,1,0:T(8,128)(2,1)S(1)}, bf16[8,128,128]{2,1,0:T(8,128)(2,1)S(1)}, bf16[8,128,128]{2,1,0:T(8,128)(2,1)S(1)}) custom-call(s32[1]{0:T(128)} %bitcast.6.refs_0_, s32[2]{0:T(128)S(1)} %collective-permute-done.refs_1_, s32[2]{0:T(128)S(1)} %collective-permute-done.1.refs_2_, s32[2]{0:T(128)S(1)} %collective-permute-done.2.refs_3_, ...), custom_call_target="tpu_custom_call" | custom-call | flops 1000 | bytes 1000 | tf_op jit(solution)/shard_map/pack/pallas_call | solution.py:164
  19.6 1.6 %collective-permute-start.6 = (bf16[8,128,128]{2,1,0:T(8,128)(2,1)S(1)}, bf16[8,128,128]{2,1,0:T(8,128)(2,1)S(1)}, u32[]{:S(2)}, u32[]{:S(2)}) collective-permute-start(bf16[8,128,128]{2,1,0:T(8,128)(2,1)S(1)} %get-tuple-element.87), channel_id=1, source_target_pairs={{0,8},{8,0},{16,24},{24,16},{1,9},{9,1},{17,25},{25,17},{2,10},{10... | collective-permute-start | bytes 786440 | tf_op jit(solution)/shard_map/state8from1/ppermute | solution.py:459
  21.2 1.5 %collective-permute-start.7 = (bf16[8,128,128]{2,1,0:T(8,128)(2,1)S(1)}, bf16[8,128,128]{2,1,0:T(8,128)(2,1)S(1)}, u32[]{:S(2)}, u32[]{:S(2)}) collective-permute-start(bf16[8,128,128]{2,1,0:T(8,128)(2,1)S(1)} %get-tuple-element.88), channel_id=1, source_target_pairs={{0,16},{8,24},{16,0},{24,8},{1,17},{9,25},{17,1},{25,9},{2,18},{10... | collective-permute-start | bytes 786440 | tf_op jit(solution)/shard_map/state8from2/ppermute | solution.py:459
  23.3 2.4 %collective-permute-start.8 = (bf16[8,128,128]{2,1,0:T(8,128)(2,1)S(1)}, bf16[8,128,128]{2,1,0:T(8,128)(2,1)S(1)}, u32[]{:S(2)}, u32[]{:S(2)}) collective-permute-start(bf16[8,128,128]{2,1,0:T(8,128)(2,1)S(1)} %get-tuple-element.89), channel_id=1, source_target_pairs={{0,24},{8,16},{16,8},{24,0},{1,25},{9,17},{17,9},{25,1},{2,26},{10... | collective-permute-start | bytes 786440 | tf_op jit(solution)/shard_map/state8from3/ppermute | solution.py:459
  25.8 3.5 %collective-permute-done.4.refs_3_ = bf16[8,128,128]{2,1,0:T(8,128)(2,1)S(1)} collective-permute-done((bf16[8,128,128]{2,1,0:T(8,128)(2,1)S(1)}, bf16[8,128,128]{2,1,0:T(8,128)(2,1)S(1)}, u32[]{:S(2)}, u32[]{:S(2)}) %collective-permute-start.4) | collective-permute-done | bytes 262176 | tf_op jit(solution)/shard_map/state0from2/ppermute | solution.py:459
  31.9 4.5 %resume.2 = (bf16[128,1024]{1,0:T(8,128)(2,1)S(1)}, f32[8,128,128]{2,1,0:T(8,128)S(1)}) custom-call(s32[2]{0:T(128)S(1)} %pad_add_fusion.1.refs_0_, f32[1,2,16,128,128]{4,3,2,1,0:T(8,128)} %refs_1_.7, bf16[8,128,128]{2,1,0:T(8,128)(2,1)S(1)} %collective-permute-done.3.refs_2_, bf16[8,128,128]{2,1,0:T(8,128)(2,1)S(1)} %collective-permute-done.4.refs_3_, ...), custom_call_target="tpu_custom_call" | custom-call | flops 1000 | bytes 1000 | tf_op jit(solution)/shard_map/resume/pallas_call | solution.py:282
  36.9 6.8 %prepare.3 = (bf16[8,256,128]{2,1,0:T(8,128)(2,1)S(1)}, bf16[8,128,128]{2,1,0:T(8,128)(2,1)S(1)}, bf16[8,256,128]{2,1,0:T(8,128)(2,1)S(1)}, bf16[4,2048,512]{2,1,0:T(8,128)(2,1)S(1)}, bf16[4,512,2048]{2,1,0:T(8,128)(2,1)S(1)}) custom-call(bf16[128,2048]{1,0:T(8,128)(2,1)} %refs_0_.3, bf16[128,2048]{1,0:T(8,128)(2,1)} %refs_1_.6, ...), custom_call_target="tpu_custom_call" | custom-call | flops 1000 | bytes 1000 | tf_op jit(solution)/shard_map/prepare/pallas_call | solution.py:113
  43.8 5.4 %resume.3 = (bf16[128,1152]{1,0:T(8,128)(2,1)S(1)}, f32[8,128,128]{2,1,0:T(8,128)S(1)}, bf16[4,2048,512]{2,1,0:T(8,128)(2,1)S(1)}) custom-call(s32[2]{0:T(128)S(1)} %pad_add_fusion.1.refs_0_, f32[1,2,16,128,128]{4,3,2,1,0:T(8,128)} %refs_1_.7, bf16[8,128,128]{2,1,0:T(8,128)(2,1)S(1)} %collective-permute-done.6.refs_2_, ...), custom_call_target="tpu_custom_call" | custom-call | flops 1000 | bytes 1000 | tf_op jit(solution)/shard_map/resume/pallas_call | solution.py:282
  49.9 2.5 %collective-permute-start.17 = (bf16[128,1152]{1,0:T(8,128)(2,1)S(1)}, bf16[128,1152]{1,0:T(8,128)(2,1)S(1)}, u32[]{:S(2)}, u32[]{:S(2)}) collective-permute-start(bf16[128,1152]{1,0:T(8,128)(2,1)S(1)} %get-tuple-element.106.refs_2_), channel_id=1, source_target_pairs={{0,4},{1,5},{2,6},{3,7},{4,0},{5,1},{6,2},{7,3},{8,12},{9,13},{10,... | collective-permute-start | bytes 884744 | tf_op jit(solution)/shard_map/rows1chip2/ppermute | solution.py:459
  52.4 1.7 %collective-permute-start.14 = (bf16[128,1152]{1,0:T(8,128)(2,1)S(1)}, bf16[128,1152]{1,0:T(8,128)(2,1)S(1)}, u32[]{:S(2)}, u32[]{:S(2)}) collective-permute-start(bf16[128,1152]{1,0:T(8,128)(2,1)S(1)} %get-tuple-element.106.refs_2_), channel_id=1, source_target_pairs={{0,2},{1,3},{2,0},{3,1},{4,6},{5,7},{6,4},{7,5},{8,10},{9,11},{10,... | collective-permute-start | bytes 884744 | tf_op jit(solution)/shard_map/rows1chip1/ppermute | solution.py:459
  56.3 8.2 %experts.3 = (bf16[1,128,2048]{2,1,0:T(8,128)(2,1)S(1)}, bf16[1,128,2048]{2,1,0:T(8,128)(2,1)S(1)}) custom-call(s32[1]{0:T(128)} %bitcast.11.refs_0_, bf16[128,1024]{1,0:T(8,128)(2,1)S(1)} %get-tuple-element.105.refs_1_, bf16[128,1152]{1,0:T(8,128)(2,1)S(1)} %get-tuple-element.106.refs_2_, bf16[128,1024]{1,0:T(8,128)(2,1)S(1)} %collective-permute-done.9.refs_3_, ...), custom_call_target="tpu_custom_call" | custom-call | flops 1000 | bytes 1000 | tf_op jit(solution)/shard_map/experts/pallas_call | solution.py:419
  65.3 3.0 %collective-permute-done.14.refs_2_ = bf16[128,1152]{1,0:T(8,128)(2,1)S(1)} collective-permute-done((bf16[128,1152]{1,0:T(8,128)(2,1)S(1)}, bf16[128,1152]{1,0:T(8,128)(2,1)S(1)}, u32[]{:S(2)}, u32[]{:S(2)}) %collective-permute-start.14) | collective-permute-done | bytes 294944 | tf_op jit(solution)/shard_map/rows1chip1/ppermute | solution.py:459
  68.3 4.7 %collective-permute-done.13.refs_1_ = bf16[128,1024]{1,0:T(8,128)(2,1)S(1)} collective-permute-done((bf16[128,1024]{1,0:T(8,128)(2,1)S(1)}, bf16[128,1024]{1,0:T(8,128)(2,1)S(1)}, u32[]{:S(2)}, u32[]{:S(2)}) %collective-permute-start.13) | collective-permute-done | bytes 262176 | tf_op jit(solution)/shard_map/rows0chip1/ppermute | solution.py:459
  73.0 1.6 %collective-permute-start.25 = (bf16[128,1152]{1,0:T(8,128)(2,1)S(1)}, bf16[128,1152]{1,0:T(8,128)(2,1)S(1)}, u32[]{:S(2)}, u32[]{:S(2)}) collective-permute-start(bf16[128,1152]{1,0:T(8,128)(2,1)S(1)} %collective-permute-done.17.refs_6_), channel_id=1, source_target_pairs={{0,2},{1,3},{2,0},{3,1},{4,6},{5,7},{6,4},{7,5},{8,10},{9,11},{10,... | collective-permute-start | bytes 884744 | tf_op jit(solution)/shard_map/rows1chip3/ppermute | solution.py:459
  75.1 13.7 %experts.4 = (bf16[2,128,2048]{2,1,0:T(8,128)(2,1)S(1)}, bf16[2,128,1024]{2,1,0:T(8,128)(2,1)S(1)}, bf16[2,128,1024]{2,1,0:T(8,128)(2,1)S(1)}) custom-call(s32[1]{0:T(128)} %bitcast.11.refs_0_, bf16[128,1024]{1,0:T(8,128)(2,1)S(1)} %collective-permute-done.13.refs_1_, bf16[128,1152]{1,0:T(8,128)(2,1)S(1)} %collective-permute-done.14.refs_2_, ...), custom_call_target="tpu_custom_call" | custom-call | flops 1000 | bytes 1000 | tf_op jit(solution)/shard_map/experts/pallas_call | solution.py:419
  92.0 1.7 %collective-permute-start.22 = (bf16[128,2048]{1,0:T(8,128)(2,1)S(1)}, bf16[128,2048]{1,0:T(8,128)(2,1)S(1)}, u32[]{:S(2)}, u32[]{:S(2)}) collective-permute-start(bf16[128,2048]{1,0:T(8,128)(2,1)S(1)} %pad_maximum_fusion.1), channel_id=1, source_target_pairs={{0,2},{1,3},{2,0},{3,1},{4,6},{5,7},{6,4},{7,5},{8,10},{9,11},{10,... | collective-permute-start | bytes 1572872 | tf_op jit(solution)/shard_map/sums1chip/ppermute | solution.py:459
  93.8 8.2 %experts.5 = (bf16[1,128,2048]{2,1,0:T(8,128)(2,1)S(1)}, bf16[1,128,512]{2,1,0:T(8,128)(2,1)S(1)}, bf16[1,128,512]{2,1,0:T(8,128)(2,1)S(1)}, bf16[1,128,512]{2,1,0:T(8,128)(2,1)S(1)}, bf16[1,128,512]{2,1,0:T(8,128)(2,1)S(1)}) custom-call(s32[1]{0:T(128)} %bitcast.11.refs_0_, bf16[128,1024]{1,0:T(8,128)(2,1)S(1)} %collective-permute-done.24.refs_1_, ...), custom_call_target="tpu_custom_call" | custom-call | flops 1000 | bytes 1000 | tf_op jit(solution)/shard_map/experts/pallas_call | solution.py:419
  105.1 1.9 %collective-permute-start.29 = (bf16[128,512]{1,0:T(8,128)(2,1)S(1)}, bf16[128,512]{1,0:T(8,128)(2,1)S(1)}, u32[]{:S(2)}, u32[]{:S(2)}) collective-permute-start(bf16[128,512]{1,0:T(8,128)(2,1)S(1)} %get-tuple-element.129), channel_id=1, source_target_pairs={{0,6},{1,7},{2,4},{3,5},{4,2},{5,3},{6,0},{7,1},{8,14},{9,15},{10,... | collective-permute-start | bytes 393224 | tf_op jit(solution)/shard_map/sums3chip/ppermute | solution.py:459
  107.2 6.7 %collective-permute-done.22 = bf16[128,2048]{1,0:T(8,128)(2,1)S(1)} collective-permute-done((bf16[128,2048]{1,0:T(8,128)(2,1)S(1)}, bf16[128,2048]{1,0:T(8,128)(2,1)S(1)}, u32[]{:S(2)}, u32[]{:S(2)}) %collective-permute-start.22) | collective-permute-done | bytes 524320 | tf_op jit(solution)/shard_map/sums1chip/ppermute | solution.py:459
  113.9 8.3 %collective-permute-done.23 = bf16[128,2048]{1,0:T(8,128)(2,1)S(1)} collective-permute-done((bf16[128,2048]{1,0:T(8,128)(2,1)S(1)}, bf16[128,2048]{1,0:T(8,128)(2,1)S(1)}, u32[]{:S(2)}, u32[]{:S(2)}) %collective-permute-start.23) | collective-permute-done | bytes 524320 | tf_op jit(solution)/shard_map/sums2chip/ppermute | solution.py:459
  122.2 2.7 %collective-permute-start.34 = (bf16[128,512]{1,0:T(8,128)(2,1)S(1)}, bf16[128,512]{1,0:T(8,128)(2,1)S(1)}, u32[]{:S(2)}, u32[]{:S(2)}) collective-permute-start(bf16[128,512]{1,0:T(8,128)(2,1)S(1)} %get-tuple-element.124), channel_id=1, source_target_pairs={{0,6},{1,7},{2,4},{3,5},{4,2},{5,3},{6,0},{7,1},{8,14},{9,15},{10,... | collective-permute-start | bytes 393224 | tf_op jit(solution)/shard_map/sums3chip/ppermute | solution.py:459
  124.9 8.8 %collective-permute-done.29 = bf16[128,512]{1,0:T(8,128)(2,1)S(1)} collective-permute-done((bf16[128,512]{1,0:T(8,128)(2,1)S(1)}, bf16[128,512]{1,0:T(8,128)(2,1)S(1)}, u32[]{:S(2)}, u32[]{:S(2)}) %collective-permute-start.29) | collective-permute-done | bytes 131104 | tf_op jit(solution)/shard_map/sums3chip/ppermute | solution.py:459
  133.7 2.8 %collective-permute-done.31 = bf16[128,512]{1,0:T(8,128)(2,1)S(1)} collective-permute-done((bf16[128,512]{1,0:T(8,128)(2,1)S(1)}, bf16[128,512]{1,0:T(8,128)(2,1)S(1)}, u32[]{:S(2)}, u32[]{:S(2)}) %collective-permute-start.31) | collective-permute-done | bytes 131104 | tf_op jit(solution)/shard_map/sums3chip/ppermute | solution.py:459
  136.5 2.8 %collective-permute-done.34 = bf16[128,512]{1,0:T(8,128)(2,1)S(1)} collective-permute-done((bf16[128,512]{1,0:T(8,128)(2,1)S(1)}, bf16[128,512]{1,0:T(8,128)(2,1)S(1)}, u32[]{:S(2)}, u32[]{:S(2)}) %collective-permute-start.34) | collective-permute-done | bytes 131104 | tf_op jit(solution)/shard_map/sums3chip/ppermute | solution.py:459
  139.3 1.7 %collective-permute-done.35 = bf16[128,512]{1,0:T(8,128)(2,1)S(1)} collective-permute-done((bf16[128,512]{1,0:T(8,128)(2,1)S(1)}, bf16[128,512]{1,0:T(8,128)(2,1)S(1)}, u32[]{:S(2)}, u32[]{:S(2)}) %collective-permute-start.35) | collective-permute-done | bytes 131104 | tf_op jit(solution)/shard_map/sums3chip/ppermute | solution.py:459
  141.1 1.2 fusion.2
  (76 shorter events, 16.3 us)
Async XLA Ops:
  2.0 9.9 %collective-permute-start = (s32[2]{0:T(128)S(1)}, s32[2]{0:T(128)S(1)}, u32[]{:S(2)}, u32[]{:S(2)}) collective-permute-start(s32[2]{0:T(128)S(1)} %pad_add_fusion), channel_id=1, source_target_pairs={{0,8},{8,0},{16,24},{24,16},{1,9},{9,1},{17,25},{25,17},{2,10},{10... | collective-permute-start | bytes 32 | tf_op jit(solution)/shard_map/hits1/ppermute | solution.py:459
  3.5 8.4 %collective-permute-start.1 = (s32[2]{0:T(128)S(1)}, s32[2]{0:T(128)S(1)}, u32[]{:S(2)}, u32[]{:S(2)}) collective-permute-start(s32[2]{0:T(128)S(1)} %pad_add_fusion), channel_id=1, source_target_pairs={{0,16},{8,24},{16,0},{24,8},{1,17},{9,25},{17,1},{25,9},{2,18},{10... | collective-permute-start | bytes 32 | tf_op jit(solution)/shard_map/hits2/ppermute | solution.py:459
  5.0 6.9 %collective-permute-start.2 = (s32[2]{0:T(128)S(1)}, s32[2]{0:T(128)S(1)}, u32[]{:S(2)}, u32[]{:S(2)}) collective-permute-start(s32[2]{0:T(128)S(1)} %pad_add_fusion), channel_id=1, source_target_pairs={{0,24},{8,16},{16,8},{24,0},{1,25},{9,17},{17,9},{25,1},{2,26},{10... | collective-permute-start | bytes 32 | tf_op jit(solution)/shard_map/hits3/ppermute | solution.py:459
  14.0 9.3 %collective-permute-start.3 = (bf16[8,128,128]{2,1,0:T(8,128)(2,1)S(1)}, bf16[8,128,128]{2,1,0:T(8,128)(2,1)S(1)}, u32[]{:S(2)}, u32[]{:S(2)}) collective-permute-start(bf16[8,128,128]{2,1,0:T(8,128)(2,1)S(1)} %get-tuple-element.73), channel_id=1, source_target_pairs={{0,8},{8,0},{16,24},{24,16},{1,9},{9,1},{17,25},{25,17},{2,10},{10... | collective-permute-start | bytes 786440 | tf_op jit(solution)/shard_map/state0from1/ppermute | solution.py:459
  15.6 13.7 %collective-permute-start.4 = (bf16[8,128,128]{2,1,0:T(8,128)(2,1)S(1)}, bf16[8,128,128]{2,1,0:T(8,128)(2,1)S(1)}, u32[]{:S(2)}, u32[]{:S(2)}) collective-permute-start(bf16[8,128,128]{2,1,0:T(8,128)(2,1)S(1)} %get-tuple-element.74), channel_id=1, source_target_pairs={{0,16},{8,24},{16,0},{24,8},{1,17},{9,25},{17,1},{25,9},{2,18},{10... | collective-permute-start | bytes 786440 | tf_op jit(solution)/shard_map/state0from2/ppermute | solution.py:459
  17.1 12.8 %collective-permute-start.5 = (bf16[8,128,128]{2,1,0:T(8,128)(2,1)S(1)}, bf16[8,128,128]{2,1,0:T(8,128)(2,1)S(1)}, u32[]{:S(2)}, u32[]{:S(2)}) collective-permute-start(bf16[8,128,128]{2,1,0:T(8,128)(2,1)S(1)} %get-tuple-element.75), channel_id=1, source_target_pairs={{0,24},{8,16},{16,8},{24,0},{1,25},{9,17},{17,9},{25,1},{2,26},{10... | collective-permute-start | bytes 786440 | tf_op jit(solution)/shard_map/state0from3/ppermute | solution.py:459
  19.6 24.2 %collective-permute-start.6 = (bf16[8,128,128]{2,1,0:T(8,128)(2,1)S(1)}, bf16[8,128,128]{2,1,0:T(8,128)(2,1)S(1)}, u32[]{:S(2)}, u32[]{:S(2)}) collective-permute-start(bf16[8,128,128]{2,1,0:T(8,128)(2,1)S(1)} %get-tuple-element.87), channel_id=1, source_target_pairs={{0,8},{8,0},{16,24},{24,16},{1,9},{9,1},{17,25},{25,17},{2,10},{10... | collective-permute-start | bytes 786440 | tf_op jit(solution)/shard_map/state8from1/ppermute | solution.py:459
  21.2 22.6 %collective-permute-start.7 = (bf16[8,128,128]{2,1,0:T(8,128)(2,1)S(1)}, bf16[8,128,128]{2,1,0:T(8,128)(2,1)S(1)}, u32[]{:S(2)}, u32[]{:S(2)}) collective-permute-start(bf16[8,128,128]{2,1,0:T(8,128)(2,1)S(1)} %get-tuple-element.88), channel_id=1, source_target_pairs={{0,16},{8,24},{16,0},{24,8},{1,17},{9,25},{17,1},{25,9},{2,18},{10... | collective-permute-start | bytes 786440 | tf_op jit(solution)/shard_map/state8from2/ppermute | solution.py:459
  23.3 20.5 %collective-permute-start.8 = (bf16[8,128,128]{2,1,0:T(8,128)(2,1)S(1)}, bf16[8,128,128]{2,1,0:T(8,128)(2,1)S(1)}, u32[]{:S(2)}, u32[]{:S(2)}) collective-permute-start(bf16[8,128,128]{2,1,0:T(8,128)(2,1)S(1)} %get-tuple-element.89), channel_id=1, source_target_pairs={{0,24},{8,16},{16,8},{24,0},{1,25},{9,17},{17,9},{25,1},{2,26},{10... | collective-permute-start | bytes 786440 | tf_op jit(solution)/shard_map/state8from3/ppermute | solution.py:459
  36.4 18.5 %collective-permute-start.11 = (bf16[128,1024]{1,0:T(8,128)(2,1)S(1)}, bf16[128,1024]{1,0:T(8,128)(2,1)S(1)}, u32[]{:S(2)}, u32[]{:S(2)}) collective-permute-start(bf16[128,1024]{1,0:T(8,128)(2,1)S(1)} %get-tuple-element.105.refs_1_), channel_id=1, source_target_pairs={{0,4},{1,5},{2,6},{3,7},{4,0},{5,1},{6,2},{7,3},{8,12},{9,13},{10,... | collective-permute-start | bytes 786440 | tf_op jit(solution)/shard_map/rows0chip2/ppermute | solution.py:459
  49.3 7.0 %collective-permute-start.10 = (bf16[128,1152]{1,0:T(8,128)(2,1)S(1)}, bf16[128,1152]{1,0:T(8,128)(2,1)S(1)}, u32[]{:S(2)}, u32[]{:S(2)}) collective-permute-start(bf16[128,1152]{1,0:T(8,128)(2,1)S(1)} %get-tuple-element.106.refs_2_), channel_id=1, source_target_pairs={{0,1},{1,0},{2,3},{3,2},{4,5},{5,4},{6,7},{7,6},{8,9},{9,8},{10,11... | collective-permute-start | bytes 884744 | tf_op jit(solution)/shard_map/rows1pair0/ppermute | solution.py:459
  49.4 6.9 %collective-permute-start.9 = (bf16[128,1024]{1,0:T(8,128)(2,1)S(1)}, bf16[128,1024]{1,0:T(8,128)(2,1)S(1)}, u32[]{:S(2)}, u32[]{:S(2)}) collective-permute-start(bf16[128,1024]{1,0:T(8,128)(2,1)S(1)} %get-tuple-element.105.refs_1_), channel_id=1, source_target_pairs={{0,1},{1,0},{2,3},{3,2},{4,5},{5,4},{6,7},{7,6},{8,9},{9,8},{10,11... | collective-permute-start | bytes 786440 | tf_op jit(solution)/shard_map/rows0pair0/ppermute | solution.py:459
  49.9 15.4 %collective-permute-start.17 = (bf16[128,1152]{1,0:T(8,128)(2,1)S(1)}, bf16[128,1152]{1,0:T(8,128)(2,1)S(1)}, u32[]{:S(2)}, u32[]{:S(2)}) collective-permute-start(bf16[128,1152]{1,0:T(8,128)(2,1)S(1)} %get-tuple-element.106.refs_2_), channel_id=1, source_target_pairs={{0,4},{1,5},{2,6},{3,7},{4,0},{5,1},{6,2},{7,3},{8,12},{9,13},{10,... | collective-permute-start | bytes 884744 | tf_op jit(solution)/shard_map/rows1chip2/ppermute | solution.py:459
  52.4 15.9 %collective-permute-start.14 = (bf16[128,1152]{1,0:T(8,128)(2,1)S(1)}, bf16[128,1152]{1,0:T(8,128)(2,1)S(1)}, u32[]{:S(2)}, u32[]{:S(2)}) collective-permute-start(bf16[128,1152]{1,0:T(8,128)(2,1)S(1)} %get-tuple-element.106.refs_2_), channel_id=1, source_target_pairs={{0,2},{1,3},{2,0},{3,1},{4,6},{5,7},{6,4},{7,5},{8,10},{9,11},{10,... | collective-permute-start | bytes 884744 | tf_op jit(solution)/shard_map/rows1chip1/ppermute | solution.py:459
  54.9 18.1 %collective-permute-start.13 = (bf16[128,1024]{1,0:T(8,128)(2,1)S(1)}, bf16[128,1024]{1,0:T(8,128)(2,1)S(1)}, u32[]{:S(2)}, u32[]{:S(2)}) collective-permute-start(bf16[128,1024]{1,0:T(8,128)(2,1)S(1)} %get-tuple-element.105.refs_1_), channel_id=1, source_target_pairs={{0,2},{1,3},{2,0},{3,1},{4,6},{5,7},{6,4},{7,5},{8,10},{9,11},{10,... | collective-permute-start | bytes 786440 | tf_op jit(solution)/shard_map/rows0chip1/ppermute | solution.py:459
  64.5 10.1 %collective-permute-start.18 = (bf16[128,1024]{1,0:T(8,128)(2,1)S(1)}, bf16[128,1024]{1,0:T(8,128)(2,1)S(1)}, u32[]{:S(2)}, u32[]{:S(2)}) collective-permute-start(bf16[128,1024]{1,0:T(8,128)(2,1)S(1)} %collective-permute-done.11.refs_5_), channel_id=1, source_target_pairs={{0,1},{1,0},{2,3},{3,2},{4,5},{5,4},{6,7},{7,6},{8,9},{9,8},{10,11... | collective-permute-start | bytes 786440 | tf_op jit(solution)/shard_map/rows0pair2/ppermute | solution.py:459
  65.3 9.7 %collective-permute-start.19 = (bf16[128,1152]{1,0:T(8,128)(2,1)S(1)}, bf16[128,1152]{1,0:T(8,128)(2,1)S(1)}, u32[]{:S(2)}, u32[]{:S(2)}) collective-permute-start(bf16[128,1152]{1,0:T(8,128)(2,1)S(1)} %collective-permute-done.17.refs_6_), channel_id=1, source_target_pairs={{0,1},{1,0},{2,3},{3,2},{4,5},{5,4},{6,7},{7,6},{8,9},{9,8},{10,11... | collective-permute-start | bytes 884744 | tf_op jit(solution)/shard_map/rows1pair2/ppermute | solution.py:459
  68.3 6.8 %collective-permute-start.16 = (bf16[128,1152]{1,0:T(8,128)(2,1)S(1)}, bf16[128,1152]{1,0:T(8,128)(2,1)S(1)}, u32[]{:S(2)}, u32[]{:S(2)}) collective-permute-start(bf16[128,1152]{1,0:T(8,128)(2,1)S(1)} %collective-permute-done.14.refs_2_), channel_id=1, source_target_pairs={{0,1},{1,0},{2,3},{3,2},{4,5},{5,4},{6,7},{7,6},{8,9},{9,8},{10,11... | collective-permute-start | bytes 884744 | tf_op jit(solution)/shard_map/rows1pair1/ppermute | solution.py:459
  73.0 2.0 %collective-permute-start.15 = (bf16[128,1024]{1,0:T(8,128)(2,1)S(1)}, bf16[128,1024]{1,0:T(8,128)(2,1)S(1)}, u32[]{:S(2)}, u32[]{:S(2)}) collective-permute-start(bf16[128,1024]{1,0:T(8,128)(2,1)S(1)} %collective-permute-done.13.refs_1_), channel_id=1, source_target_pairs={{0,1},{1,0},{2,3},{3,2},{4,5},{5,4},{6,7},{7,6},{8,9},{9,8},{10,11... | collective-permute-start | bytes 786440 | tf_op jit(solution)/shard_map/rows0pair1/ppermute | solution.py:459
  73.0 16.3 %collective-permute-start.25 = (bf16[128,1152]{1,0:T(8,128)(2,1)S(1)}, bf16[128,1152]{1,0:T(8,128)(2,1)S(1)}, u32[]{:S(2)}, u32[]{:S(2)}) collective-permute-start(bf16[128,1152]{1,0:T(8,128)(2,1)S(1)} %collective-permute-done.17.refs_6_), channel_id=1, source_target_pairs={{0,2},{1,3},{2,0},{3,1},{4,6},{5,7},{6,4},{7,5},{8,10},{9,11},{10,... | collective-permute-start | bytes 884744 | tf_op jit(solution)/shard_map/rows1chip3/ppermute | solution.py:459
  74.6 14.8 %collective-permute-start.24 = (bf16[128,1024]{1,0:T(8,128)(2,1)S(1)}, bf16[128,1024]{1,0:T(8,128)(2,1)S(1)}, u32[]{:S(2)}, u32[]{:S(2)}) collective-permute-start(bf16[128,1024]{1,0:T(8,128)(2,1)S(1)} %collective-permute-done.11.refs_5_), channel_id=1, source_target_pairs={{0,2},{1,3},{2,0},{3,1},{4,6},{5,7},{6,4},{7,5},{8,10},{9,11},{10,... | collective-permute-start | bytes 786440 | tf_op jit(solution)/shard_map/rows0chip3/ppermute | solution.py:459
  88.8 2.0 %collective-permute-start.20 = (bf16[2,128,1024]{2,1,0:T(8,128)(2,1)S(1)}, bf16[2,128,1024]{2,1,0:T(8,128)(2,1)S(1)}, u32[]{:S(2)}, u32[]{:S(2)}) collective-permute-start(bf16[2,128,1024]{2,1,0:T(8,128)(2,1)S(1)} %get-tuple-element.113), channel_id=1, source_target_pairs={{0,1},{1,0},{2,3},{3,2},{4,5},{5,4},{6,7},{7,6},{8,9},{9,8},{10,11... | collective-permute-start | bytes 1572872 | tf_op jit(solution)/shard_map/sums1pair/ppermute | solution.py:459
  88.9 2.6 %collective-permute-start.21 = (bf16[2,128,1024]{2,1,0:T(8,128)(2,1)S(1)}, bf16[2,128,1024]{2,1,0:T(8,128)(2,1)S(1)}, u32[]{:S(2)}, u32[]{:S(2)}) collective-permute-start(bf16[2,128,1024]{2,1,0:T(8,128)(2,1)S(1)} %get-tuple-element.114), channel_id=1, source_target_pairs={{0,1},{1,0},{2,3},{3,2},{4,5},{5,4},{6,7},{7,6},{8,9},{9,8},{10,11... | collective-permute-start | bytes 1572872 | tf_op jit(solution)/shard_map/sums1pair/ppermute | solution.py:459
  89.4 4.4 %collective-permute-start.27 = (bf16[128,1152]{1,0:T(8,128)(2,1)S(1)}, bf16[128,1152]{1,0:T(8,128)(2,1)S(1)}, u32[]{:S(2)}, u32[]{:S(2)}) collective-permute-start(bf16[128,1152]{1,0:T(8,128)(2,1)S(1)} %collective-permute-done.25.refs_2_), channel_id=1, source_target_pairs={{0,1},{1,0},{2,3},{3,2},{4,5},{5,4},{6,7},{7,6},{8,9},{9,8},{10,11... | collective-permute-start | bytes 884744 | tf_op jit(solution)/shard_map/rows1pair3/ppermute | solution.py:459
  89.5 4.3 %collective-permute-start.26 = (bf16[128,1024]{1,0:T(8,128)(2,1)S(1)}, bf16[128,1024]{1,0:T(8,128)(2,1)S(1)}, u32[]{:S(2)}, u32[]{:S(2)}) collective-permute-start(bf16[128,1024]{1,0:T(8,128)(2,1)S(1)} %collective-permute-done.24.refs_1_), channel_id=1, source_target_pairs={{0,1},{1,0},{2,3},{3,2},{4,5},{5,4},{6,7},{7,6},{8,9},{9,8},{10,11... | collective-permute-start | bytes 786440 | tf_op jit(solution)/shard_map/rows0pair3/ppermute | solution.py:459
  92.0 21.9 %collective-permute-start.22 = (bf16[128,2048]{1,0:T(8,128)(2,1)S(1)}, bf16[128,2048]{1,0:T(8,128)(2,1)S(1)}, u32[]{:S(2)}, u32[]{:S(2)}) collective-permute-start(bf16[128,2048]{1,0:T(8,128)(2,1)S(1)} %pad_maximum_fusion.1), channel_id=1, source_target_pairs={{0,2},{1,3},{2,0},{3,1},{4,6},{5,7},{6,4},{7,5},{8,10},{9,11},{10,... | collective-permute-start | bytes 1572872 | tf_op jit(solution)/shard_map/sums1chip/ppermute | solution.py:459
  93.7 28.5 %collective-permute-start.23 = (bf16[128,2048]{1,0:T(8,128)(2,1)S(1)}, bf16[128,2048]{1,0:T(8,128)(2,1)S(1)}, u32[]{:S(2)}, u32[]{:S(2)}) collective-permute-start(bf16[128,2048]{1,0:T(8,128)(2,1)S(1)} %pad_maximum_fusion.2), channel_id=1, source_target_pairs={{0,4},{1,5},{2,6},{3,7},{4,0},{5,1},{6,2},{7,3},{8,12},{9,13},{10,... | collective-permute-start | bytes 1572872 | tf_op jit(solution)/shard_map/sums2chip/ppermute | solution.py:459
  102.6 22.3 %collective-permute-start.12 = (bf16[1,128,2048]{2,1,0:T(8,128)(2,1)S(1)}, bf16[1,128,2048]{2,1,0:T(8,128)(2,1)S(1)}, u32[]{:S(2)}, u32[]{:S(2)}) collective-permute-start(bf16[1,128,2048]{2,1,0:T(8,128)(2,1)S(1)} %get-tuple-element.104), channel_id=1, source_target_pairs={{0,1},{1,0},{2,3},{3,2},{4,5},{5,4},{6,7},{7,6},{8,9},{9,8},{10,11... | collective-permute-start | bytes 1572872 | tf_op jit(solution)/shard_map/sums0pair/ppermute | solution.py:459
  105.1 28.6 %collective-permute-start.29 = (bf16[128,512]{1,0:T(8,128)(2,1)S(1)}, bf16[128,512]{1,0:T(8,128)(2,1)S(1)}, u32[]{:S(2)}, u32[]{:S(2)}) collective-permute-start(bf16[128,512]{1,0:T(8,128)(2,1)S(1)} %get-tuple-element.129), channel_id=1, source_target_pairs={{0,6},{1,7},{2,4},{3,5},{4,2},{5,3},{6,0},{7,1},{8,14},{9,15},{10,... | collective-permute-start | bytes 393224 | tf_op jit(solution)/shard_map/sums3chip/ppermute | solution.py:459
  107.0 29.5 %collective-permute-start.31 = (bf16[128,512]{1,0:T(8,128)(2,1)S(1)}, bf16[128,512]{1,0:T(8,128)(2,1)S(1)}, u32[]{:S(2)}, u32[]{:S(2)}) collective-permute-start(bf16[128,512]{1,0:T(8,128)(2,1)S(1)} %get-tuple-element.132), channel_id=1, source_target_pairs={{0,6},{1,7},{2,4},{3,5},{4,2},{5,3},{6,0},{7,1},{8,14},{9,15},{10,... | collective-permute-start | bytes 393224 | tf_op jit(solution)/shard_map/sums3chip/ppermute | solution.py:459
  122.2 17.2 %collective-permute-start.34 = (bf16[128,512]{1,0:T(8,128)(2,1)S(1)}, bf16[128,512]{1,0:T(8,128)(2,1)S(1)}, u32[]{:S(2)}, u32[]{:S(2)}) collective-permute-start(bf16[128,512]{1,0:T(8,128)(2,1)S(1)} %get-tuple-element.124), channel_id=1, source_target_pairs={{0,6},{1,7},{2,4},{3,5},{4,2},{5,3},{6,0},{7,1},{8,14},{9,15},{10,... | collective-permute-start | bytes 393224 | tf_op jit(solution)/shard_map/sums3chip/ppermute | solution.py:459
  124.8 16.2 %collective-permute-start.35 = (bf16[128,512]{1,0:T(8,128)(2,1)S(1)}, bf16[128,512]{1,0:T(8,128)(2,1)S(1)}, u32[]{:S(2)}, u32[]{:S(2)}) collective-permute-start(bf16[128,512]{1,0:T(8,128)(2,1)S(1)} %get-tuple-element.125), channel_id=1, source_target_pairs={{0,6},{1,7},{2,4},{3,5},{4,2},{5,3},{6,0},{7,1},{8,14},{9,15},{10,... | collective-permute-start | bytes 393224 | tf_op jit(solution)/shard_map/sums3chip/ppermute | solution.py:459
  (11 other events, 40.8 us)

commit v5 on v4

--- a/solution.py
+++ b/solution.py
@@ -480,9 +480,12 @@
 ):
     rows, d = queries.shape
     head_count = log_decay.shape[0]
-    queries, keys_in, values_in, out_gate, residual_in, state_cache = (
+    queries, keys_in, values_in, out_gate, residual_in, state_cache, ids_t, weight_t, head_gain = (
         pltpu.with_memory_space_constraint(x, pltpu.HBM)
-        for x in (queries, keys_in, values_in, out_gate, residual_in, state_cache)
+        for x in (
+            queries, keys_in, values_in, out_gate, residual_in, state_cache, expert_ids.T,
+            gate_weight.T, head_gain[None],
+        )
     )
     holders = lax.axis_size("dp")
     group = lax.axis_size("expert")
@@ -507,8 +510,7 @@
 
     wish = jnp.concatenate([hit_holder, hit_slot])
     asked = [swap(wish, "dp", j, f"hits{j}") for j in range(1, holders)]
-    *ready, held = prepare(queries, keys_in, lb, lbt, 0, chunks[0], ())
-    asked[0], lb, lbt, pick, *ready = after(asked[0], lb, lbt, pick, *ready)
+    asked[0], lb, lbt, pick = after(asked[0], lb, lbt, pick)
     got = []
     for first, heads in zip(starts, chunks):
         pieces = pack(own_dp[None], asked, state_cache, first, heads)
@@ -518,21 +520,20 @@
         )
 
     lb = after(lb, asked[0])[0]
-    mixed, states = [], []
+    mixed, states, held = [], [], []
+    carry = {("prepare", 1): (w_up, w_down), ("resume", 1): (w_gate,)}
     for g, (first, heads) in enumerate(zip(starts, chunks)):
         last = g == len(chunks) - 1
-        if g:
-            more = (w_up, w_down) if g == 1 else ()
-            *ready, new = prepare(queries, keys_in, lb, lbt, first, heads, more)
-            held = held + new
+        *ready, new = prepare(queries, keys_in, lb, lbt, first, heads, carry.pop(("prepare", g), ()))
+        held += new
         kq, t, mk = ready
-        more = (w_gate,) if g == 1 else ()
+        more = carry.pop(("resume", g), ())
         m, s, new = resume(
             pick, state_cache, got[g], kq, t, mk, values_in, lb, lbt, out_gate, residual_in,
-            head_gain[None], expert_ids.T, gate_weight.T, first, heads, all_experts if last else 0,
+            head_gain, ids_t, weight_t, first, heads, all_experts if last else 0,
             more,
         )
-        held = new + held
+        held += new
         pick, lb = after(pick, lb, m)[:2]
         mixed.append(m)
         states.append(s)
@@ -542,7 +543,7 @@
 
     gain = moe_gain[None]
     first_expert = (own_ep * experts)[None].astype(jnp.int32)
-    weights = held
+    weights = [held[n] for n in (2, 0, 1)]
     if group == 8:
         near = [mixed, [], [], []]
         for c in range(parts):

time: 143 us -> 138 us (0.965)
  starting transfers between devices: 29 us -> 25 us
  local copies, waits for them, and re-layouts: 2.28 us -> 0.22 us
    ppermute x36, starting transfers between devices: 29 us -> 25 us  [swap(): return lax.ppermute(x, axis, [(i, i ^ bits) for i in range(size)])]
    unnamed x14 -> x2, local copies, waits for them, and re-layouts: 2.07 us -> 0.01 us
  transfers between devices with their start and end apart: 36 -> 36, of which waited for: 17 -> 17; matrix products, arithmetic and copies ran while one was open for 2% -> 3% of each run, Pallas kernels for 38% -> 40%
where the time goes in v5:
time: 138 us; the launch traced here: 137 us
  Pallas kernels  56.6 us (41%)
  waiting for transfers between devices  48.5 us (35%)
  starting transfers between devices  25 us (18%)
  other arithmetic  4.55 us (3%)
  between operations  2.2 us (2%)
    ppermute x36, waiting for transfers between devices, swap(): return lax.ppermute(x, axis, [(i, i ^ bits) for i in range(size)])  48.5 us
    pallas_call x3, Pallas kernels, expert_stage(): pl.pallas_call(lambda *refs: expert_kernel(*refs, blocks=blocks, parts=pa...  30.1 us
    ppermute x36, starting transfers between devices, swap(): return lax.ppermute(x, axis, [(i, i ^ bits) for i in range(size)])  25 us
    pallas_call x2, Pallas kernels, prepare(): pl.pallas_call(lambda *refs: prepare_kernel(*refs, carried=len(carry)), g...  12.3 us
    pallas_call x2, Pallas kernels, resume(): pl.pallas_call(lambda *refs: resume_kernel(*refs, peers=len(got), first_h...  10.1 us
    pallas_call x2, Pallas kernels, pack(): pl.pallas_call(lambda *refs: pack_kernel(*refs, peers=peers, first=first)...  4.1 us
  transfers between devices with their start and end apart: 36, of which 17 were waited for; matrix products, arithmetic and copies ran while one was open for 3% of the time, Pallas kernels for 40%

profile of v5, /device:TPU:16, one launch (start us, length us, event | category | flops | bytes accessed | tf_op | source)
XLA Modules:
  0.0 137.1 jit_solution(12628465049032537742)
XLA Ops:
  2.0 1.5 %collective-permute-start = (s32[2]{0:T(128)S(1)}, s32[2]{0:T(128)S(1)}, u32[]{:S(2)}, u32[]{:S(2)}) collective-permute-start(s32[2]{0:T(128)S(1)} %pad_add_fusion), channel_id=1, source_target_pairs={{0,8},{8,0},{16,24},{24,16},{1,9},{9,1},{17,25},{25,17},{2,10},{10... | collective-permute-start | bytes 32 | tf_op jit(solution)/shard_map/hits1/ppermute | solution.py:459
  3.5 1.5 %collective-permute-start.1 = (s32[2]{0:T(128)S(1)}, s32[2]{0:T(128)S(1)}, u32[]{:S(2)}, u32[]{:S(2)}) collective-permute-start(s32[2]{0:T(128)S(1)} %pad_add_fusion), channel_id=1, source_target_pairs={{0,16},{8,24},{16,0},{24,8},{1,17},{9,25},{17,1},{25,9},{2,18},{10... | collective-permute-start | bytes 32 | tf_op jit(solution)/shard_map/hits2/ppermute | solution.py:459
  7.0 2.4 %collective-permute-done.2.refs_3_ = s32[2]{0:T(128)S(1)} collective-permute-done((s32[2]{0:T(128)S(1)}, s32[2]{0:T(128)S(1)}, u32[]{:S(2)}, u32[]{:S(2)}) %collective-permute-start.2) | collective-permute-done | bytes 40 | tf_op jit(solution)/shard_map/hits3/ppermute | solution.py:459
  9.5 2.1 %pack.2 = (bf16[8,128,128]{2,1,0:T(8,128)(2,1)S(1)}, bf16[8,128,128]{2,1,0:T(8,128)(2,1)S(1)}, bf16[8,128,128]{2,1,0:T(8,128)(2,1)S(1)}) custom-call(s32[1]{0:T(128)} %bitcast.6.refs_0_, s32[2]{0:T(128)S(1)} %collective-permute-done.refs_1_, s32[2]{0:T(128)S(1)} %collective-permute-done.1.refs_2_, s32[2]{0:T(128)S(1)} %collective-permute-done.2.refs_3_, ...), custom_call_target="tpu_custom_call" | custom-call | flops 1000 | bytes 1000 | tf_op jit(solution)/shard_map/pack/pallas_call | solution.py:164
  12.6 2.4 %collective-permute-start.5 = (bf16[8,128,128]{2,1,0:T(8,128)(2,1)S(1)}, bf16[8,128,128]{2,1,0:T(8,128)(2,1)S(1)}, u32[]{:S(2)}, u32[]{:S(2)}) collective-permute-start(bf16[8,128,128]{2,1,0:T(8,128)(2,1)S(1)} %get-tuple-element.69), channel_id=1, source_target_pairs={{0,24},{8,16},{16,8},{24,0},{1,25},{9,17},{17,9},{25,1},{2,26},{10... | collective-permute-start | bytes 786440 | tf_op jit(solution)/shard_map/state0from3/ppermute | solution.py:459
  15.1 2.0 %pack.3 = (bf16[8,128,128]{2,1,0:T(8,128)(2,1)S(1)}, bf16[8,128,128]{2,1,0:T(8,128)(2,1)S(1)}, bf16[8,128,128]{2,1,0:T(8,128)(2,1)S(1)}) custom-call(s32[1]{0:T(128)} %bitcast.6.refs_0_, s32[2]{0:T(128)S(1)} %collective-permute-done.refs_1_, s32[2]{0:T(128)S(1)} %collective-permute-done.1.refs_2_, s32[2]{0:T(128)S(1)} %collective-permute-done.2.refs_3_, ...), custom_call_target="tpu_custom_call" | custom-call | flops 1000 | bytes 1000 | tf_op jit(solution)/shard_map/pack/pallas_call | solution.py:164
  18.2 2.6 %collective-permute-done.3.refs_2_ = bf16[8,128,128]{2,1,0:T(8,128)(2,1)S(1)} collective-permute-done((bf16[8,128,128]{2,1,0:T(8,128)(2,1)S(1)}, bf16[8,128,128]{2,1,0:T(8,128)(2,1)S(1)}, u32[]{:S(2)}, u32[]{:S(2)}) %collective-permute-start.3) | collective-permute-done | bytes 262176 | tf_op jit(solution)/shard_map/state0from1/ppermute | solution.py:459
  21.3 5.5 %prepare.2 = (bf16[8,256,128]{2,1,0:T(8,128)(2,1)S(1)}, bf16[8,128,128]{2,1,0:T(8,128)(2,1)S(1)}, bf16[8,256,128]{2,1,0:T(8,128)(2,1)S(1)}) custom-call(bf16[128,2048]{1,0:T(8,128)(2,1)} %refs_0_.3, bf16[128,2048]{1,0:T(8,128)(2,1)} %refs_1_.6, f32[4,8,128]{2,1,0:T(8,128)S(1)} %pad_maximum_fusion.3.refs_2_.refs_9_, f32[4,128,8]{2,1,0:T(8,128)S(1)} %bitcast.59), custom_call_target="tpu_custom_call" | custom-call | flops 1000 | bytes 1000 | tf_op jit(solution)/shard_map/prepare/pallas_call | solution.py:113
  26.8 4.6 %resume.2 = (bf16[128,1024]{1,0:T(8,128)(2,1)S(1)}, f32[8,128,128]{2,1,0:T(8,128)S(1)}) custom-call(s32[2]{0:T(128)S(1)} %pad_add_fusion.1.refs_0_, f32[1,2,16,128,128]{4,3,2,1,0:T(8,128)} %refs_1_.7, bf16[8,128,128]{2,1,0:T(8,128)(2,1)S(1)} %collective-permute-done.3.refs_2_, bf16[8,128,128]{2,1,0:T(8,128)(2,1)S(1)} %collective-permute-done.4.refs_3_, ...), custom_call_target="tpu_custom_call" | custom-call | flops 1000 | bytes 1000 | tf_op jit(solution)/shard_map/resume/pallas_call | solution.py:282
  31.5 6.8 %prepare.3 = (bf16[8,256,128]{2,1,0:T(8,128)(2,1)S(1)}, bf16[8,128,128]{2,1,0:T(8,128)(2,1)S(1)}, bf16[8,256,128]{2,1,0:T(8,128)(2,1)S(1)}, bf16[4,2048,512]{2,1,0:T(8,128)(2,1)S(1)}, bf16[4,512,2048]{2,1,0:T(8,128)(2,1)S(1)}) custom-call(bf16[128,2048]{1,0:T(8,128)(2,1)} %refs_0_.3, bf16[128,2048]{1,0:T(8,128)(2,1)} %refs_1_.6, ...), custom_call_target="tpu_custom_call" | custom-call | flops 1000 | bytes 1000 | tf_op jit(solution)/shard_map/prepare/pallas_call | solution.py:113
  38.4 5.5 %resume.3 = (bf16[128,1152]{1,0:T(8,128)(2,1)S(1)}, f32[8,128,128]{2,1,0:T(8,128)S(1)}, bf16[4,2048,512]{2,1,0:T(8,128)(2,1)S(1)}) custom-call(s32[2]{0:T(128)S(1)} %pad_add_fusion.1.refs_0_, f32[1,2,16,128,128]{4,3,2,1,0:T(8,128)} %refs_1_.7, bf16[8,128,128]{2,1,0:T(8,128)(2,1)S(1)} %collective-permute-done.6.refs_2_, ...), custom_call_target="tpu_custom_call" | custom-call | flops 1000 | bytes 1000 | tf_op jit(solution)/shard_map/resume/pallas_call | solution.py:282
  44.4 2.9 %collective-permute-start.17 = (bf16[128,1152]{1,0:T(8,128)(2,1)S(1)}, bf16[128,1152]{1,0:T(8,128)(2,1)S(1)}, u32[]{:S(2)}, u32[]{:S(2)}) collective-permute-start(bf16[128,1152]{1,0:T(8,128)(2,1)S(1)} %get-tuple-element.100.refs_2_), channel_id=1, source_target_pairs={{0,4},{1,5},{2,6},{3,7},{4,0},{5,1},{6,2},{7,3},{8,12},{9,13},{10,... | collective-permute-start | bytes 884744 | tf_op jit(solution)/shard_map/rows1chip2/ppermute | solution.py:459
  47.3 1.6 %collective-permute-start.14 = (bf16[128,1152]{1,0:T(8,128)(2,1)S(1)}, bf16[128,1152]{1,0:T(8,128)(2,1)S(1)}, u32[]{:S(2)}, u32[]{:S(2)}) collective-permute-start(bf16[128,1152]{1,0:T(8,128)(2,1)S(1)} %get-tuple-element.100.refs_2_), channel_id=1, source_target_pairs={{0,2},{1,3},{2,0},{3,1},{4,6},{5,7},{6,4},{7,5},{8,10},{9,11},{10,... | collective-permute-start | bytes 884744 | tf_op jit(solution)/shard_map/rows1chip1/ppermute | solution.py:459
  48.9 0.8 pad_maximum_fusion
  50.2 1.0 maximum_bitcast_fusion
  51.2 8.2 %experts.3 = (bf16[1,128,2048]{2,1,0:T(8,128)(2,1)S(1)}, bf16[1,128,2048]{2,1,0:T(8,128)(2,1)S(1)}) custom-call(s32[1]{0:T(128)} %bitcast.11.refs_0_, bf16[128,1024]{1,0:T(8,128)(2,1)S(1)} %get-tuple-element.99.refs_1_, bf16[128,1152]{1,0:T(8,128)(2,1)S(1)} %get-tuple-element.100.refs_2_, bf16[128,1024]{1,0:T(8,128)(2,1)S(1)} %collective-permute-done.9.refs_3_, ...), custom_call_target="tpu_custom_call" | custom-call | flops 1000 | bytes 1000 | tf_op jit(solution)/shard_map/experts/pallas_call | solution.py:419
  60.3 2.9 %collective-permute-done.14.refs_2_ = bf16[128,1152]{1,0:T(8,128)(2,1)S(1)} collective-permute-done((bf16[128,1152]{1,0:T(8,128)(2,1)S(1)}, bf16[128,1152]{1,0:T(8,128)(2,1)S(1)}, u32[]{:S(2)}, u32[]{:S(2)}) %collective-permute-start.14) | collective-permute-done | bytes 294944 | tf_op jit(solution)/shard_map/rows1chip1/ppermute | solution.py:459
  63.1 4.7 %collective-permute-done.13.refs_1_ = bf16[128,1024]{1,0:T(8,128)(2,1)S(1)} collective-permute-done((bf16[128,1024]{1,0:T(8,128)(2,1)S(1)}, bf16[128,1024]{1,0:T(8,128)(2,1)S(1)}, u32[]{:S(2)}, u32[]{:S(2)}) %collective-permute-start.13) | collective-permute-done | bytes 262176 | tf_op jit(solution)/shard_map/rows0chip1/ppermute | solution.py:459
  67.9 1.6 %collective-permute-start.25 = (bf16[128,1152]{1,0:T(8,128)(2,1)S(1)}, bf16[128,1152]{1,0:T(8,128)(2,1)S(1)}, u32[]{:S(2)}, u32[]{:S(2)}) collective-permute-start(bf16[128,1152]{1,0:T(8,128)(2,1)S(1)} %collective-permute-done.17.refs_6_), channel_id=1, source_target_pairs={{0,2},{1,3},{2,0},{3,1},{4,6},{5,7},{6,4},{7,5},{8,10},{9,11},{10,... | collective-permute-start | bytes 884744 | tf_op jit(solution)/shard_map/rows1chip3/ppermute | solution.py:459
  69.9 13.7 %experts.4 = (bf16[2,128,2048]{2,1,0:T(8,128)(2,1)S(1)}, bf16[2,128,1024]{2,1,0:T(8,128)(2,1)S(1)}, bf16[2,128,1024]{2,1,0:T(8,128)(2,1)S(1)}) custom-call(s32[1]{0:T(128)} %bitcast.11.refs_0_, bf16[128,1024]{1,0:T(8,128)(2,1)S(1)} %collective-permute-done.13.refs_1_, bf16[128,1152]{1,0:T(8,128)(2,1)S(1)} %collective-permute-done.14.refs_2_, ...), custom_call_target="tpu_custom_call" | custom-call | flops 1000 | bytes 1000 | tf_op jit(solution)/shard_map/experts/pallas_call | solution.py:419
  86.8 1.7 %collective-permute-start.22 = (bf16[128,2048]{1,0:T(8,128)(2,1)S(1)}, bf16[128,2048]{1,0:T(8,128)(2,1)S(1)}, u32[]{:S(2)}, u32[]{:S(2)}) collective-permute-start(bf16[128,2048]{1,0:T(8,128)(2,1)S(1)} %pad_maximum_fusion.1), channel_id=1, source_target_pairs={{0,2},{1,3},{2,0},{3,1},{4,6},{5,7},{6,4},{7,5},{8,10},{9,11},{10,... | collective-permute-start | bytes 1572872 | tf_op jit(solution)/shard_map/sums1chip/ppermute | solution.py:459
  88.6 8.2 %experts.5 = (bf16[1,128,2048]{2,1,0:T(8,128)(2,1)S(1)}, bf16[1,128,512]{2,1,0:T(8,128)(2,1)S(1)}, bf16[1,128,512]{2,1,0:T(8,128)(2,1)S(1)}, bf16[1,128,512]{2,1,0:T(8,128)(2,1)S(1)}, bf16[1,128,512]{2,1,0:T(8,128)(2,1)S(1)}) custom-call(s32[1]{0:T(128)} %bitcast.11.refs_0_, bf16[128,1024]{1,0:T(8,128)(2,1)S(1)} %collective-permute-done.24.refs_1_, ...), custom_call_target="tpu_custom_call" | custom-call | flops 1000 | bytes 1000 | tf_op jit(solution)/shard_map/experts/pallas_call | solution.py:419
  98.7 0.8 collective-permute-done.32
  99.9 1.9 %collective-permute-start.29 = (bf16[128,512]{1,0:T(8,128)(2,1)S(1)}, bf16[128,512]{1,0:T(8,128)(2,1)S(1)}, u32[]{:S(2)}, u32[]{:S(2)}) collective-permute-start(bf16[128,512]{1,0:T(8,128)(2,1)S(1)} %get-tuple-element.123), channel_id=1, source_target_pairs={{0,6},{1,7},{2,4},{3,5},{4,2},{5,3},{6,0},{7,1},{8,14},{9,15},{10,... | collective-permute-start | bytes 393224 | tf_op jit(solution)/shard_map/sums3chip/ppermute | solution.py:459
  102.0 6.7 %collective-permute-done.22 = bf16[128,2048]{1,0:T(8,128)(2,1)S(1)} collective-permute-done((bf16[128,2048]{1,0:T(8,128)(2,1)S(1)}, bf16[128,2048]{1,0:T(8,128)(2,1)S(1)}, u32[]{:S(2)}, u32[]{:S(2)}) %collective-permute-start.22) | collective-permute-done | bytes 524320 | tf_op jit(solution)/shard_map/sums1chip/ppermute | solution.py:459
  108.7 8.3 %collective-permute-done.23 = bf16[128,2048]{1,0:T(8,128)(2,1)S(1)} collective-permute-done((bf16[128,2048]{1,0:T(8,128)(2,1)S(1)}, bf16[128,2048]{1,0:T(8,128)(2,1)S(1)}, u32[]{:S(2)}, u32[]{:S(2)}) %collective-permute-start.23) | collective-permute-done | bytes 524320 | tf_op jit(solution)/shard_map/sums2chip/ppermute | solution.py:459
  117.0 2.7 %collective-permute-start.34 = (bf16[128,512]{1,0:T(8,128)(2,1)S(1)}, bf16[128,512]{1,0:T(8,128)(2,1)S(1)}, u32[]{:S(2)}, u32[]{:S(2)}) collective-permute-start(bf16[128,512]{1,0:T(8,128)(2,1)S(1)} %get-tuple-element.118), channel_id=1, source_target_pairs={{0,6},{1,7},{2,4},{3,5},{4,2},{5,3},{6,0},{7,1},{8,14},{9,15},{10,... | collective-permute-start | bytes 393224 | tf_op jit(solution)/shard_map/sums3chip/ppermute | solution.py:459
  119.7 8.8 %collective-permute-done.29 = bf16[128,512]{1,0:T(8,128)(2,1)S(1)} collective-permute-done((bf16[128,512]{1,0:T(8,128)(2,1)S(1)}, bf16[128,512]{1,0:T(8,128)(2,1)S(1)}, u32[]{:S(2)}, u32[]{:S(2)}) %collective-permute-start.29) | collective-permute-done | bytes 131104 | tf_op jit(solution)/shard_map/sums3chip/ppermute | solution.py:459
  128.5 2.8 %collective-permute-done.31 = bf16[128,512]{1,0:T(8,128)(2,1)S(1)} collective-permute-done((bf16[128,512]{1,0:T(8,128)(2,1)S(1)}, bf16[128,512]{1,0:T(8,128)(2,1)S(1)}, u32[]{:S(2)}, u32[]{:S(2)}) %collective-permute-start.31) | collective-permute-done | bytes 131104 | tf_op jit(solution)/shard_map/sums3chip/ppermute | solution.py:459
  131.3 2.8 %collective-permute-done.34 = bf16[128,512]{1,0:T(8,128)(2,1)S(1)} collective-permute-done((bf16[128,512]{1,0:T(8,128)(2,1)S(1)}, bf16[128,512]{1,0:T(8,128)(2,1)S(1)}, u32[]{:S(2)}, u32[]{:S(2)}) %collective-permute-start.34) | collective-permute-done | bytes 131104 | tf_op jit(solution)/shard_map/sums3chip/ppermute | solution.py:459
  134.1 1.7 %collective-permute-done.35 = bf16[128,512]{1,0:T(8,128)(2,1)S(1)} collective-permute-done((bf16[128,512]{1,0:T(8,128)(2,1)S(1)}, bf16[128,512]{1,0:T(8,128)(2,1)S(1)}, u32[]{:S(2)}, u32[]{:S(2)}) %collective-permute-start.35) | collective-permute-done | bytes 131104 | tf_op jit(solution)/shard_map/sums3chip/ppermute | solution.py:459
  135.9 1.2 fusion.2
  (64 shorter events, 12.8 us)
Async XLA Ops:
  2.0 4.4 %collective-permute-start = (s32[2]{0:T(128)S(1)}, s32[2]{0:T(128)S(1)}, u32[]{:S(2)}, u32[]{:S(2)}) collective-permute-start(s32[2]{0:T(128)S(1)} %pad_add_fusion), channel_id=1, source_target_pairs={{0,8},{8,0},{16,24},{24,16},{1,9},{9,1},{17,25},{25,17},{2,10},{10... | collective-permute-start | bytes 32 | tf_op jit(solution)/shard_map/hits1/ppermute | solution.py:459
  3.5 3.5 %collective-permute-start.1 = (s32[2]{0:T(128)S(1)}, s32[2]{0:T(128)S(1)}, u32[]{:S(2)}, u32[]{:S(2)}) collective-permute-start(s32[2]{0:T(128)S(1)} %pad_add_fusion), channel_id=1, source_target_pairs={{0,16},{8,24},{16,0},{24,8},{1,17},{9,25},{17,1},{25,9},{2,18},{10... | collective-permute-start | bytes 32 | tf_op jit(solution)/shard_map/hits2/ppermute | solution.py:459
  5.0 4.4 %collective-permute-start.2 = (s32[2]{0:T(128)S(1)}, s32[2]{0:T(128)S(1)}, u32[]{:S(2)}, u32[]{:S(2)}) collective-permute-start(s32[2]{0:T(128)S(1)} %pad_add_fusion), channel_id=1, source_target_pairs={{0,24},{8,16},{16,8},{24,0},{1,25},{9,17},{17,9},{25,1},{2,26},{10... | collective-permute-start | bytes 32 | tf_op jit(solution)/shard_map/hits3/ppermute | solution.py:459
  11.5 9.3 %collective-permute-start.3 = (bf16[8,128,128]{2,1,0:T(8,128)(2,1)S(1)}, bf16[8,128,128]{2,1,0:T(8,128)(2,1)S(1)}, u32[]{:S(2)}, u32[]{:S(2)}) collective-permute-start(bf16[8,128,128]{2,1,0:T(8,128)(2,1)S(1)} %get-tuple-element.67), channel_id=1, source_target_pairs={{0,8},{8,0},{16,24},{24,16},{1,9},{9,1},{17,25},{25,17},{2,10},{10... | collective-permute-start | bytes 786440 | tf_op jit(solution)/shard_map/state0from1/ppermute | solution.py:459
  12.1 14.7 %collective-permute-start.4 = (bf16[8,128,128]{2,1,0:T(8,128)(2,1)S(1)}, bf16[8,128,128]{2,1,0:T(8,128)(2,1)S(1)}, u32[]{:S(2)}, u32[]{:S(2)}) collective-permute-start(bf16[8,128,128]{2,1,0:T(8,128)(2,1)S(1)} %get-tuple-element.68), channel_id=1, source_target_pairs={{0,16},{8,24},{16,0},{24,8},{1,17},{9,25},{17,1},{25,9},{2,18},{10... | collective-permute-start | bytes 786440 | tf_op jit(solution)/shard_map/state0from2/ppermute | solution.py:459
  12.6 14.2 %collective-permute-start.5 = (bf16[8,128,128]{2,1,0:T(8,128)(2,1)S(1)}, bf16[8,128,128]{2,1,0:T(8,128)(2,1)S(1)}, u32[]{:S(2)}, u32[]{:S(2)}) collective-permute-start(bf16[8,128,128]{2,1,0:T(8,128)(2,1)S(1)} %get-tuple-element.69), channel_id=1, source_target_pairs={{0,24},{8,16},{16,8},{24,0},{1,25},{9,17},{17,9},{25,1},{2,26},{10... | collective-permute-start | bytes 786440 | tf_op jit(solution)/shard_map/state0from3/ppermute | solution.py:459
  17.1 21.2 %collective-permute-start.6 = (bf16[8,128,128]{2,1,0:T(8,128)(2,1)S(1)}, bf16[8,128,128]{2,1,0:T(8,128)(2,1)S(1)}, u32[]{:S(2)}, u32[]{:S(2)}) collective-permute-start(bf16[8,128,128]{2,1,0:T(8,128)(2,1)S(1)} %get-tuple-element.81), channel_id=1, source_target_pairs={{0,8},{8,0},{16,24},{24,16},{1,9},{9,1},{17,25},{25,17},{2,10},{10... | collective-permute-start | bytes 786440 | tf_op jit(solution)/shard_map/state8from1/ppermute | solution.py:459
  17.7 20.6 %collective-permute-start.7 = (bf16[8,128,128]{2,1,0:T(8,128)(2,1)S(1)}, bf16[8,128,128]{2,1,0:T(8,128)(2,1)S(1)}, u32[]{:S(2)}, u32[]{:S(2)}) collective-permute-start(bf16[8,128,128]{2,1,0:T(8,128)(2,1)S(1)} %get-tuple-element.82), channel_id=1, source_target_pairs={{0,16},{8,24},{16,0},{24,8},{1,17},{9,25},{17,1},{25,9},{2,18},{10... | collective-permute-start | bytes 786440 | tf_op jit(solution)/shard_map/state8from2/ppermute | solution.py:459
  20.8 17.5 %collective-permute-start.8 = (bf16[8,128,128]{2,1,0:T(8,128)(2,1)S(1)}, bf16[8,128,128]{2,1,0:T(8,128)(2,1)S(1)}, u32[]{:S(2)}, u32[]{:S(2)}) collective-permute-start(bf16[8,128,128]{2,1,0:T(8,128)(2,1)S(1)} %get-tuple-element.83), channel_id=1, source_target_pairs={{0,24},{8,16},{16,8},{24,0},{1,25},{9,17},{17,9},{25,1},{2,26},{10... | collective-permute-start | bytes 786440 | tf_op jit(solution)/shard_map/state8from3/ppermute | solution.py:459
  31.4 18.3 %collective-permute-start.11 = (bf16[128,1024]{1,0:T(8,128)(2,1)S(1)}, bf16[128,1024]{1,0:T(8,128)(2,1)S(1)}, u32[]{:S(2)}, u32[]{:S(2)}) collective-permute-start(bf16[128,1024]{1,0:T(8,128)(2,1)S(1)} %get-tuple-element.99.refs_1_), channel_id=1, source_target_pairs={{0,4},{1,5},{2,6},{3,7},{4,0},{5,1},{6,2},{7,3},{8,12},{9,13},{10,... | collective-permute-start | bytes 786440 | tf_op jit(solution)/shard_map/rows0chip2/ppermute | solution.py:459
  43.9 7.4 %collective-permute-start.10 = (bf16[128,1152]{1,0:T(8,128)(2,1)S(1)}, bf16[128,1152]{1,0:T(8,128)(2,1)S(1)}, u32[]{:S(2)}, u32[]{:S(2)}) collective-permute-start(bf16[128,1152]{1,0:T(8,128)(2,1)S(1)} %get-tuple-element.100.refs_2_), channel_id=1, source_target_pairs={{0,1},{1,0},{2,3},{3,2},{4,5},{5,4},{6,7},{7,6},{8,9},{9,8},{10,11... | collective-permute-start | bytes 884744 | tf_op jit(solution)/shard_map/rows1pair0/ppermute | solution.py:459
  43.9 7.3 %collective-permute-start.9 = (bf16[128,1024]{1,0:T(8,128)(2,1)S(1)}, bf16[128,1024]{1,0:T(8,128)(2,1)S(1)}, u32[]{:S(2)}, u32[]{:S(2)}) collective-permute-start(bf16[128,1024]{1,0:T(8,128)(2,1)S(1)} %get-tuple-element.99.refs_1_), channel_id=1, source_target_pairs={{0,1},{1,0},{2,3},{3,2},{4,5},{5,4},{6,7},{7,6},{8,9},{9,8},{10,11... | collective-permute-start | bytes 786440 | tf_op jit(solution)/shard_map/rows0pair0/ppermute | solution.py:459
  44.4 15.8 %collective-permute-start.17 = (bf16[128,1152]{1,0:T(8,128)(2,1)S(1)}, bf16[128,1152]{1,0:T(8,128)(2,1)S(1)}, u32[]{:S(2)}, u32[]{:S(2)}) collective-permute-start(bf16[128,1152]{1,0:T(8,128)(2,1)S(1)} %get-tuple-element.100.refs_2_), channel_id=1, source_target_pairs={{0,4},{1,5},{2,6},{3,7},{4,0},{5,1},{6,2},{7,3},{8,12},{9,13},{10,... | collective-permute-start | bytes 884744 | tf_op jit(solution)/shard_map/rows1chip2/ppermute | solution.py:459
  47.3 15.8 %collective-permute-start.14 = (bf16[128,1152]{1,0:T(8,128)(2,1)S(1)}, bf16[128,1152]{1,0:T(8,128)(2,1)S(1)}, u32[]{:S(2)}, u32[]{:S(2)}) collective-permute-start(bf16[128,1152]{1,0:T(8,128)(2,1)S(1)} %get-tuple-element.100.refs_2_), channel_id=1, source_target_pairs={{0,2},{1,3},{2,0},{3,1},{4,6},{5,7},{6,4},{7,5},{8,10},{9,11},{10,... | collective-permute-start | bytes 884744 | tf_op jit(solution)/shard_map/rows1chip1/ppermute | solution.py:459
  49.7 18.1 %collective-permute-start.13 = (bf16[128,1024]{1,0:T(8,128)(2,1)S(1)}, bf16[128,1024]{1,0:T(8,128)(2,1)S(1)}, u32[]{:S(2)}, u32[]{:S(2)}) collective-permute-start(bf16[128,1024]{1,0:T(8,128)(2,1)S(1)} %get-tuple-element.99.refs_1_), channel_id=1, source_target_pairs={{0,2},{1,3},{2,0},{3,1},{4,6},{5,7},{6,4},{7,5},{8,10},{9,11},{10,... | collective-permute-start | bytes 786440 | tf_op jit(solution)/shard_map/rows0chip1/ppermute | solution.py:459
  59.5 10.0 %collective-permute-start.18 = (bf16[128,1024]{1,0:T(8,128)(2,1)S(1)}, bf16[128,1024]{1,0:T(8,128)(2,1)S(1)}, u32[]{:S(2)}, u32[]{:S(2)}) collective-permute-start(bf16[128,1024]{1,0:T(8,128)(2,1)S(1)} %collective-permute-done.11.refs_5_), channel_id=1, source_target_pairs={{0,1},{1,0},{2,3},{3,2},{4,5},{5,4},{6,7},{7,6},{8,9},{9,8},{10,11... | collective-permute-start | bytes 786440 | tf_op jit(solution)/shard_map/rows0pair2/ppermute | solution.py:459
  60.2 9.6 %collective-permute-start.19 = (bf16[128,1152]{1,0:T(8,128)(2,1)S(1)}, bf16[128,1152]{1,0:T(8,128)(2,1)S(1)}, u32[]{:S(2)}, u32[]{:S(2)}) collective-permute-start(bf16[128,1152]{1,0:T(8,128)(2,1)S(1)} %collective-permute-done.17.refs_6_), channel_id=1, source_target_pairs={{0,1},{1,0},{2,3},{3,2},{4,5},{5,4},{6,7},{7,6},{8,9},{9,8},{10,11... | collective-permute-start | bytes 884744 | tf_op jit(solution)/shard_map/rows1pair2/ppermute | solution.py:459
  63.1 6.8 %collective-permute-start.16 = (bf16[128,1152]{1,0:T(8,128)(2,1)S(1)}, bf16[128,1152]{1,0:T(8,128)(2,1)S(1)}, u32[]{:S(2)}, u32[]{:S(2)}) collective-permute-start(bf16[128,1152]{1,0:T(8,128)(2,1)S(1)} %collective-permute-done.14.refs_2_), channel_id=1, source_target_pairs={{0,1},{1,0},{2,3},{3,2},{4,5},{5,4},{6,7},{7,6},{8,9},{9,8},{10,11... | collective-permute-start | bytes 884744 | tf_op jit(solution)/shard_map/rows1pair1/ppermute | solution.py:459
  67.9 2.0 %collective-permute-start.15 = (bf16[128,1024]{1,0:T(8,128)(2,1)S(1)}, bf16[128,1024]{1,0:T(8,128)(2,1)S(1)}, u32[]{:S(2)}, u32[]{:S(2)}) collective-permute-start(bf16[128,1024]{1,0:T(8,128)(2,1)S(1)} %collective-permute-done.13.refs_1_), channel_id=1, source_target_pairs={{0,1},{1,0},{2,3},{3,2},{4,5},{5,4},{6,7},{7,6},{8,9},{9,8},{10,11... | collective-permute-start | bytes 786440 | tf_op jit(solution)/shard_map/rows0pair1/ppermute | solution.py:459
  67.9 16.3 %collective-permute-start.25 = (bf16[128,1152]{1,0:T(8,128)(2,1)S(1)}, bf16[128,1152]{1,0:T(8,128)(2,1)S(1)}, u32[]{:S(2)}, u32[]{:S(2)}) collective-permute-start(bf16[128,1152]{1,0:T(8,128)(2,1)S(1)} %collective-permute-done.17.refs_6_), channel_id=1, source_target_pairs={{0,2},{1,3},{2,0},{3,1},{4,6},{5,7},{6,4},{7,5},{8,10},{9,11},{10,... | collective-permute-start | bytes 884744 | tf_op jit(solution)/shard_map/rows1chip3/ppermute | solution.py:459
  69.5 14.8 %collective-permute-start.24 = (bf16[128,1024]{1,0:T(8,128)(2,1)S(1)}, bf16[128,1024]{1,0:T(8,128)(2,1)S(1)}, u32[]{:S(2)}, u32[]{:S(2)}) collective-permute-start(bf16[128,1024]{1,0:T(8,128)(2,1)S(1)} %collective-permute-done.11.refs_5_), channel_id=1, source_target_pairs={{0,2},{1,3},{2,0},{3,1},{4,6},{5,7},{6,4},{7,5},{8,10},{9,11},{10,... | collective-permute-start | bytes 786440 | tf_op jit(solution)/shard_map/rows0chip3/ppermute | solution.py:459
  83.6 2.0 %collective-permute-start.20 = (bf16[2,128,1024]{2,1,0:T(8,128)(2,1)S(1)}, bf16[2,128,1024]{2,1,0:T(8,128)(2,1)S(1)}, u32[]{:S(2)}, u32[]{:S(2)}) collective-permute-start(bf16[2,128,1024]{2,1,0:T(8,128)(2,1)S(1)} %get-tuple-element.107), channel_id=1, source_target_pairs={{0,1},{1,0},{2,3},{3,2},{4,5},{5,4},{6,7},{7,6},{8,9},{9,8},{10,11... | collective-permute-start | bytes 1572872 | tf_op jit(solution)/shard_map/sums1pair/ppermute | solution.py:459
  83.7 2.6 %collective-permute-start.21 = (bf16[2,128,1024]{2,1,0:T(8,128)(2,1)S(1)}, bf16[2,128,1024]{2,1,0:T(8,128)(2,1)S(1)}, u32[]{:S(2)}, u32[]{:S(2)}) collective-permute-start(bf16[2,128,1024]{2,1,0:T(8,128)(2,1)S(1)} %get-tuple-element.108), channel_id=1, source_target_pairs={{0,1},{1,0},{2,3},{3,2},{4,5},{5,4},{6,7},{7,6},{8,9},{9,8},{10,11... | collective-permute-start | bytes 1572872 | tf_op jit(solution)/shard_map/sums1pair/ppermute | solution.py:459
  84.2 4.4 %collective-permute-start.27 = (bf16[128,1152]{1,0:T(8,128)(2,1)S(1)}, bf16[128,1152]{1,0:T(8,128)(2,1)S(1)}, u32[]{:S(2)}, u32[]{:S(2)}) collective-permute-start(bf16[128,1152]{1,0:T(8,128)(2,1)S(1)} %collective-permute-done.25.refs_2_), channel_id=1, source_target_pairs={{0,1},{1,0},{2,3},{3,2},{4,5},{5,4},{6,7},{7,6},{8,9},{9,8},{10,11... | collective-permute-start | bytes 884744 | tf_op jit(solution)/shard_map/rows1pair3/ppermute | solution.py:459
  84.3 4.3 %collective-permute-start.26 = (bf16[128,1024]{1,0:T(8,128)(2,1)S(1)}, bf16[128,1024]{1,0:T(8,128)(2,1)S(1)}, u32[]{:S(2)}, u32[]{:S(2)}) collective-permute-start(bf16[128,1024]{1,0:T(8,128)(2,1)S(1)} %collective-permute-done.24.refs_1_), channel_id=1, source_target_pairs={{0,1},{1,0},{2,3},{3,2},{4,5},{5,4},{6,7},{7,6},{8,9},{9,8},{10,11... | collective-permute-start | bytes 786440 | tf_op jit(solution)/shard_map/rows0pair3/ppermute | solution.py:459
  86.8 21.8 %collective-permute-start.22 = (bf16[128,2048]{1,0:T(8,128)(2,1)S(1)}, bf16[128,2048]{1,0:T(8,128)(2,1)S(1)}, u32[]{:S(2)}, u32[]{:S(2)}) collective-permute-start(bf16[128,2048]{1,0:T(8,128)(2,1)S(1)} %pad_maximum_fusion.1), channel_id=1, source_target_pairs={{0,2},{1,3},{2,0},{3,1},{4,6},{5,7},{6,4},{7,5},{8,10},{9,11},{10,... | collective-permute-start | bytes 1572872 | tf_op jit(solution)/shard_map/sums1chip/ppermute | solution.py:459
  88.5 28.5 %collective-permute-start.23 = (bf16[128,2048]{1,0:T(8,128)(2,1)S(1)}, bf16[128,2048]{1,0:T(8,128)(2,1)S(1)}, u32[]{:S(2)}, u32[]{:S(2)}) collective-permute-start(bf16[128,2048]{1,0:T(8,128)(2,1)S(1)} %pad_maximum_fusion.2), channel_id=1, source_target_pairs={{0,4},{1,5},{2,6},{3,7},{4,0},{5,1},{6,2},{7,3},{8,12},{9,13},{10,... | collective-permute-start | bytes 1572872 | tf_op jit(solution)/shard_map/sums2chip/ppermute | solution.py:459
  97.4 22.3 %collective-permute-start.12 = (bf16[1,128,2048]{2,1,0:T(8,128)(2,1)S(1)}, bf16[1,128,2048]{2,1,0:T(8,128)(2,1)S(1)}, u32[]{:S(2)}, u32[]{:S(2)}) collective-permute-start(bf16[1,128,2048]{2,1,0:T(8,128)(2,1)S(1)} %get-tuple-element.98), channel_id=1, source_target_pairs={{0,1},{1,0},{2,3},{3,2},{4,5},{5,4},{6,7},{7,6},{8,9},{9,8},{10,11... | collective-permute-start | bytes 1572872 | tf_op jit(solution)/shard_map/sums0pair/ppermute | solution.py:459
  99.9 28.6 %collective-permute-start.29 = (bf16[128,512]{1,0:T(8,128)(2,1)S(1)}, bf16[128,512]{1,0:T(8,128)(2,1)S(1)}, u32[]{:S(2)}, u32[]{:S(2)}) collective-permute-start(bf16[128,512]{1,0:T(8,128)(2,1)S(1)} %get-tuple-element.123), channel_id=1, source_target_pairs={{0,6},{1,7},{2,4},{3,5},{4,2},{5,3},{6,0},{7,1},{8,14},{9,15},{10,... | collective-permute-start | bytes 393224 | tf_op jit(solution)/shard_map/sums3chip/ppermute | solution.py:459
  101.8 29.5 %collective-permute-start.31 = (bf16[128,512]{1,0:T(8,128)(2,1)S(1)}, bf16[128,512]{1,0:T(8,128)(2,1)S(1)}, u32[]{:S(2)}, u32[]{:S(2)}) collective-permute-start(bf16[128,512]{1,0:T(8,128)(2,1)S(1)} %get-tuple-element.126), channel_id=1, source_target_pairs={{0,6},{1,7},{2,4},{3,5},{4,2},{5,3},{6,0},{7,1},{8,14},{9,15},{10,... | collective-permute-start | bytes 393224 | tf_op jit(solution)/shard_map/sums3chip/ppermute | solution.py:459
  117.0 17.2 %collective-permute-start.34 = (bf16[128,512]{1,0:T(8,128)(2,1)S(1)}, bf16[128,512]{1,0:T(8,128)(2,1)S(1)}, u32[]{:S(2)}, u32[]{:S(2)}) collective-permute-start(bf16[128,512]{1,0:T(8,128)(2,1)S(1)} %get-tuple-element.118), channel_id=1, source_target_pairs={{0,6},{1,7},{2,4},{3,5},{4,2},{5,3},{6,0},{7,1},{8,14},{9,15},{10,... | collective-permute-start | bytes 393224 | tf_op jit(solution)/shard_map/sums3chip/ppermute | solution.py:459
  119.6 16.2 %collective-permute-start.35 = (bf16[128,512]{1,0:T(8,128)(2,1)S(1)}, bf16[128,512]{1,0:T(8,128)(2,1)S(1)}, u32[]{:S(2)}, u32[]{:S(2)}) collective-permute-start(bf16[128,512]{1,0:T(8,128)(2,1)S(1)} %get-tuple-element.119), channel_id=1, source_target_pairs={{0,6},{1,7},{2,4},{3,5},{4,2},{5,3},{6,0},{7,1},{8,14},{9,15},{10,... | collective-permute-start | bytes 393224 | tf_op jit(solution)/shard_map/sums3chip/ppermute | solution.py:459
  (5 other events, 18.5 us)

commit v6 on v5

--- a/solution.py
+++ b/solution.py
@@ -368,7 +368,7 @@
                 xs_ref[pl.ds(to, slab), :] = (x * (1.0 / jnp.sqrt(mean + EPS)) * gain).astype(BF)
                 return carry
 
-            lax.fori_loop(0, rows // slab, norm, 0, unroll=2)
+            lax.fori_loop(0, rows // slab, norm, 0, unroll=8)
 
     if True:
         for p in range(pairs):
@@ -580,7 +580,8 @@
                     chip = jnp.concatenate(chip, axis=1).astype(BF)
                     ready.append(chip)
                     chip = swap(chip, "expert", 2 * r, f"sums{r}chip")
-                    landed.append(chip)
+                    if r == 2:
+                        landed.append(chip)
                     chip = [chip.astype(F32)]
                 elif r == 3:
                     chip = [c.astype(BF) for c in chip]

time: 138 us -> 135 us (0.978)
  Pallas kernels: 56.6 us -> 51.1 us
  waiting for transfers between devices: 48.5 us -> 51.1 us
    pallas_call x3, Pallas kernels: 30.1 us -> 24.6 us  [expert_stage(): pl.pallas_call(lambda *refs: expert_kernel(*refs, blocks=blocks, parts=pa...]
    ppermute x36, waiting for transfers between devices: 48.5 us -> 51.1 us  [swap(): return lax.ppermute(x, axis, [(i, i ^ bits) for i in range(size)])]
  transfers between devices with their start and end apart: 36 -> 36, of which waited for: 17 -> 17; matrix products, arithmetic and copies ran while one was open for 3% -> 3% of each run, Pallas kernels for 40% -> 37%
where the time goes in v6:
time: 135 us; the launch traced here: 134 us
  waiting for transfers between devices  51.1 us (38%)
  Pallas kernels  51.1 us (38%)
  starting transfers between devices  24.8 us (18%)
  other arithmetic  4.55 us (3%)
  between operations  2.18 us (2%)
    ppermute x36, waiting for transfers between devices, swap(): return lax.ppermute(x, axis, [(i, i ^ bits) for i in range(size)])  51.1 us
    ppermute x36, starting transfers between devices, swap(): return lax.ppermute(x, axis, [(i, i ^ bits) for i in range(size)])  24.8 us
    pallas_call x3, Pallas kernels, expert_stage(): pl.pallas_call(lambda *refs: expert_kernel(*refs, blocks=blocks, parts=pa...  24.6 us
    pallas_call x2, Pallas kernels, prepare(): pl.pallas_call(lambda *refs: prepare_kernel(*refs, carried=len(carry)), g...  12.3 us
    pallas_call x2, Pallas kernels, resume(): pl.pallas_call(lambda *refs: resume_kernel(*refs, peers=len(got), first_h...  10.1 us
    pallas_call x2, Pallas kernels, pack(): pl.pallas_call(lambda *refs: pack_kernel(*refs, peers=peers, first=first)...  4.1 us
  transfers between devices with their start and end apart: 36, of which 17 were waited for; matrix products, arithmetic and copies ran while one was open for 3% of the time, Pallas kernels for 37%

profile of v6, /device:TPU:16, one launch (start us, length us, event | category | flops | bytes accessed | tf_op | source)
XLA Modules:
  0.0 133.9 jit_solution(15012238632942437791)
XLA Ops:
  2.0 1.5 %collective-permute-start = (s32[2]{0:T(128)S(1)}, s32[2]{0:T(128)S(1)}, u32[]{:S(2)}, u32[]{:S(2)}) collective-permute-start(s32[2]{0:T(128)S(1)} %pad_add_fusion), channel_id=1, source_target_pairs={{0,8},{8,0},{16,24},{24,16},{1,9},{9,1},{17,25},{25,17},{2,10},{10... | collective-permute-start | bytes 32 | tf_op jit(solution)/shard_map/hits1/ppermute | solution.py:459
  3.5 1.5 %collective-permute-start.1 = (s32[2]{0:T(128)S(1)}, s32[2]{0:T(128)S(1)}, u32[]{:S(2)}, u32[]{:S(2)}) collective-permute-start(s32[2]{0:T(128)S(1)} %pad_add_fusion), channel_id=1, source_target_pairs={{0,16},{8,24},{16,0},{24,8},{1,17},{9,25},{17,1},{25,9},{2,18},{10... | collective-permute-start | bytes 32 | tf_op jit(solution)/shard_map/hits2/ppermute | solution.py:459
  7.0 2.4 %collective-permute-done.2.refs_3_ = s32[2]{0:T(128)S(1)} collective-permute-done((s32[2]{0:T(128)S(1)}, s32[2]{0:T(128)S(1)}, u32[]{:S(2)}, u32[]{:S(2)}) %collective-permute-start.2) | collective-permute-done | bytes 40 | tf_op jit(solution)/shard_map/hits3/ppermute | solution.py:459
  9.5 2.1 %pack.2 = (bf16[8,128,128]{2,1,0:T(8,128)(2,1)S(1)}, bf16[8,128,128]{2,1,0:T(8,128)(2,1)S(1)}, bf16[8,128,128]{2,1,0:T(8,128)(2,1)S(1)}) custom-call(s32[1]{0:T(128)} %bitcast.6.refs_0_, s32[2]{0:T(128)S(1)} %collective-permute-done.refs_1_, s32[2]{0:T(128)S(1)} %collective-permute-done.1.refs_2_, s32[2]{0:T(128)S(1)} %collective-permute-done.2.refs_3_, ...), custom_call_target="tpu_custom_call" | custom-call | flops 1000 | bytes 1000 | tf_op jit(solution)/shard_map/pack/pallas_call | solution.py:164
  12.6 2.4 %collective-permute-start.5 = (bf16[8,128,128]{2,1,0:T(8,128)(2,1)S(1)}, bf16[8,128,128]{2,1,0:T(8,128)(2,1)S(1)}, u32[]{:S(2)}, u32[]{:S(2)}) collective-permute-start(bf16[8,128,128]{2,1,0:T(8,128)(2,1)S(1)} %get-tuple-element.69), channel_id=1, source_target_pairs={{0,24},{8,16},{16,8},{24,0},{1,25},{9,17},{17,9},{25,1},{2,26},{10... | collective-permute-start | bytes 786440 | tf_op jit(solution)/shard_map/state0from3/ppermute | solution.py:459
  15.1 2.0 %pack.3 = (bf16[8,128,128]{2,1,0:T(8,128)(2,1)S(1)}, bf16[8,128,128]{2,1,0:T(8,128)(2,1)S(1)}, bf16[8,128,128]{2,1,0:T(8,128)(2,1)S(1)}) custom-call(s32[1]{0:T(128)} %bitcast.6.refs_0_, s32[2]{0:T(128)S(1)} %collective-permute-done.refs_1_, s32[2]{0:T(128)S(1)} %collective-permute-done.1.refs_2_, s32[2]{0:T(128)S(1)} %collective-permute-done.2.refs_3_, ...), custom_call_target="tpu_custom_call" | custom-call | flops 1000 | bytes 1000 | tf_op jit(solution)/shard_map/pack/pallas_call | solution.py:164
  18.2 2.6 %collective-permute-done.3.refs_2_ = bf16[8,128,128]{2,1,0:T(8,128)(2,1)S(1)} collective-permute-done((bf16[8,128,128]{2,1,0:T(8,128)(2,1)S(1)}, bf16[8,128,128]{2,1,0:T(8,128)(2,1)S(1)}, u32[]{:S(2)}, u32[]{:S(2)}) %collective-permute-start.3) | collective-permute-done | bytes 262176 | tf_op jit(solution)/shard_map/state0from1/ppermute | solution.py:459
  21.3 5.5 %prepare.2 = (bf16[8,256,128]{2,1,0:T(8,128)(2,1)S(1)}, bf16[8,128,128]{2,1,0:T(8,128)(2,1)S(1)}, bf16[8,256,128]{2,1,0:T(8,128)(2,1)S(1)}) custom-call(bf16[128,2048]{1,0:T(8,128)(2,1)} %refs_0_.3, bf16[128,2048]{1,0:T(8,128)(2,1)} %refs_1_.6, f32[4,8,128]{2,1,0:T(8,128)S(1)} %pad_maximum_fusion.3.refs_2_.refs_9_, f32[4,128,8]{2,1,0:T(8,128)S(1)} %bitcast.59), custom_call_target="tpu_custom_call" | custom-call | flops 1000 | bytes 1000 | tf_op jit(solution)/shard_map/prepare/pallas_call | solution.py:113
  26.8 4.6 %resume.2 = (bf16[128,1024]{1,0:T(8,128)(2,1)S(1)}, f32[8,128,128]{2,1,0:T(8,128)S(1)}) custom-call(s32[2]{0:T(128)S(1)} %pad_add_fusion.1.refs_0_, f32[1,2,16,128,128]{4,3,2,1,0:T(8,128)} %refs_1_.7, bf16[8,128,128]{2,1,0:T(8,128)(2,1)S(1)} %collective-permute-done.3.refs_2_, bf16[8,128,128]{2,1,0:T(8,128)(2,1)S(1)} %collective-permute-done.4.refs_3_, ...), custom_call_target="tpu_custom_call" | custom-call | flops 1000 | bytes 1000 | tf_op jit(solution)/shard_map/resume/pallas_call | solution.py:282
  31.5 6.8 %prepare.3 = (bf16[8,256,128]{2,1,0:T(8,128)(2,1)S(1)}, bf16[8,128,128]{2,1,0:T(8,128)(2,1)S(1)}, bf16[8,256,128]{2,1,0:T(8,128)(2,1)S(1)}, bf16[4,2048,512]{2,1,0:T(8,128)(2,1)S(1)}, bf16[4,512,2048]{2,1,0:T(8,128)(2,1)S(1)}) custom-call(bf16[128,2048]{1,0:T(8,128)(2,1)} %refs_0_.3, bf16[128,2048]{1,0:T(8,128)(2,1)} %refs_1_.6, ...), custom_call_target="tpu_custom_call" | custom-call | flops 1000 | bytes 1000 | tf_op jit(solution)/shard_map/prepare/pallas_call | solution.py:113
  38.4 5.5 %resume.3 = (bf16[128,1152]{1,0:T(8,128)(2,1)S(1)}, f32[8,128,128]{2,1,0:T(8,128)S(1)}, bf16[4,2048,512]{2,1,0:T(8,128)(2,1)S(1)}) custom-call(s32[2]{0:T(128)S(1)} %pad_add_fusion.1.refs_0_, f32[1,2,16,128,128]{4,3,2,1,0:T(8,128)} %refs_1_.7, bf16[8,128,128]{2,1,0:T(8,128)(2,1)S(1)} %collective-permute-done.6.refs_2_, ...), custom_call_target="tpu_custom_call" | custom-call | flops 1000 | bytes 1000 | tf_op jit(solution)/shard_map/resume/pallas_call | solution.py:282
  44.4 2.7 %collective-permute-start.17 = (bf16[128,1152]{1,0:T(8,128)(2,1)S(1)}, bf16[128,1152]{1,0:T(8,128)(2,1)S(1)}, u32[]{:S(2)}, u32[]{:S(2)}) collective-permute-start(bf16[128,1152]{1,0:T(8,128)(2,1)S(1)} %get-tuple-element.100.refs_2_), channel_id=1, source_target_pairs={{0,4},{1,5},{2,6},{3,7},{4,0},{5,1},{6,2},{7,3},{8,12},{9,13},{10,... | collective-permute-start | bytes 884744 | tf_op jit(solution)/shard_map/rows1chip2/ppermute | solution.py:459
  47.1 1.8 %collective-permute-start.14 = (bf16[128,1152]{1,0:T(8,128)(2,1)S(1)}, bf16[128,1152]{1,0:T(8,128)(2,1)S(1)}, u32[]{:S(2)}, u32[]{:S(2)}) collective-permute-start(bf16[128,1152]{1,0:T(8,128)(2,1)S(1)} %get-tuple-element.100.refs_2_), channel_id=1, source_target_pairs={{0,2},{1,3},{2,0},{3,1},{4,6},{5,7},{6,4},{7,5},{8,10},{9,11},{10,... | collective-permute-start | bytes 884744 | tf_op jit(solution)/shard_map/rows1chip1/ppermute | solution.py:459
  50.0 1.0 maximum_bitcast_fusion
  51.0 6.8 %experts.3 = (bf16[1,128,2048]{2,1,0:T(8,128)(2,1)S(1)}, bf16[1,128,2048]{2,1,0:T(8,128)(2,1)S(1)}) custom-call(s32[1]{0:T(128)} %bitcast.11.refs_0_, bf16[128,1024]{1,0:T(8,128)(2,1)S(1)} %get-tuple-element.99.refs_1_, bf16[128,1152]{1,0:T(8,128)(2,1)S(1)} %get-tuple-element.100.refs_2_, bf16[128,1024]{1,0:T(8,128)(2,1)S(1)} %collective-permute-done.9.refs_3_, ...), custom_call_target="tpu_custom_call" | custom-call | flops 1000 | bytes 1000 | tf_op jit(solution)/shard_map/experts/pallas_call | solution.py:419
  57.9 2.1 %collective-permute-done.17.refs_6_ = bf16[128,1152]{1,0:T(8,128)(2,1)S(1)} collective-permute-done((bf16[128,1152]{1,0:T(8,128)(2,1)S(1)}, bf16[128,1152]{1,0:T(8,128)(2,1)S(1)}, u32[]{:S(2)}, u32[]{:S(2)}) %collective-permute-start.17) | collective-permute-done | bytes 294944 | tf_op jit(solution)/shard_map/rows1chip2/ppermute | solution.py:459
  60.0 3.1 %collective-permute-done.14.refs_2_ = bf16[128,1152]{1,0:T(8,128)(2,1)S(1)} collective-permute-done((bf16[128,1152]{1,0:T(8,128)(2,1)S(1)}, bf16[128,1152]{1,0:T(8,128)(2,1)S(1)}, u32[]{:S(2)}, u32[]{:S(2)}) %collective-permute-start.14) | collective-permute-done | bytes 294944 | tf_op jit(solution)/shard_map/rows1chip1/ppermute | solution.py:459
  63.1 4.7 %collective-permute-done.13.refs_1_ = bf16[128,1024]{1,0:T(8,128)(2,1)S(1)} collective-permute-done((bf16[128,1024]{1,0:T(8,128)(2,1)S(1)}, bf16[128,1024]{1,0:T(8,128)(2,1)S(1)}, u32[]{:S(2)}, u32[]{:S(2)}) %collective-permute-start.13) | collective-permute-done | bytes 262176 | tf_op jit(solution)/shard_map/rows0chip1/ppermute | solution.py:459
  67.8 1.6 %collective-permute-start.25 = (bf16[128,1152]{1,0:T(8,128)(2,1)S(1)}, bf16[128,1152]{1,0:T(8,128)(2,1)S(1)}, u32[]{:S(2)}, u32[]{:S(2)}) collective-permute-start(bf16[128,1152]{1,0:T(8,128)(2,1)S(1)} %collective-permute-done.17.refs_6_), channel_id=1, source_target_pairs={{0,2},{1,3},{2,0},{3,1},{4,6},{5,7},{6,4},{7,5},{8,10},{9,11},{10,... | collective-permute-start | bytes 884744 | tf_op jit(solution)/shard_map/rows1chip3/ppermute | solution.py:459
  69.9 11.0 %experts.4 = (bf16[2,128,2048]{2,1,0:T(8,128)(2,1)S(1)}, bf16[2,128,1024]{2,1,0:T(8,128)(2,1)S(1)}, bf16[2,128,1024]{2,1,0:T(8,128)(2,1)S(1)}) custom-call(s32[1]{0:T(128)} %bitcast.11.refs_0_, bf16[128,1024]{1,0:T(8,128)(2,1)S(1)} %collective-permute-done.13.refs_1_, bf16[128,1152]{1,0:T(8,128)(2,1)S(1)} %collective-permute-done.14.refs_2_, ...), custom_call_target="tpu_custom_call" | custom-call | flops 1000 | bytes 1000 | tf_op jit(solution)/shard_map/experts/pallas_call | solution.py:419
  82.0 0.9 collective-permute-done.24.refs_1_
  85.1 6.8 %experts.5 = (bf16[1,128,2048]{2,1,0:T(8,128)(2,1)S(1)}, bf16[1,128,512]{2,1,0:T(8,128)(2,1)S(1)}, bf16[1,128,512]{2,1,0:T(8,128)(2,1)S(1)}, bf16[1,128,512]{2,1,0:T(8,128)(2,1)S(1)}, bf16[1,128,512]{2,1,0:T(8,128)(2,1)S(1)}) custom-call(s32[1]{0:T(128)} %bitcast.11.refs_0_, bf16[128,1024]{1,0:T(8,128)(2,1)S(1)} %collective-permute-done.24.refs_1_, ...), custom_call_target="tpu_custom_call" | custom-call | flops 1000 | bytes 1000 | tf_op jit(solution)/shard_map/experts/pallas_call | solution.py:419
  92.5 1.6 %collective-permute-start.22 = (bf16[128,2048]{1,0:T(8,128)(2,1)S(1)}, bf16[128,2048]{1,0:T(8,128)(2,1)S(1)}, u32[]{:S(2)}, u32[]{:S(2)}) collective-permute-start(bf16[128,2048]{1,0:T(8,128)(2,1)S(1)} %pad_maximum_fusion.1), channel_id=1, source_target_pairs={{0,2},{1,3},{2,0},{3,1},{4,6},{5,7},{6,4},{7,5},{8,10},{9,11},{10,... | collective-permute-start | bytes 1572872 | tf_op jit(solution)/shard_map/sums1chip/ppermute | solution.py:459
  94.7 0.8 collective-permute-done.32
  95.8 1.4 %collective-permute-start.29 = (bf16[128,512]{1,0:T(8,128)(2,1)S(1)}, bf16[128,512]{1,0:T(8,128)(2,1)S(1)}, u32[]{:S(2)}, u32[]{:S(2)}) collective-permute-start(bf16[128,512]{1,0:T(8,128)(2,1)S(1)} %get-tuple-element.123), channel_id=1, source_target_pairs={{0,6},{1,7},{2,4},{3,5},{4,2},{5,3},{6,0},{7,1},{8,14},{9,15},{10,... | collective-permute-start | bytes 393224 | tf_op jit(solution)/shard_map/sums3chip/ppermute | solution.py:459
  97.9 10.0 %collective-permute-done.23 = bf16[128,2048]{1,0:T(8,128)(2,1)S(1)} collective-permute-done((bf16[128,2048]{1,0:T(8,128)(2,1)S(1)}, bf16[128,2048]{1,0:T(8,128)(2,1)S(1)}, u32[]{:S(2)}, u32[]{:S(2)}) %collective-permute-start.23) | collective-permute-done | bytes 524320 | tf_op jit(solution)/shard_map/sums2chip/ppermute | solution.py:459
  107.9 2.5 %collective-permute-start.34 = (bf16[128,512]{1,0:T(8,128)(2,1)S(1)}, bf16[128,512]{1,0:T(8,128)(2,1)S(1)}, u32[]{:S(2)}, u32[]{:S(2)}) collective-permute-start(bf16[128,512]{1,0:T(8,128)(2,1)S(1)} %get-tuple-element.118), channel_id=1, source_target_pairs={{0,6},{1,7},{2,4},{3,5},{4,2},{5,3},{6,0},{7,1},{8,14},{9,15},{10,... | collective-permute-start | bytes 393224 | tf_op jit(solution)/shard_map/sums3chip/ppermute | solution.py:459
  110.5 13.9 %collective-permute-done.29 = bf16[128,512]{1,0:T(8,128)(2,1)S(1)} collective-permute-done((bf16[128,512]{1,0:T(8,128)(2,1)S(1)}, bf16[128,512]{1,0:T(8,128)(2,1)S(1)}, u32[]{:S(2)}, u32[]{:S(2)}) %collective-permute-start.29) | collective-permute-done | bytes 131104 | tf_op jit(solution)/shard_map/sums3chip/ppermute | solution.py:459
  124.4 2.8 %collective-permute-done.31 = bf16[128,512]{1,0:T(8,128)(2,1)S(1)} collective-permute-done((bf16[128,512]{1,0:T(8,128)(2,1)S(1)}, bf16[128,512]{1,0:T(8,128)(2,1)S(1)}, u32[]{:S(2)}, u32[]{:S(2)}) %collective-permute-start.31) | collective-permute-done | bytes 131104 | tf_op jit(solution)/shard_map/sums3chip/ppermute | solution.py:459
  128.0 2.0 %collective-permute-done.34 = bf16[128,512]{1,0:T(8,128)(2,1)S(1)} collective-permute-done((bf16[128,512]{1,0:T(8,128)(2,1)S(1)}, bf16[128,512]{1,0:T(8,128)(2,1)S(1)}, u32[]{:S(2)}, u32[]{:S(2)}) %collective-permute-start.34) | collective-permute-done | bytes 131104 | tf_op jit(solution)/shard_map/sums3chip/ppermute | solution.py:459
  130.0 2.7 %collective-permute-done.35 = bf16[128,512]{1,0:T(8,128)(2,1)S(1)} collective-permute-done((bf16[128,512]{1,0:T(8,128)(2,1)S(1)}, bf16[128,512]{1,0:T(8,128)(2,1)S(1)}, u32[]{:S(2)}, u32[]{:S(2)}) %collective-permute-start.35) | collective-permute-done | bytes 131104 | tf_op jit(solution)/shard_map/sums3chip/ppermute | solution.py:459
  132.7 1.2 fusion.2
  (64 shorter events, 13.3 us)
Async XLA Ops:
  2.0 4.4 %collective-permute-start = (s32[2]{0:T(128)S(1)}, s32[2]{0:T(128)S(1)}, u32[]{:S(2)}, u32[]{:S(2)}) collective-permute-start(s32[2]{0:T(128)S(1)} %pad_add_fusion), channel_id=1, source_target_pairs={{0,8},{8,0},{16,24},{24,16},{1,9},{9,1},{17,25},{25,17},{2,10},{10... | collective-permute-start | bytes 32 | tf_op jit(solution)/shard_map/hits1/ppermute | solution.py:459
  3.5 3.5 %collective-permute-start.1 = (s32[2]{0:T(128)S(1)}, s32[2]{0:T(128)S(1)}, u32[]{:S(2)}, u32[]{:S(2)}) collective-permute-start(s32[2]{0:T(128)S(1)} %pad_add_fusion), channel_id=1, source_target_pairs={{0,16},{8,24},{16,0},{24,8},{1,17},{9,25},{17,1},{25,9},{2,18},{10... | collective-permute-start | bytes 32 | tf_op jit(solution)/shard_map/hits2/ppermute | solution.py:459
  5.0 4.4 %collective-permute-start.2 = (s32[2]{0:T(128)S(1)}, s32[2]{0:T(128)S(1)}, u32[]{:S(2)}, u32[]{:S(2)}) collective-permute-start(s32[2]{0:T(128)S(1)} %pad_add_fusion), channel_id=1, source_target_pairs={{0,24},{8,16},{16,8},{24,0},{1,25},{9,17},{17,9},{25,1},{2,26},{10... | collective-permute-start | bytes 32 | tf_op jit(solution)/shard_map/hits3/ppermute | solution.py:459
  11.5 9.3 %collective-permute-start.3 = (bf16[8,128,128]{2,1,0:T(8,128)(2,1)S(1)}, bf16[8,128,128]{2,1,0:T(8,128)(2,1)S(1)}, u32[]{:S(2)}, u32[]{:S(2)}) collective-permute-start(bf16[8,128,128]{2,1,0:T(8,128)(2,1)S(1)} %get-tuple-element.67), channel_id=1, source_target_pairs={{0,8},{8,0},{16,24},{24,16},{1,9},{9,1},{17,25},{25,17},{2,10},{10... | collective-permute-start | bytes 786440 | tf_op jit(solution)/shard_map/state0from1/ppermute | solution.py:459
  12.1 14.7 %collective-permute-start.4 = (bf16[8,128,128]{2,1,0:T(8,128)(2,1)S(1)}, bf16[8,128,128]{2,1,0:T(8,128)(2,1)S(1)}, u32[]{:S(2)}, u32[]{:S(2)}) collective-permute-start(bf16[8,128,128]{2,1,0:T(8,128)(2,1)S(1)} %get-tuple-element.68), channel_id=1, source_target_pairs={{0,16},{8,24},{16,0},{24,8},{1,17},{9,25},{17,1},{25,9},{2,18},{10... | collective-permute-start | bytes 786440 | tf_op jit(solution)/shard_map/state0from2/ppermute | solution.py:459
  12.6 14.2 %collective-permute-start.5 = (bf16[8,128,128]{2,1,0:T(8,128)(2,1)S(1)}, bf16[8,128,128]{2,1,0:T(8,128)(2,1)S(1)}, u32[]{:S(2)}, u32[]{:S(2)}) collective-permute-start(bf16[8,128,128]{2,1,0:T(8,128)(2,1)S(1)} %get-tuple-element.69), channel_id=1, source_target_pairs={{0,24},{8,16},{16,8},{24,0},{1,25},{9,17},{17,9},{25,1},{2,26},{10... | collective-permute-start | bytes 786440 | tf_op jit(solution)/shard_map/state0from3/ppermute | solution.py:459
  17.1 21.2 %collective-permute-start.6 = (bf16[8,128,128]{2,1,0:T(8,128)(2,1)S(1)}, bf16[8,128,128]{2,1,0:T(8,128)(2,1)S(1)}, u32[]{:S(2)}, u32[]{:S(2)}) collective-permute-start(bf16[8,128,128]{2,1,0:T(8,128)(2,1)S(1)} %get-tuple-element.81), channel_id=1, source_target_pairs={{0,8},{8,0},{16,24},{24,16},{1,9},{9,1},{17,25},{25,17},{2,10},{10... | collective-permute-start | bytes 786440 | tf_op jit(solution)/shard_map/state8from1/ppermute | solution.py:459
  17.7 20.6 %collective-permute-start.7 = (bf16[8,128,128]{2,1,0:T(8,128)(2,1)S(1)}, bf16[8,128,128]{2,1,0:T(8,128)(2,1)S(1)}, u32[]{:S(2)}, u32[]{:S(2)}) collective-permute-start(bf16[8,128,128]{2,1,0:T(8,128)(2,1)S(1)} %get-tuple-element.82), channel_id=1, source_target_pairs={{0,16},{8,24},{16,0},{24,8},{1,17},{9,25},{17,1},{25,9},{2,18},{10... | collective-permute-start | bytes 786440 | tf_op jit(solution)/shard_map/state8from2/ppermute | solution.py:459
  20.8 17.5 %collective-permute-start.8 = (bf16[8,128,128]{2,1,0:T(8,128)(2,1)S(1)}, bf16[8,128,128]{2,1,0:T(8,128)(2,1)S(1)}, u32[]{:S(2)}, u32[]{:S(2)}) collective-permute-start(bf16[8,128,128]{2,1,0:T(8,128)(2,1)S(1)} %get-tuple-element.83), channel_id=1, source_target_pairs={{0,24},{8,16},{16,8},{24,0},{1,25},{9,17},{17,9},{25,1},{2,26},{10... | collective-permute-start | bytes 786440 | tf_op jit(solution)/shard_map/state8from3/ppermute | solution.py:459
  31.4 18.3 %collective-permute-start.11 = (bf16[128,1024]{1,0:T(8,128)(2,1)S(1)}, bf16[128,1024]{1,0:T(8,128)(2,1)S(1)}, u32[]{:S(2)}, u32[]{:S(2)}) collective-permute-start(bf16[128,1024]{1,0:T(8,128)(2,1)S(1)} %get-tuple-element.99.refs_1_), channel_id=1, source_target_pairs={{0,4},{1,5},{2,6},{3,7},{4,0},{5,1},{6,2},{7,3},{8,12},{9,13},{10,... | collective-permute-start | bytes 786440 | tf_op jit(solution)/shard_map/rows0chip2/ppermute | solution.py:459
  43.9 7.1 %collective-permute-start.10 = (bf16[128,1152]{1,0:T(8,128)(2,1)S(1)}, bf16[128,1152]{1,0:T(8,128)(2,1)S(1)}, u32[]{:S(2)}, u32[]{:S(2)}) collective-permute-start(bf16[128,1152]{1,0:T(8,128)(2,1)S(1)} %get-tuple-element.100.refs_2_), channel_id=1, source_target_pairs={{0,1},{1,0},{2,3},{3,2},{4,5},{5,4},{6,7},{7,6},{8,9},{9,8},{10,11... | collective-permute-start | bytes 884744 | tf_op jit(solution)/shard_map/rows1pair0/ppermute | solution.py:459
  43.9 7.1 %collective-permute-start.9 = (bf16[128,1024]{1,0:T(8,128)(2,1)S(1)}, bf16[128,1024]{1,0:T(8,128)(2,1)S(1)}, u32[]{:S(2)}, u32[]{:S(2)}) collective-permute-start(bf16[128,1024]{1,0:T(8,128)(2,1)S(1)} %get-tuple-element.99.refs_1_), channel_id=1, source_target_pairs={{0,1},{1,0},{2,3},{3,2},{4,5},{5,4},{6,7},{7,6},{8,9},{9,8},{10,11... | collective-permute-start | bytes 786440 | tf_op jit(solution)/shard_map/rows0pair0/ppermute | solution.py:459
  44.4 15.6 %collective-permute-start.17 = (bf16[128,1152]{1,0:T(8,128)(2,1)S(1)}, bf16[128,1152]{1,0:T(8,128)(2,1)S(1)}, u32[]{:S(2)}, u32[]{:S(2)}) collective-permute-start(bf16[128,1152]{1,0:T(8,128)(2,1)S(1)} %get-tuple-element.100.refs_2_), channel_id=1, source_target_pairs={{0,4},{1,5},{2,6},{3,7},{4,0},{5,1},{6,2},{7,3},{8,12},{9,13},{10,... | collective-permute-start | bytes 884744 | tf_op jit(solution)/shard_map/rows1chip2/ppermute | solution.py:459
  47.1 16.0 %collective-permute-start.14 = (bf16[128,1152]{1,0:T(8,128)(2,1)S(1)}, bf16[128,1152]{1,0:T(8,128)(2,1)S(1)}, u32[]{:S(2)}, u32[]{:S(2)}) collective-permute-start(bf16[128,1152]{1,0:T(8,128)(2,1)S(1)} %get-tuple-element.100.refs_2_), channel_id=1, source_target_pairs={{0,2},{1,3},{2,0},{3,1},{4,6},{5,7},{6,4},{7,5},{8,10},{9,11},{10,... | collective-permute-start | bytes 884744 | tf_op jit(solution)/shard_map/rows1chip1/ppermute | solution.py:459
  49.7 18.1 %collective-permute-start.13 = (bf16[128,1024]{1,0:T(8,128)(2,1)S(1)}, bf16[128,1024]{1,0:T(8,128)(2,1)S(1)}, u32[]{:S(2)}, u32[]{:S(2)}) collective-permute-start(bf16[128,1024]{1,0:T(8,128)(2,1)S(1)} %get-tuple-element.99.refs_1_), channel_id=1, source_target_pairs={{0,2},{1,3},{2,0},{3,1},{4,6},{5,7},{6,4},{7,5},{8,10},{9,11},{10,... | collective-permute-start | bytes 786440 | tf_op jit(solution)/shard_map/rows0chip1/ppermute | solution.py:459
  57.9 11.6 %collective-permute-start.18 = (bf16[128,1024]{1,0:T(8,128)(2,1)S(1)}, bf16[128,1024]{1,0:T(8,128)(2,1)S(1)}, u32[]{:S(2)}, u32[]{:S(2)}) collective-permute-start(bf16[128,1024]{1,0:T(8,128)(2,1)S(1)} %collective-permute-done.11.refs_5_), channel_id=1, source_target_pairs={{0,1},{1,0},{2,3},{3,2},{4,5},{5,4},{6,7},{7,6},{8,9},{9,8},{10,11... | collective-permute-start | bytes 786440 | tf_op jit(solution)/shard_map/rows0pair2/ppermute | solution.py:459
  60.0 9.9 %collective-permute-start.19 = (bf16[128,1152]{1,0:T(8,128)(2,1)S(1)}, bf16[128,1152]{1,0:T(8,128)(2,1)S(1)}, u32[]{:S(2)}, u32[]{:S(2)}) collective-permute-start(bf16[128,1152]{1,0:T(8,128)(2,1)S(1)} %collective-permute-done.17.refs_6_), channel_id=1, source_target_pairs={{0,1},{1,0},{2,3},{3,2},{4,5},{5,4},{6,7},{7,6},{8,9},{9,8},{10,11... | collective-permute-start | bytes 884744 | tf_op jit(solution)/shard_map/rows1pair2/ppermute | solution.py:459
  63.1 6.8 %collective-permute-start.16 = (bf16[128,1152]{1,0:T(8,128)(2,1)S(1)}, bf16[128,1152]{1,0:T(8,128)(2,1)S(1)}, u32[]{:S(2)}, u32[]{:S(2)}) collective-permute-start(bf16[128,1152]{1,0:T(8,128)(2,1)S(1)} %collective-permute-done.14.refs_2_), channel_id=1, source_target_pairs={{0,1},{1,0},{2,3},{3,2},{4,5},{5,4},{6,7},{7,6},{8,9},{9,8},{10,11... | collective-permute-start | bytes 884744 | tf_op jit(solution)/shard_map/rows1pair1/ppermute | solution.py:459
  67.8 13.7 %collective-permute-start.25 = (bf16[128,1152]{1,0:T(8,128)(2,1)S(1)}, bf16[128,1152]{1,0:T(8,128)(2,1)S(1)}, u32[]{:S(2)}, u32[]{:S(2)}) collective-permute-start(bf16[128,1152]{1,0:T(8,128)(2,1)S(1)} %collective-permute-done.17.refs_6_), channel_id=1, source_target_pairs={{0,2},{1,3},{2,0},{3,1},{4,6},{5,7},{6,4},{7,5},{8,10},{9,11},{10,... | collective-permute-start | bytes 884744 | tf_op jit(solution)/shard_map/rows1chip3/ppermute | solution.py:459
  69.5 13.4 %collective-permute-start.24 = (bf16[128,1024]{1,0:T(8,128)(2,1)S(1)}, bf16[128,1024]{1,0:T(8,128)(2,1)S(1)}, u32[]{:S(2)}, u32[]{:S(2)}) collective-permute-start(bf16[128,1024]{1,0:T(8,128)(2,1)S(1)} %collective-permute-done.11.refs_5_), channel_id=1, source_target_pairs={{0,2},{1,3},{2,0},{3,1},{4,6},{5,7},{6,4},{7,5},{8,10},{9,11},{10,... | collective-permute-start | bytes 786440 | tf_op jit(solution)/shard_map/rows0chip3/ppermute | solution.py:459
  80.9 2.1 %collective-permute-start.20 = (bf16[2,128,1024]{2,1,0:T(8,128)(2,1)S(1)}, bf16[2,128,1024]{2,1,0:T(8,128)(2,1)S(1)}, u32[]{:S(2)}, u32[]{:S(2)}) collective-permute-start(bf16[2,128,1024]{2,1,0:T(8,128)(2,1)S(1)} %get-tuple-element.107), channel_id=1, source_target_pairs={{0,1},{1,0},{2,3},{3,2},{4,5},{5,4},{6,7},{7,6},{8,9},{9,8},{10,11... | collective-permute-start | bytes 1572872 | tf_op jit(solution)/shard_map/sums1pair/ppermute | solution.py:459
  81.0 2.6 %collective-permute-start.21 = (bf16[2,128,1024]{2,1,0:T(8,128)(2,1)S(1)}, bf16[2,128,1024]{2,1,0:T(8,128)(2,1)S(1)}, u32[]{:S(2)}, u32[]{:S(2)}) collective-permute-start(bf16[2,128,1024]{2,1,0:T(8,128)(2,1)S(1)} %get-tuple-element.108), channel_id=1, source_target_pairs={{0,1},{1,0},{2,3},{3,2},{4,5},{5,4},{6,7},{7,6},{8,9},{9,8},{10,11... | collective-permute-start | bytes 1572872 | tf_op jit(solution)/shard_map/sums1pair/ppermute | solution.py:459
  81.4 29.0 %collective-permute-start.12 = (bf16[1,128,2048]{2,1,0:T(8,128)(2,1)S(1)}, bf16[1,128,2048]{2,1,0:T(8,128)(2,1)S(1)}, u32[]{:S(2)}, u32[]{:S(2)}) collective-permute-start(bf16[1,128,2048]{2,1,0:T(8,128)(2,1)S(1)} %get-tuple-element.98), channel_id=1, source_target_pairs={{0,1},{1,0},{2,3},{3,2},{4,5},{5,4},{6,7},{7,6},{8,9},{9,8},{10,11... | collective-permute-start | bytes 1572872 | tf_op jit(solution)/shard_map/sums0pair/ppermute | solution.py:459
  81.5 3.6 %collective-permute-start.27 = (bf16[128,1152]{1,0:T(8,128)(2,1)S(1)}, bf16[128,1152]{1,0:T(8,128)(2,1)S(1)}, u32[]{:S(2)}, u32[]{:S(2)}) collective-permute-start(bf16[128,1152]{1,0:T(8,128)(2,1)S(1)} %collective-permute-done.25.refs_2_), channel_id=1, source_target_pairs={{0,1},{1,0},{2,3},{3,2},{4,5},{5,4},{6,7},{7,6},{8,9},{9,8},{10,11... | collective-permute-start | bytes 884744 | tf_op jit(solution)/shard_map/rows1pair3/ppermute | solution.py:459
  82.9 2.3 %collective-permute-start.26 = (bf16[128,1024]{1,0:T(8,128)(2,1)S(1)}, bf16[128,1024]{1,0:T(8,128)(2,1)S(1)}, u32[]{:S(2)}, u32[]{:S(2)}) collective-permute-start(bf16[128,1024]{1,0:T(8,128)(2,1)S(1)} %collective-permute-done.24.refs_1_), channel_id=1, source_target_pairs={{0,1},{1,0},{2,3},{3,2},{4,5},{5,4},{6,7},{7,6},{8,9},{9,8},{10,11... | collective-permute-start | bytes 786440 | tf_op jit(solution)/shard_map/rows0pair3/ppermute | solution.py:459
  84.1 23.9 %collective-permute-start.23 = (bf16[128,2048]{1,0:T(8,128)(2,1)S(1)}, bf16[128,2048]{1,0:T(8,128)(2,1)S(1)}, u32[]{:S(2)}, u32[]{:S(2)}) collective-permute-start(bf16[128,2048]{1,0:T(8,128)(2,1)S(1)} %pad_maximum_fusion.2), channel_id=1, source_target_pairs={{0,4},{1,5},{2,6},{3,7},{4,0},{5,1},{6,2},{7,3},{8,12},{9,13},{10,... | collective-permute-start | bytes 1572872 | tf_op jit(solution)/shard_map/sums2chip/ppermute | solution.py:459
  92.0 2.2 %collective-permute-start.28 = (bf16[1,128,512]{2,1,0:T(8,128)(2,1)S(1)}, bf16[1,128,512]{2,1,0:T(8,128)(2,1)S(1)}, u32[]{:S(2)}, u32[]{:S(2)}) collective-permute-start(bf16[1,128,512]{2,1,0:T(8,128)(2,1)S(1)} %get-tuple-element.114), channel_id=1, source_target_pairs={{0,1},{1,0},{2,3},{3,2},{4,5},{5,4},{6,7},{7,6},{8,9},{9,8},{10,11... | collective-permute-start | bytes 393224 | tf_op jit(solution)/shard_map/sums3pair/ppermute | solution.py:459
  92.5 35.5 %collective-permute-start.22 = (bf16[128,2048]{1,0:T(8,128)(2,1)S(1)}, bf16[128,2048]{1,0:T(8,128)(2,1)S(1)}, u32[]{:S(2)}, u32[]{:S(2)}) collective-permute-start(bf16[128,2048]{1,0:T(8,128)(2,1)S(1)} %pad_maximum_fusion.1), channel_id=1, source_target_pairs={{0,2},{1,3},{2,0},{3,1},{4,6},{5,7},{6,4},{7,5},{8,10},{9,11},{10,... | collective-permute-start | bytes 1572872 | tf_op jit(solution)/shard_map/sums1chip/ppermute | solution.py:459
  95.8 28.6 %collective-permute-start.29 = (bf16[128,512]{1,0:T(8,128)(2,1)S(1)}, bf16[128,512]{1,0:T(8,128)(2,1)S(1)}, u32[]{:S(2)}, u32[]{:S(2)}) collective-permute-start(bf16[128,512]{1,0:T(8,128)(2,1)S(1)} %get-tuple-element.123), channel_id=1, source_target_pairs={{0,6},{1,7},{2,4},{3,5},{4,2},{5,3},{6,0},{7,1},{8,14},{9,15},{10,... | collective-permute-start | bytes 393224 | tf_op jit(solution)/shard_map/sums3chip/ppermute | solution.py:459
  97.3 29.9 %collective-permute-start.31 = (bf16[128,512]{1,0:T(8,128)(2,1)S(1)}, bf16[128,512]{1,0:T(8,128)(2,1)S(1)}, u32[]{:S(2)}, u32[]{:S(2)}) collective-permute-start(bf16[128,512]{1,0:T(8,128)(2,1)S(1)} %get-tuple-element.126), channel_id=1, source_target_pairs={{0,6},{1,7},{2,4},{3,5},{4,2},{5,3},{6,0},{7,1},{8,14},{9,15},{10,... | collective-permute-start | bytes 393224 | tf_op jit(solution)/shard_map/sums3chip/ppermute | solution.py:459
  107.9 22.1 %collective-permute-start.34 = (bf16[128,512]{1,0:T(8,128)(2,1)S(1)}, bf16[128,512]{1,0:T(8,128)(2,1)S(1)}, u32[]{:S(2)}, u32[]{:S(2)}) collective-permute-start(bf16[128,512]{1,0:T(8,128)(2,1)S(1)} %get-tuple-element.118), channel_id=1, source_target_pairs={{0,6},{1,7},{2,4},{3,5},{4,2},{5,3},{6,0},{7,1},{8,14},{9,15},{10,... | collective-permute-start | bytes 393224 | tf_op jit(solution)/shard_map/sums3chip/ppermute | solution.py:459
  110.5 22.3 %collective-permute-start.35 = (bf16[128,512]{1,0:T(8,128)(2,1)S(1)}, bf16[128,512]{1,0:T(8,128)(2,1)S(1)}, u32[]{:S(2)}, u32[]{:S(2)}) collective-permute-start(bf16[128,512]{1,0:T(8,128)(2,1)S(1)} %get-tuple-element.119), channel_id=1, source_target_pairs={{0,6},{1,7},{2,4},{3,5},{4,2},{5,3},{6,0},{7,1},{8,14},{9,15},{10,... | collective-permute-start | bytes 393224 | tf_op jit(solution)/shard_map/sums3chip/ppermute | solution.py:459
  (5 other events, 19.6 us)
